TPU v7x, 32 devices: a whole 2x2x4 slice. The times are simulated.
32 devices in a mesh: ctx: 8 (over z, y), head: 4 (over x, core).
Axes of the slice: x: 2, y: 2, z: 4, core: 2. Of those that a mesh axis runs over, the one named last changes fastest.
Arguments:
- patches: bfloat16 [4096, 1152], P(('ctx', 'head')), may hold values from -44 to 44
- clip_start: int32 [8], replicated, may hold values from 0 to 511, as said below
- clip_len: int32 [8], replicated, may hold values from 1 to 512
- text_rows: bfloat16 [4096, 2048], P('ctx', 'head'), may hold values from -6 to 6
- vision_qkv: bfloat16 [1152, 3, 1152], P(None, None, 'head'), may hold values from -10 to 10
- vision_out: bfloat16 [1152, 1152], P('head'), may hold values from -0.75 to 0.75
- projector: bfloat16 [1152, 2048], P(None, 'head'), may hold values from -0.1875 to 0.1875
- layer_qkv: bfloat16 [2048, 3, 2048], P(None, None, 'head'), may hold values from -0.125 to 0.125
- head_gain: float32 [2048], P('head'), may hold values from 0.5 to 1.5
- state_in: float32 [16, 128, 128], P('head'), may hold values from -32768 to 32768
Outputs:
- attended: bfloat16 [4096, 2048], P('ctx', 'head')
Inputs may be any that keep to these rules, and one draw needn't show every extreme that they name: Clip c occupies clip_len[c] positions from c * 512 + clip_start[c] on; no two clips share a position, and the last clip ends within the last 512 positions.
All inputs are finite; a program needn't handle non-finite values.
Results may differ from a plain program's by a relative error of at most 0.015.
Values may be sent and summed in bfloat16 or wider, within the bound.
No kernel may reach another device: no remote copies, remote signals or barrier semaphores. Data moves between devices by JAX's collectives and lax.ppermute only.
A program may use at most 64 MiB of HBM per device.

v0:
```python
import jax
import jax.numpy as jnp
from jax import lax
from jax.sharding import PartitionSpec as P

VIT_HEADS = 16
VIT_HD = 72
HEADS = 16
HD = 128


EPS = 1e-06
HIGH = lax.Precision.HIGHEST


def shifted(value, axis, steps):
    count = lax.axis_size(axis)
    leading, last = (max(0, -steps), min(count, count - steps))
    return lax.ppermute(value, axis, [(source, source + steps) for source in range(leading, last)])


def unit_rows(values):
    values = values.astype(jnp.float32)
    return values * lax.rsqrt(jnp.mean(values * values, axis=-1, keepdims=True) + EPS)


def clip_attention(frame, length, vision_qkv, head_count):
    rows = frame.shape[0]
    normed = unit_rows(frame).astype(jnp.bfloat16)
    mixed = jnp.dot(
        normed, vision_qkv.reshape(vision_qkv.shape[0], -1), preferred_element_type=jnp.float32
    )
    mixed = mixed.astype(jnp.bfloat16).reshape(rows, 3, head_count, VIT_HD)
    scores = jnp.einsum(
        "thd,shd->hts", mixed[:, 0], mixed[:, 1], preferred_element_type=jnp.float32
    ) * VIT_HD ** (-0.5)
    live = jnp.arange(rows) < length
    scores = jnp.where(live[None, None, :], scores, -jnp.inf)
    highest = jnp.max(scores, axis=-1, keepdims=True)
    powers = jnp.exp(scores - highest)
    probs = (powers / jnp.sum(powers, axis=-1, keepdims=True)).astype(jnp.bfloat16)
    context = jnp.einsum("hts,shd->thd", probs, mixed[:, 2], preferred_element_type=jnp.float32)
    return context.astype(jnp.bfloat16).reshape(rows, head_count * VIT_HD)


def local(
    patches,
    clip_start,
    clip_len,
    text_rows,
    vision_qkv,
    vision_out,
    projector,
    layer_qkv,
    head_gain,
    state_in,
):
    groups = lax.axis_size("head")
    place = lax.axis_index("ctx")
    span = text_rows.shape[0]
    length = lax.dynamic_index_in_dim(clip_len, place, keepdims=False)
    start = lax.dynamic_index_in_dim(clip_start, place, keepdims=False)
    frame = lax.all_gather(patches, "head", axis=0, tiled=True)
    context = clip_attention(frame, length, vision_qkv, VIT_HEADS // groups)
    partial_value = jnp.dot(context, vision_out, preferred_element_type=jnp.float32)
    total = lax.psum(partial_value.astype(jnp.bfloat16), "head").astype(jnp.float32)
    merged = unit_rows(frame.astype(jnp.float32) + total).astype(jnp.bfloat16)
    visual = jnp.dot(merged, projector, preferred_element_type=jnp.float32).astype(jnp.bfloat16)
    within = jnp.arange(span)
    visual = jnp.where((within < length)[:, None], visual, jnp.zeros_like(visual))
    window = jnp.zeros((2 * span, visual.shape[1]), jnp.bfloat16)
    window = lax.dynamic_update_slice_in_dim(window, visual, start, 0)
    arrived = shifted(window[span:], "ctx", 1)
    own_live = (within >= start) & (within < start + length)
    prior = jnp.maximum(place - 1, 0)
    prior_start = lax.dynamic_index_in_dim(clip_start, prior, keepdims=False)
    prior_len = lax.dynamic_index_in_dim(clip_len, prior, keepdims=False)
    prior_live = (place > 0) & (within + span - prior_start < prior_len)
    sequence = jnp.where(
        own_live[:, None], window[:span], jnp.where(prior_live[:, None], arrived, text_rows)
    )
    full = lax.all_gather(sequence, "head", axis=1, tiled=True)
    unit = unit_rows(full).astype(jnp.bfloat16)
    heads = HEADS // groups
    layer_mix = jnp.dot(
        unit, layer_qkv.reshape(layer_qkv.shape[0], -1), preferred_element_type=jnp.float32
    )
    layer_mix = layer_mix.astype(jnp.bfloat16).reshape(span, 3, heads, HD)
    query, keys, values = (layer_mix[:, 0], layer_mix[:, 1], layer_mix[:, 2])
    delta = jnp.einsum("shd,she->hde", keys, values, preferred_element_type=jnp.float32)
    piece = lax.all_gather(delta.astype(jnp.bfloat16), "ctx", axis=0, tiled=True).astype(
        jnp.float32
    )
    count = piece.shape[0] // heads
    owners = jnp.arange(count)
    keep = (owners < place).astype(jnp.float32)
    carried = jnp.zeros_like(delta) + jnp.einsum(
        "n,nhde->hde", keep, piece.reshape(count, heads, HD, HD), precision=HIGH
    )
    carried = carried + state_in
    weights = jnp.einsum("thd,shd->hts", query, keys, preferred_element_type=jnp.float32)
    causal = within[:, None] >= within[None, :]
    weights = jnp.where(causal[None], weights, 0.0)
    intra = jnp.einsum("hts,she->the", weights, values.astype(jnp.float32), precision=HIGH)
    inter = jnp.einsum("thd,hde->the", query.astype(jnp.float32), carried, precision=HIGH)
    lin = inter + intra
    scaled = lin * lax.rsqrt(jnp.mean(lin * lin, axis=-1, keepdims=True) + EPS)
    scaled = scaled * head_gain.reshape(heads, HD)
    return scaled.astype(jnp.bfloat16).reshape(span, heads * HD)


def solution(mesh):
    placed = (
        P(("ctx", "head"), None),
        P(),
        P(),
        P("ctx", "head"),
        P(None, None, "head"),
        P("head", None),
        P(None, "head"),
        P(None, None, "head"),
        P("head"),
        P("head", None, None),
    )
    return jax.shard_map(
        local, mesh=mesh, in_specs=placed, out_specs=P("ctx", "head"), check_vma=False
    )
```

profile of v0, /device:TPU:0, one launch (start us, length us, event | category | flops | bytes accessed | tf_op | source)
XLA Modules:
  0.0 206.0 jit_solution(6839096813537360044)
XLA Ops:
  6.5 0.7 all-gather.4.cloned.1.call-update
  7.3 1.4 fusion.47
  9.4 19.7 %all-gather.4.cloned.1.call-done = bf16[512,1152]{1,0:T(8,128)(2,1)} async-done(((bf16[128,1152]{1,0:T(8,128)(2,1)}), bf16[512,1152]{1,0:T(8,128)(2,1)}) %all-gather.4.cloned.1.call-update) | async-done | bytes 1179664 | tf_op jit(solution)/shard_map/all_gather | solution.py:63
  29.1 1.6 fusion.6
  30.7 2.7 %convolution_convert_fusion.2 = bf16[512,864]{0,1:T(8,128)(2,1)S(1)} fusion(bf16[1152,864]{0,1:T(8,128)(2,1)S(1)} %bitcast.67, bf16[512,1152]{1,0:T(8,128)(2,1)} %all-gather.4.cloned.1.call-done, f32[512]{0:T(512)S(1)} %add_rsqrt_fusion.3), kind=kOutput, calls=%fused_computation.27 | convolution fusion | flops 1021427712 | bytes 4057088 | tf_op jit(solution)/shard_map/dot_general | solution.py:30
  33.4 3.6 %fusion.49 = (f32[4,512]{1,0:T(4,128)S(1)}, f32[4,512,512]{1,2,0:T(8,128)}) fusion(pred[512]{0:T(512)(128)(4,1)S(1)} %iota_compare_fusion.1, bf16[512,3,4,72]{0,3,2,1:T(8,128)(2,1)S(1)} %bitcast.73), kind=kOutput, calls=%fused_computation.74 | convolution fusion | flops 155189760 | bytes 4792832 | tf_op jit(solution)/shard_map/sub | solution.py:40
  36.9 2.7 %fusion.23 = bf16[4,72,512]{2,1,0:T(8,128)(2,1)S(1)} fusion(f32[4,512,512]{1,2,0:T(8,128)} %get-tuple-element.13, f32[4,512]{1,0:T(4,128)S(1)} %get-tuple-element.12, bf16[512,3,4,72]{0,3,2,1:T(8,128)(2,1)S(1)} %bitcast.74), kind=kOutput, calls=%fused_computation.32 | convolution fusion | flops 153239552 | bytes 4792320 | tf_op jit(solution)/shard_map/hts,shd->thd/dot_general | solution.py:42
  39.7 1.9 convolution_convert_fusion.1
  43.6 35.8 %all-reduce.2.cloned.1.call-done = bf16[512,1152]{1,0:T(8,128)(2,1)} async-done(((bf16[512,1152]{1,0:T(8,128)(2,1)}), bf16[512,1152]{1,0:T(8,128)(2,1)}) %all-reduce.2.cloned.1.call-update) | async-done | bytes 1179664 | tf_op jit(solution)/shard_map/psum | solution.py:66
  79.4 1.9 multiply_reduce_fusion
  81.3 1.7 fusion.22
  83.1 4.2 %dynamic_update_slice.3 = bf16[1024,512]{1,0:T(8,128)(2,1)S(1)} dynamic-update-slice(bf16[1024,512]{1,0:T(8,128)(2,1)S(1)} %broadcast_in_dim.62, bf16[512,512]{1,0:T(8,128)(2,1)} %fusion.22, s32[]{:T(128)S(6)} %select_n.31, s32[]{:T(128)} %constant.36.clone.1) | dynamic-update-slice | bytes 1048580 | tf_op jit(solution)/shard_map/dynamic_update_slice | solution.py:72
  87.3 0.8 slice.36
  88.1 4.2 %collective-permute-start = (bf16[512,512]{1,0:T(8,128)(2,1)}, bf16[512,512]{1,0:T(8,128)(2,1)}, u32[]{:S(2)}, u32[]{:S(2)}) collective-permute-start(bf16[512,512]{1,0:T(8,128)(2,1)} %slice.36), channel_id=1, source_target_pairs={{0,4},{4,8},{8,12},{12,16},{16,20},{20,24},{24,28},{1,5},{5,9},{9,... | collective-permute-start | bytes 1572872 | tf_op jit(solution)/shard_map/ppermute | solution.py:19
  93.6 0.6 fusion.38
  94.2 1.3 fusion.37
  95.5 7.3 %collective-permute-done = bf16[512,512]{1,0:T(8,128)(2,1)} collective-permute-done((bf16[512,512]{1,0:T(8,128)(2,1)}, bf16[512,512]{1,0:T(8,128)(2,1)}, u32[]{:S(2)}, u32[]{:S(2)}) %collective-permute-start) | collective-permute-done | bytes 524320 | tf_op jit(solution)/shard_map/ppermute | solution.py:19
  102.8 2.2 %slice_select_fusion = bf16[512,512]{1,0:T(8,128)(2,1)} fusion(bf16[1024,512]{1,0:T(8,128)(2,1)S(1)} %dynamic_update_slice.3, bf16[512,512]{1,0:T(8,128)(2,1)} %collective-permute-done, bf16[512,512]{1,0:T(8,128)(2,1)} %param.13, pred[512]{0:T(512)(128)(4,1)S(1)} %fusion.37, pred[512]{0:T(512)(128)(4,1)S(1)} %fusion.38), kind=kLoop, calls=%fused_computation.41 | loop fusion | flops 524288 | bytes 2098176 | tf_op jit(solution)/shard_map/jit(_where)/select_n | solution.py:79
  105.3 8.9 %copy.27 = bf16[2048,3,512]{0,2,1:T(8,128)(2,1)} copy(bf16[2048,3,512]{2,0,1:T(8,128)(2,1)} %param.17) | data formatting | bytes 12582912 | tf_op args[7]
  114.1 14.7 %all-gather.6.cloned.1.call-done = bf16[512,2048]{1,0:T(8,128)(2,1)} async-done(((bf16[512,512]{1,0:T(8,128)(2,1)}), bf16[512,2048]{1,0:T(8,128)(2,1)}) %all-gather.6.cloned.1.call-update) | async-done | bytes 2097168 | tf_op jit(solution)/shard_map/all_gather | solution.py:82
  128.8 2.1 %fusion.1 = f32[512]{0:T(512)S(1)} fusion(bf16[512,2048]{1,0:T(8,128)(2,1)} %all-gather.6.cloned.1.call-done), kind=kLoop, calls=%fused_computation.3 | loop fusion | flops 3145216 | bytes 2099200 | tf_op jit(solution)/shard_map/reduce_sum | solution.py:24
  130.9 8.1 %convolution_convert_fusion = bf16[512,1536]{1,0:T(8,128)(2,1)} fusion(bf16[2048,1536]{0,1:T(8,128)(2,1)} %bitcast.68, bf16[512,2048]{1,0:T(8,128)(2,1)} %all-gather.6.cloned.1.call-done, f32[512]{0:T(512)S(1)} %add_rsqrt_fusion.1), kind=kOutput, calls=%fused_computation.14 | convolution fusion | flops 3225157632 | bytes 9963520 | tf_op jit(solution)/shard_map/dot_general | solution.py:85
  139.1 4.0 %reshape.94 = bf16[512,3,4,128]{3,2,1,0:T(4,128)(2,1)} reshape(bf16[512,1536]{1,0:T(8,128)(2,1)} %convolution_convert_fusion) | data formatting | bytes 3145728 | tf_op jit(solution)/shard_map/reshape | solution.py:88
  143.0 2.9 %fusion.46 = (bf16[512,1,4,128]{3,2,1,0:T(4,128)(2,1)}, bf16[512,1,4,128]{3,2,1,0:T(4,128)(2,1)}, bf16[512,1,4,128]{3,2,1,0:T(4,128)(2,1)S(1)}) fusion(bf16[512,3,4,128]{3,2,1,0:T(4,128)(2,1)} %reshape.94), kind=kLoop, calls=%fused_computation.71 | loop fusion | bytes 3145728 | tf_op jit(solution)/shard_map/slice | solution.py:89
  145.9 1.3 copy.42
  147.2 2.0 convolution_convert_fusion.4
  149.3 2.6 %fusion.29 = f32[4,512,512]{2,1,0:T(8,128)} fusion(bf16[512,1,4,128]{0,3,2,1:T(8,128)(2,1)S(1)} %copy.42, bf16[512,1,4,128]{3,2,1,0:T(4,128)(2,1)S(1)} %get-tuple-element.7), kind=kOutput, calls=%fused_computation.44 | convolution fusion | flops 268435456 | bytes 5242880 | tf_op jit(solution)/shard_map/thd,shd->hts/dot_general | solution.py:101
  151.9 37.7 %all-gather.8.cloned.1.call-done = bf16[32,128,128]{2,1,0:T(8,128)(2,1)} async-done(((bf16[4,128,128]{2,1,0:T(8,128)(2,1)}), bf16[32,128,128]{2,1,0:T(8,128)(2,1)}) %all-gather.8.cloned.1.call-update) | async-done | bytes 1048592 | tf_op jit(solution)/shard_map/all_gather | solution.py:91
  189.6 2.0 fusion.27
  191.6 1.6 fusion.32
  193.2 5.1 %multiply_reduce_fusion.1 = (f32[512,4]{0,1:T(4,128)S(1)}, f32[512,4,128]{0,2,1:T(8,128)S(1)}) fusion(f32[4,128,512]{2,1,0:T(8,128)S(1)} %fusion.32, f32[4,512,512]{2,1,0:T(8,128)} %fusion.29, pred[512,512]{1,0:T(8,128)(4,1)S(1)} %iota_compare_fusion, bf16[512,1,4,128]{3,2,1,0:T(4,128)(2,1)S(1)} %copy-done.2), kind=kOutput, calls=%fused_computation.39 | convolution fusion | flops 1612445696 | bytes 7086080 | tf_op jit(solution)/shard_map/hts,she->the/dot_general | solution.py:104
  198.5 1.0 copy.34
  (29 shorter events, 1.5 us)
Async XLA Ops:
  6.5 24.1 %copy-start = (bf16[1152,3,288]{0,2,1:T(8,128)(2,1)S(1)}, bf16[1152,3,288]{0,2,1:T(8,128)(2,1)}, u32[]{:S(2)}) copy-start(bf16[1152,3,288]{0,2,1:T(8,128)(2,1)} %param.14) | copy-start | bytes 5971972
  6.5 22.5 %all-gather.4.cloned.1.call-start = ((), (), s32[]{:S(2)}) async-start(), calls=%async_computation | async-start | bytes 1474560 | tf_op jit(solution)/shard_map/all_gather | solution.py:63
  7.3 72.1 %all-reduce.2.cloned.1.call-start = ((), (), s32[]{:S(2)}) async-start(), calls=%async_computation.1 | async-start | bytes 2359296 | tf_op jit(solution)/shard_map/psum | solution.py:66
  36.9 2.8 %copy-start.6 = (bf16[288,1152]{1,0:T(8,128)(2,1)S(1)}, bf16[288,1152]{1,0:T(8,128)(2,1)}, u32[]{:S(2)}) copy-start(bf16[288,1152]{1,0:T(8,128)(2,1)} %param.15) | copy-start | bytes 1990660
  39.7 39.7 %copy-start.1 = (bf16[512,1152]{1,0:T(8,128)(2,1)S(1)}, bf16[512,1152]{1,0:T(8,128)(2,1)}, u32[]{:S(2)}) copy-start(bf16[512,1152]{1,0:T(8,128)(2,1)} %all-gather.4.cloned.1.call-done) | copy-start | bytes 3538948
  41.6 87.2 %all-gather.6.cloned.1.call-start = ((), (), s32[]{:S(2)}) async-start(), calls=%async_computation.2 | async-start | bytes 2621440 | tf_op jit(solution)/shard_map/all_gather | solution.py:82
  79.4 1.9 copy-start.3
  79.4 2.0 copy-start.5
  88.1 14.7 %collective-permute-start = (bf16[512,512]{1,0:T(8,128)(2,1)}, bf16[512,512]{1,0:T(8,128)(2,1)}, u32[]{:S(2)}, u32[]{:S(2)}) collective-permute-start(bf16[512,512]{1,0:T(8,128)(2,1)} %slice.36), channel_id=1, source_target_pairs={{0,4},{4,8},{8,12},{12,16},{16,20},{20,24},{24,28},{1,5},{5,9},{9,... | collective-permute-start | bytes 1572872 | tf_op jit(solution)/shard_map/ppermute | solution.py:19
  105.0 84.6 %all-gather.8.cloned.1.call-start = ((), (), s32[]{:S(2)}) async-start(), calls=%async_computation.3 | async-start | bytes 1179648 | tf_op jit(solution)/shard_map/all_gather | solution.py:91
  151.9 41.3 %copy-start.2 = (bf16[512,1,4,128]{3,2,1,0:T(4,128)(2,1)S(1)}, bf16[512,1,4,128]{3,2,1,0:T(4,128)(2,1)}, u32[]{:S(2)}) copy-start(bf16[512,1,4,128]{3,2,1,0:T(4,128)(2,1)} %get-tuple-element.5) | copy-start | bytes 1572868
  193.2 5.1 %copy-start.4 = (f32[512]{0:T(512)S(1)}, f32[512]{0:T(512)}, u32[]{:S(2)}) copy-start(f32[512]{0:T(512)} %param.18) | copy-start | bytes 6148
Sparse Core Ops, SparseCore 0:
  8.9 20.1 all-gather.3
  41.7 37.5 all-reduce.1
  105.2 23.6 all-gather.5
  149.3 40.2 all-gather.7
where the time goes:
time: 207 us; the launch traced here: 206 us
  waiting for transfers between devices  116 us (56%)
  matrix products  33.9 us (16%)
  local copies, waits for them, and re-layouts  24.6 us (12%)
  between operations  16.5 us (8%)
  other arithmetic  10.6 us (5%)
  starting transfers between devices  4.46 us (2%)
    all_gather x1, waiting for transfers between devices, local(): lax.all_gather(delta.astype(jnp.bfloat16), 'ctx', axis=0, tiled=True)  37.7 us
    psum x1, waiting for transfers between devices, local(): lax.psum(partial_value.astype(jnp.bfloat16), 'head').astype(jnp.float32)  35.8 us
    all_gather x1, waiting for transfers between devices, local(): frame = lax.all_gather(patches, 'head', axis=0, tiled=True)  19.7 us
    all_gather x1, waiting for transfers between devices, local(): full = lax.all_gather(sequence, 'head', axis=1, tiled=True)  14.7 us
    unnamed x16, local copies, waits for them, and re-layouts  10.3 us
    dot_general x1, matrix products, local(): jnp.dot(unit, layer_qkv.reshape(layer_qkv.shape[0], -1), preferred_elemen...  8.13 us
    ppermute x1, waiting for transfers between devices, shifted(): lax.ppermute(value, axis, [(source, source + steps) for source in range(l...  7.29 us
    reduce_sum x3, other arithmetic, unit_rows(): jnp.mean(values * values, axis=-1, keepdims=True) + EPS  5.53 us
  transfers between devices with their start and end apart: 5, of which 5 were waited for; matrix products, arithmetic and copies ran while one was open for 8% of the time, Pallas kernels for 0%

commit v1 on v0

--- a/solution.py
+++ b/solution.py
@@ -10,13 +10,62 @@
 
 
 EPS = 1e-06
-HIGH = lax.Precision.HIGHEST
 
 
 def shifted(value, axis, steps):
     count = lax.axis_size(axis)
-    leading, last = (max(0, -steps), min(count, count - steps))
-    return lax.ppermute(value, axis, [(source, source + steps) for source in range(leading, last)])
+    return lax.ppermute(value, axis, [(source, source + steps) for source in range(count - steps)])
+
+
+def swapped(value, axis, bit):
+    count = lax.axis_size(axis)
+    return lax.ppermute(value, axis, [(source, source ^ bit) for source in range(count)])
+
+
+def gathered(value, axis):
+    count = lax.axis_size(axis)
+    blocks = [value] + [None] * (count - 1)
+    far = count // 2
+    stride = far
+    known = [0]
+    while stride >= 1:
+        fresh = []
+        for key in known:
+            blocks[key ^ stride] = swapped(blocks[key], axis, stride)
+            fresh.append(key ^ stride)
+        known = known + fresh
+        stride //= 2
+    return blocks
+
+
+def in_order(blocks, axis):
+    place = lax.axis_index(axis)
+    count = len(blocks)
+    stack = list(blocks)
+    stride = 1
+    while stride < count:
+        flip = (place & stride) != 0
+        stack = [jnp.where(flip, stack[key ^ stride], stack[key]) for key in range(count)]
+        stride *= 2
+    return stack
+
+
+def earlier_sum(value, axis):
+    count = lax.axis_size(axis)
+    place = lax.axis_index(axis)
+    wide = lambda part: part.astype(jnp.float32)
+    slim = lambda part: part.astype(jnp.bfloat16)
+    partner = swapped(value, axis, 1)
+    total = wide(value) + wide(partner)
+    before = jnp.where(place % 2 == 1, wide(partner), 0.0)
+    pairs = jnp.zeros_like(total)
+    step = 1
+    while 2 * step < count:
+        arrived = wide(shifted(slim(total), axis, 2 * step))
+        pairs = pairs + arrived
+        total = total + arrived
+        step *= 2
+    return before + pairs
 
 
 def unit_rows(values):
@@ -60,11 +109,17 @@
     span = text_rows.shape[0]
     length = lax.dynamic_index_in_dim(clip_len, place, keepdims=False)
     start = lax.dynamic_index_in_dim(clip_start, place, keepdims=False)
-    frame = lax.all_gather(patches, "head", axis=0, tiled=True)
+    frame = jnp.concatenate(in_order(gathered(patches, "head"), "head"), axis=0)
+    outs = gathered(vision_out, "head")
     context = clip_attention(frame, length, vision_qkv, VIT_HEADS // groups)
-    partial_value = jnp.dot(context, vision_out, preferred_element_type=jnp.float32)
-    total = lax.psum(partial_value.astype(jnp.bfloat16), "head").astype(jnp.float32)
-    merged = unit_rows(frame.astype(jnp.float32) + total).astype(jnp.bfloat16)
+    contexts = gathered(context, "head")
+    total = frame.astype(jnp.float32)
+    total = total + jnp.dot(
+        jnp.concatenate(contexts, axis=1),
+        jnp.concatenate(outs, axis=0),
+        preferred_element_type=jnp.float32,
+    )
+    merged = unit_rows(total).astype(jnp.bfloat16)
     visual = jnp.dot(merged, projector, preferred_element_type=jnp.float32).astype(jnp.bfloat16)
     within = jnp.arange(span)
     visual = jnp.where((within < length)[:, None], visual, jnp.zeros_like(visual))
@@ -79,7 +134,7 @@
     sequence = jnp.where(
         own_live[:, None], window[:span], jnp.where(prior_live[:, None], arrived, text_rows)
     )
-    full = lax.all_gather(sequence, "head", axis=1, tiled=True)
+    full = jnp.concatenate(in_order(gathered(sequence, "head"), "head"), axis=1)
     unit = unit_rows(full).astype(jnp.bfloat16)
     heads = HEADS // groups
     layer_mix = jnp.dot(
@@ -88,21 +143,14 @@
     layer_mix = layer_mix.astype(jnp.bfloat16).reshape(span, 3, heads, HD)
     query, keys, values = (layer_mix[:, 0], layer_mix[:, 1], layer_mix[:, 2])
     delta = jnp.einsum("shd,she->hde", keys, values, preferred_element_type=jnp.float32)
-    piece = lax.all_gather(delta.astype(jnp.bfloat16), "ctx", axis=0, tiled=True).astype(
-        jnp.float32
-    )
-    count = piece.shape[0] // heads
-    owners = jnp.arange(count)
-    keep = (owners < place).astype(jnp.float32)
-    carried = jnp.zeros_like(delta) + jnp.einsum(
-        "n,nhde->hde", keep, piece.reshape(count, heads, HD, HD), precision=HIGH
-    )
-    carried = carried + state_in
+    carried = earlier_sum(delta.astype(jnp.bfloat16), "ctx") + state_in
     weights = jnp.einsum("thd,shd->hts", query, keys, preferred_element_type=jnp.float32)
     causal = within[:, None] >= within[None, :]
-    weights = jnp.where(causal[None], weights, 0.0)
-    intra = jnp.einsum("hts,she->the", weights, values.astype(jnp.float32), precision=HIGH)
-    inter = jnp.einsum("thd,hde->the", query.astype(jnp.float32), carried, precision=HIGH)
+    weights = jnp.where(causal[None], weights, 0.0).astype(jnp.bfloat16)
+    intra = jnp.einsum("hts,she->the", weights, values, preferred_element_type=jnp.float32)
+    inter = jnp.einsum(
+        "thd,hde->the", query, carried.astype(jnp.bfloat16), preferred_element_type=jnp.float32
+    )
     lin = inter + intra
     scaled = lin * lax.rsqrt(jnp.mean(lin * lin, axis=-1, keepdims=True) + EPS)
     scaled = scaled * head_gain.reshape(heads, HD)

time: 207 us -> 144 us (0.70)
  waiting for transfers between devices: 116 us -> 48.2 us
  starting transfers between devices: 4.46 us -> 25.5 us
  between operations: 16.5 us -> 3.22 us
  matrix products: 33.9 us -> 27.2 us
  local copies, waits for them, and re-layouts: 24.6 us -> 26.8 us
    all_gather x3 -> x0, waiting for transfers between devices: 72.1 us -> none  [the longest x1 37.7 us: local(): lax.all_gather(delta.astype(jnp.bfloat16), 'ctx', axis=0, tiled=True)]
    ppermute x1 -> x16, waiting for transfers between devices: 7.29 us -> 48.2 us  [the longest x13 35.5 us: swapped(): lax.ppermute(value, axis, [(source, source ^ bit) for source in range(cou...]
    psum x1 -> x0, waiting for transfers between devices: 35.8 us -> none  [local(): lax.psum(partial_value.astype(jnp.bfloat16), 'head').astype(jnp.float32)]
    ppermute x1 -> x16, starting transfers between devices: 4.16 us -> 25.5 us  [the longest x3 14.4 us: shifted(): lax.ppermute(value, axis, [(source, source + steps) for source in range(c...]
    reduce_sum x3 -> x2, other arithmetic: 5.53 us -> 0.79 us  [unit_rows(): jnp.mean(values * values, axis=-1, keepdims=True) + EPS]
    dot_general x1, matrix products: 8.13 us -> 4.67 us  [local(): jnp.dot(unit, layer_qkv.reshape(layer_qkv.shape[0], -1), preferred_elemen...]
    select_n x0 -> x2, other arithmetic: none -> 2.94 us  [in_order(): jnp.where(flip, stack[key ^ stride], stack[key])]
    dot_general x5 -> x3, matrix products: 13.1 us -> 10.2 us  [the longest x1 4.15 us: local(): jnp.dot(jnp.concatenate(contexts, axis=1), jnp.concatenate(outs, axis=0),...]
  transfers between devices with their start and end apart: 5 -> 16, of which waited for: 5 -> 8; matrix products, arithmetic and copies ran while one was open for 8% -> 18% of each run, Pallas kernels for 0% -> 0%
where the time goes in v1:
time: 144 us; the launch traced here: 142 us
  waiting for transfers between devices  48.2 us (33%)
  matrix products  27.2 us (19%)
  local copies, waits for them, and re-layouts  26.8 us (19%)
  starting transfers between devices  25.5 us (18%)
  other arithmetic  11.4 us (8%)
  between operations  3.22 us (2%)
    ppermute x13, waiting for transfers between devices, swapped(): lax.ppermute(value, axis, [(source, source ^ bit) for source in range(cou...  35.5 us
    ppermute x3, starting transfers between devices, shifted(): lax.ppermute(value, axis, [(source, source + steps) for source in range(c...  14.4 us
    ppermute x3, waiting for transfers between devices, shifted(): lax.ppermute(value, axis, [(source, source + steps) for source in range(c...  12.7 us
    unnamed x14, local copies, waits for them, and re-layouts  11.7 us
    ppermute x13, starting transfers between devices, swapped(): lax.ppermute(value, axis, [(source, source ^ bit) for source in range(cou...  11 us
    dot_general x1, matrix products, local(): jnp.dot(unit, layer_qkv.reshape(layer_qkv.shape[0], -1), preferred_elemen...  4.67 us
    sub x1, matrix products, clip_attention(): powers = jnp.exp(scores - highest)  4.64 us
    dynamic_update_slice x1, local copies, waits for them, and re-layouts, local(): window = lax.dynamic_update_slice_in_dim(window, visual, start, 0)  4.19 us
  transfers between devices with their start and end apart: 16, of which 8 were waited for; matrix products, arithmetic and copies ran while one was open for 18% of the time, Pallas kernels for 0%

profile of v1, /device:TPU:0, one launch (start us, length us, event | category | flops | bytes accessed | tf_op | source)
XLA Modules:
  0.0 142.4 jit_solution(15293751509944469684)
XLA Ops:
  0.0 3.0 %collective-permute-start = (bf16[128,1152]{1,0:T(8,128)(2,1)}, bf16[128,1152]{1,0:T(8,128)(2,1)S(1)}, u32[]{:S(2)}, u32[]{:S(2)}) collective-permute-start(bf16[128,1152]{1,0:T(8,128)(2,1)} %param.10), channel_id=1, source_target_pairs={{0,2},{1,3},{2,0},{3,1},{4,6},{5,7},{6,4},{7,5},{8,10},{9,11},{10,... | collective-permute-start | bytes 884744 | tf_op jit(solution)/shard_map/ppermute | solution.py:22
  3.0 7.2 %collective-permute-done = bf16[128,1152]{1,0:T(8,128)(2,1)S(1)} collective-permute-done((bf16[128,1152]{1,0:T(8,128)(2,1)}, bf16[128,1152]{1,0:T(8,128)(2,1)S(1)}, u32[]{:S(2)}, u32[]{:S(2)}) %collective-permute-start) | collective-permute-done | bytes 294944 | tf_op jit(solution)/shard_map/ppermute | solution.py:22
  10.2 1.7 %collective-permute-start.7 = (bf16[288,1152]{1,0:T(8,128)(2,1)}, bf16[288,1152]{1,0:T(8,128)(2,1)}, u32[]{:S(2)}, u32[]{:S(2)}) collective-permute-start(bf16[288,1152]{1,0:T(8,128)(2,1)} %param.15), channel_id=1, source_target_pairs={{0,2},{1,3},{2,0},{3,1},{4,6},{5,7},{6,4},{7,5},{8,10},{9,11},{10,... | collective-permute-start | bytes 1990664 | tf_op jit(solution)/shard_map/ppermute | solution.py:22
  12.2 1.4 fusion.58
  16.5 2.4 %convolution_convert_fusion.1 = bf16[512,864]{0,1:T(8,128)(2,1)} fusion(bf16[1152,864]{0,1:T(8,128)(2,1)S(1)} %bitcast.63, f32[512]{0:T(512)S(1)} %add_rsqrt_fusion.3, bf16[128,1152]{1,0:T(8,128)(2,1)S(1)} %get-tuple-element.15, bf16[128,1152]{1,0:T(8,128)(2,1)S(1)} %get-tuple-element.14, bf16[128,1152]{1,0:T(8,128)(2,1)S(1)} %get-tuple-element.13, ...), kind=kOutput, calls=%fused_computation.32 | convolution fusion | flops 1025556480 | bytes 4057088 | tf_op jit(solution)/shard_map/dot_general | solution.py:79
  18.9 4.6 %fusion.60 = (f32[4,512]{1,0:T(4,128)S(1)}, f32[4,512,512]{1,2,0:T(8,128)}) fusion(pred[512]{0:T(512)(128)(4,1)S(1)} %iota_compare_fusion.1, bf16[512,3,4,72]{0,3,2,1:T(8,128)(2,1)} %bitcast.70), kind=kOutput, calls=%fused_computation.109 | convolution fusion | flops 155189760 | bytes 4792832 | tf_op jit(solution)/shard_map/sub | solution.py:89
  23.5 4.3 %collective-permute-done.7 = bf16[288,1152]{1,0:T(8,128)(2,1)} collective-permute-done((bf16[288,1152]{1,0:T(8,128)(2,1)}, bf16[288,1152]{1,0:T(8,128)(2,1)}, u32[]{:S(2)}, u32[]{:S(2)}) %collective-permute-start.7) | collective-permute-done | bytes 663584 | tf_op jit(solution)/shard_map/ppermute | solution.py:22
  27.8 2.8 %fusion.23 = bf16[4,72,512]{2,1,0:T(8,128)(2,1)S(1)} fusion(f32[4,512,512]{1,2,0:T(8,128)} %get-tuple-element.21, f32[4,512]{1,0:T(4,128)S(1)} %get-tuple-element.20, bf16[512,3,4,72]{0,3,2,1:T(8,128)(2,1)} %bitcast.71), kind=kOutput, calls=%fused_computation.37 | convolution fusion | flops 153239552 | bytes 4792320 | tf_op jit(solution)/shard_map/hts,shd->thd/dot_general | solution.py:91
  30.6 1.8 %collective-permute-start.4 = (bf16[512,288]{0,1:T(8,128)(2,1)S(1)}, bf16[512,288]{0,1:T(8,128)(2,1)}, u32[]{:S(2)}, u32[]{:S(2)}) collective-permute-start(bf16[512,288]{0,1:T(8,128)(2,1)S(1)} %bitcast.67), channel_id=1, source_target_pairs={{0,2},{1,3},{2,0},{3,1},{4,6},{5,7},{6,4},{7,5},{8,10},{9,11},{10,... | collective-permute-start | bytes 884744 | tf_op jit(solution)/shard_map/ppermute | solution.py:22
  32.7 7.6 %collective-permute-done.4 = bf16[512,288]{0,1:T(8,128)(2,1)} collective-permute-done((bf16[512,288]{0,1:T(8,128)(2,1)S(1)}, bf16[512,288]{0,1:T(8,128)(2,1)}, u32[]{:S(2)}, u32[]{:S(2)}) %collective-permute-start.4) | collective-permute-done | bytes 294944 | tf_op jit(solution)/shard_map/ppermute | solution.py:22
  42.1 4.1 %multiply_reduce_fusion = (f32[512]{0:T(512)S(1)}, f32[512,1152]{1,0:T(8,128)S(1)}) fusion(bf16[288,1152]{1,0:T(8,128)(2,1)} %collective-permute-done.8, bf16[288,1152]{1,0:T(8,128)(2,1)} %collective-permute-done.7, bf16[288,1152]{1,0:T(8,128)(2,1)} %collective-permute-done.6, bf16[288,1152]{1,0:T(8,128)(2,1)} %param.15, ...), kind=kOutput, calls=%fused_computation.24 | convolution fusion | flops 1380777472 | bytes 7374848 | tf_op jit(solution)/shard_map/dot_general | solution.py:117
  48.4 4.2 %dynamic_update_slice.3 = bf16[1024,512]{1,0:T(8,128)(2,1)S(1)} dynamic-update-slice(bf16[1024,512]{1,0:T(8,128)(2,1)S(1)} %broadcast_in_dim.66, bf16[512,512]{1,0:T(8,128)(2,1)} %copy.20, s32[]{:T(128)S(6)} %select_n.136, s32[]{:T(128)} %constant.48.clone.1) | dynamic-update-slice | bytes 1048580 | tf_op jit(solution)/shard_map/dynamic_update_slice | solution.py:127
  53.4 4.5 %collective-permute-start.9 = (bf16[512,512]{1,0:T(8,128)(2,1)}, bf16[512,512]{1,0:T(8,128)(2,1)}, u32[]{:S(2)}, u32[]{:S(2)}) collective-permute-start(bf16[512,512]{1,0:T(8,128)(2,1)} %slice.36), channel_id=1, source_target_pairs={{0,4},{4,8},{8,12},{12,16},{16,20},{20,24},{24,28},{1,5},{5,9},{9,... | collective-permute-start | bytes 1572872 | tf_op jit(solution)/shard_map/ppermute | solution.py:17
  61.0 8.2 %collective-permute-done.9 = bf16[512,512]{1,0:T(8,128)(2,1)} collective-permute-done((bf16[512,512]{1,0:T(8,128)(2,1)}, bf16[512,512]{1,0:T(8,128)(2,1)}, u32[]{:S(2)}, u32[]{:S(2)}) %collective-permute-start.9) | collective-permute-done | bytes 524320 | tf_op jit(solution)/shard_map/ppermute | solution.py:17
  69.2 2.2 %slice_select_fusion = bf16[512,512]{1,0:T(8,128)(2,1)} fusion(bf16[1024,512]{1,0:T(8,128)(2,1)S(1)} %dynamic_update_slice.3, bf16[512,512]{1,0:T(8,128)(2,1)} %collective-permute-done.9, bf16[512,512]{1,0:T(8,128)(2,1)} %param.13, pred[512]{0:T(512)(128)(4,1)S(1)} %fusion.49, pred[512]{0:T(512)(128)(4,1)S(1)} %fusion.50), kind=kLoop, calls=%fused_computation.52 | loop fusion | flops 524288 | bytes 2098176 | tf_op jit(solution)/shard_map/jit(_where)/select_n | solution.py:134
  71.4 1.5 %collective-permute-start.10 = (bf16[512,512]{1,0:T(8,128)(2,1)}, bf16[512,512]{1,0:T(8,128)(2,1)S(1)}, u32[]{:S(2)}, u32[]{:S(2)}) collective-permute-start(bf16[512,512]{1,0:T(8,128)(2,1)} %slice_select_fusion), channel_id=1, source_target_pairs={{0,2},{1,3},{2,0},{3,1},{4,6},{5,7},{6,4},{7,5},{8,10},{9,11},{10,... | collective-permute-start | bytes 1572872 | tf_op jit(solution)/shard_map/ppermute | solution.py:22
  72.9 12.2 %collective-permute-done.10 = bf16[512,512]{1,0:T(8,128)(2,1)S(1)} collective-permute-done((bf16[512,512]{1,0:T(8,128)(2,1)}, bf16[512,512]{1,0:T(8,128)(2,1)S(1)}, u32[]{:S(2)}, u32[]{:S(2)}) %collective-permute-start.10) | collective-permute-done | bytes 524320 | tf_op jit(solution)/shard_map/ppermute | solution.py:22
  85.1 8.8 %copy.21 = bf16[2048,3,512]{0,2,1:T(8,128)(2,1)} copy(bf16[2048,3,512]{2,0,1:T(8,128)(2,1)} %param.17) | data formatting | bytes 12582912 | tf_op args[7]
  94.0 1.6 %broadcast_select_fusion.7 = (bf16[512,512]{1,0:T(8,128)(2,1)S(1)}, bf16[512,512]{1,0:T(8,128)(2,1)S(1)}, bf16[512,512]{1,0:T(8,128)(2,1)S(1)}, bf16[512,512]{1,0:T(8,128)(2,1)S(1)}) fusion(pred[]{:T(512)S(6)} %ne.15, bf16[512,512]{1,0:T(8,128)(2,1)} %collective-permute-done.11, bf16[512,512]{1,0:T(8,128)(2,1)S(1)} %collective-permute-done.10, pred[]{:T(512)S(6)} %ne.16, ...), kind=kLoop, calls=%fused_computation.64 | loop fusion | flops 2097152 | bytes 4194306 | tf_op jit(solution)/shard_map/jit(_where)/select_n | solution.py:48
  97.0 4.7 %convolution_convert_fusion = bf16[512,1536]{1,0:T(8,128)(2,1)} fusion(bf16[2048,1536]{0,1:T(8,128)(2,1)S(1)} %bitcast.64, f32[512]{0:T(512)S(1)} %add_rsqrt_fusion.1, bf16[512,512]{1,0:T(8,128)(2,1)S(1)} %get-tuple-element.8, bf16[512,512]{1,0:T(8,128)(2,1)S(1)} %get-tuple-element.7, bf16[512,512]{1,0:T(8,128)(2,1)S(1)} %get-tuple-element.6, ...), kind=kOutput, calls=%fused_computation.13 | convolution fusion | flops 3232497664 | bytes 9963520 | tf_op jit(solution)/shard_map/dot_general | solution.py:140
  101.7 3.9 %reshape.91 = bf16[512,3,4,128]{3,2,1,0:T(4,128)(2,1)} reshape(bf16[512,1536]{1,0:T(8,128)(2,1)} %convolution_convert_fusion) | data formatting | bytes 3145728 | tf_op jit(solution)/shard_map/reshape | solution.py:143
  105.7 2.7 %fusion.57 = (bf16[512,1,4,128]{3,2,1,0:T(4,128)(2,1)}, bf16[512,1,4,128]{3,2,1,0:T(4,128)(2,1)S(1)}, bf16[512,1,4,128]{3,2,1,0:T(4,128)(2,1)S(1)}) fusion(bf16[512,3,4,128]{3,2,1,0:T(4,128)(2,1)} %reshape.91), kind=kLoop, calls=%fused_computation.106 | loop fusion | bytes 3145728 | tf_op jit(solution)/shard_map/slice | solution.py:144
  109.5 1.5 %convolution_convert_fusion.3 = bf16[4,128,128]{2,1,0:T(8,128)(2,1)S(1)} fusion(bf16[512,1,4,128]{0,3,2,1:T(8,128)(2,1)} %copy.31, bf16[512,1,4,128]{3,2,1,0:T(4,128)(2,1)} %get-tuple-element.9), kind=kOutput, calls=%fused_computation.48 | convolution fusion | flops 67174400 | bytes 1179648 | tf_op jit(solution)/shard_map/shd,she->hde/dot_general | solution.py:145
  111.0 2.5 %collective-permute-start.13 = (bf16[4,128,128]{2,1,0:T(8,128)(2,1)S(1)}, bf16[4,128,128]{2,1,0:T(8,128)(2,1)S(1)}, u32[]{:S(2)}, u32[]{:S(2)}) collective-permute-start(bf16[4,128,128]{2,1,0:T(8,128)(2,1)S(1)} %convolution_convert_fusion.3), channel_id=1, source_target_pairs={{0,4},{4,0},{8,12},{12,8},{16,20},{20,16},{24,28},{28,24},{1,5},{5... | collective-permute-start | bytes 393224 | tf_op jit(solution)/shard_map/ppermute | solution.py:22
  113.6 4.2 %collective-permute-done.13 = bf16[4,128,128]{2,1,0:T(8,128)(2,1)S(1)} collective-permute-done((bf16[4,128,128]{2,1,0:T(8,128)(2,1)S(1)}, bf16[4,128,128]{2,1,0:T(8,128)(2,1)S(1)}, u32[]{:S(2)}, u32[]{:S(2)}) %collective-permute-start.13) | collective-permute-done | bytes 131104 | tf_op jit(solution)/shard_map/ppermute | solution.py:22
  117.8 4.6 %collective-permute-start.14 = (bf16[4,128,128]{2,1,0:T(8,128)(2,1)S(1)}, bf16[4,128,128]{2,1,0:T(8,128)(2,1)S(1)}, u32[]{:S(2)}, u32[]{:S(2)}) collective-permute-start(bf16[4,128,128]{2,1,0:T(8,128)(2,1)S(1)} %fusion.45), channel_id=1, source_target_pairs={{0,8},{4,12},{8,16},{12,20},{16,24},{20,28},{1,9},{5,13},{9,17},{1... | collective-permute-start | bytes 393224 | tf_op jit(solution)/shard_map/ppermute | solution.py:17
  122.4 2.5 %collective-permute-done.14 = bf16[4,128,128]{2,1,0:T(8,128)(2,1)S(1)} collective-permute-done((bf16[4,128,128]{2,1,0:T(8,128)(2,1)S(1)}, bf16[4,128,128]{2,1,0:T(8,128)(2,1)S(1)}, u32[]{:S(2)}, u32[]{:S(2)}) %collective-permute-start.14) | collective-permute-done | bytes 131104 | tf_op jit(solution)/shard_map/ppermute | solution.py:17
  125.6 5.4 %collective-permute-start.15 = (bf16[4,128,128]{2,1,0:T(8,128)(2,1)}, bf16[4,128,128]{2,1,0:T(8,128)(2,1)S(1)}, u32[]{:S(2)}, u32[]{:S(2)}) collective-permute-start(bf16[4,128,128]{2,1,0:T(8,128)(2,1)} %fusion.43), channel_id=1, source_target_pairs={{0,16},{4,20},{8,24},{12,28},{1,17},{5,21},{9,25},{13,29},{2,18},{... | collective-permute-start | bytes 393224 | tf_op jit(solution)/shard_map/ppermute | solution.py:17
  131.8 2.0 %collective-permute-done.15 = bf16[4,128,128]{2,1,0:T(8,128)(2,1)S(1)} collective-permute-done((bf16[4,128,128]{2,1,0:T(8,128)(2,1)}, bf16[4,128,128]{2,1,0:T(8,128)(2,1)S(1)}, u32[]{:S(2)}, u32[]{:S(2)}) %collective-permute-start.15) | collective-permute-done | bytes 131104 | tf_op jit(solution)/shard_map/ppermute | solution.py:17
  133.9 2.3 %fusion.37 = f32[4,128,512]{2,1,0:T(8,128)} fusion(bf16[512,1,4,128]{3,2,1,0:T(4,128)(2,1)S(1)} %get-tuple-element.11, f32[4,128,128]{2,1,0:T(8,128)} %param.19, bf16[4,128,128]{2,1,0:T(8,128)(2,1)S(1)} %collective-permute-done.13, bf16[4,128,128]{2,1,0:T(8,128)(2,1)S(1)} %collective-permute-done.14, bf16[4,128,128]{2,1,0:T(8,128)(2,1)S(1)} %collective-permute-done.15, ...), kind=kOutput, calls=%fused_computation.65 | convolution fusion | flops 67633152 | bytes 2228225 | tf_op jit(solution)/shard_map/thd,hde->the/dot_general | solution.py:151
  136.1 3.8 %multiply_reduce_fusion.1 = (f32[512,4]{0,1:T(4,128)S(1)}, f32[512,4,128]{0,2,1:T(8,128)}) fusion(f32[4,128,512]{2,1,0:T(8,128)} %fusion.37, pred[512,512]{1,0:T(8,128)(4,1)} %iota_compare_fusion, bf16[512,1,4,128]{0,3,2,1:T(8,128)(2,1)S(1)} %copy-done.3, bf16[512,1,4,128]{3,2,1,0:T(4,128)(2,1)S(1)} %get-tuple-element.11, ...), kind=kOutput, calls=%fused_computation.50 | convolution fusion | flops 539752448 | bytes 3940352 | tf_op jit(solution)/shard_map/hts,she->the/dot_general | solution.py:150
  140.0 1.4 multiply_convert_fusion.2
  (47 shorter events, 13.4 us)
Async XLA Ops:
  0.0 16.5 %copy-start = (bf16[1152,3,288]{0,2,1:T(8,128)(2,1)S(1)}, bf16[1152,3,288]{0,2,1:T(8,128)(2,1)}, u32[]{:S(2)}) copy-start(bf16[1152,3,288]{0,2,1:T(8,128)(2,1)} %param.14) | copy-start | bytes 5971972
  0.0 10.2 %collective-permute-start = (bf16[128,1152]{1,0:T(8,128)(2,1)}, bf16[128,1152]{1,0:T(8,128)(2,1)S(1)}, u32[]{:S(2)}, u32[]{:S(2)}) collective-permute-start(bf16[128,1152]{1,0:T(8,128)(2,1)} %param.10), channel_id=1, source_target_pairs={{0,2},{1,3},{2,0},{3,1},{4,6},{5,7},{6,4},{7,5},{8,10},{9,11},{10,... | collective-permute-start | bytes 884744 | tf_op jit(solution)/shard_map/ppermute | solution.py:22
  3.0 11.2 %collective-permute-start.2 = (bf16[128,1152]{1,0:T(8,128)(2,1)}, bf16[128,1152]{1,0:T(8,128)(2,1)S(1)}, u32[]{:S(2)}, u32[]{:S(2)}) collective-permute-start(bf16[128,1152]{1,0:T(8,128)(2,1)} %param.10), channel_id=1, source_target_pairs={{0,1},{1,0},{2,3},{3,2},{4,5},{5,4},{6,7},{7,6},{8,9},{9,8},{10,11... | collective-permute-start | bytes 884744 | tf_op jit(solution)/shard_map/ppermute | solution.py:22
  10.2 4.7 %collective-permute-start.1 = (bf16[128,1152]{1,0:T(8,128)(2,1)S(1)}, bf16[128,1152]{1,0:T(8,128)(2,1)}, u32[]{:S(2)}, u32[]{:S(2)}) collective-permute-start(bf16[128,1152]{1,0:T(8,128)(2,1)S(1)} %collective-permute-done), channel_id=1, source_target_pairs={{0,1},{1,0},{2,3},{3,2},{4,5},{5,4},{6,7},{7,6},{8,9},{9,8},{10,11... | collective-permute-start | bytes 884744 | tf_op jit(solution)/shard_map/ppermute | solution.py:22
  10.2 17.6 %collective-permute-start.7 = (bf16[288,1152]{1,0:T(8,128)(2,1)}, bf16[288,1152]{1,0:T(8,128)(2,1)}, u32[]{:S(2)}, u32[]{:S(2)}) collective-permute-start(bf16[288,1152]{1,0:T(8,128)(2,1)} %param.15), channel_id=1, source_target_pairs={{0,2},{1,3},{2,0},{3,1},{4,6},{5,7},{6,4},{7,5},{8,10},{9,11},{10,... | collective-permute-start | bytes 1990664 | tf_op jit(solution)/shard_map/ppermute | solution.py:22
  11.9 30.2 %collective-permute-start.6 = (bf16[288,1152]{1,0:T(8,128)(2,1)}, bf16[288,1152]{1,0:T(8,128)(2,1)}, u32[]{:S(2)}, u32[]{:S(2)}) collective-permute-start(bf16[288,1152]{1,0:T(8,128)(2,1)} %param.15), channel_id=1, source_target_pairs={{0,1},{1,0},{2,3},{3,2},{4,5},{5,4},{6,7},{7,6},{8,9},{9,8},{10,11... | collective-permute-start | bytes 1990664 | tf_op jit(solution)/shard_map/ppermute | solution.py:22
  14.1 0.7 copy-start.4
  27.8 14.3 %collective-permute-start.8 = (bf16[288,1152]{1,0:T(8,128)(2,1)}, bf16[288,1152]{1,0:T(8,128)(2,1)}, u32[]{:S(2)}, u32[]{:S(2)}) collective-permute-start(bf16[288,1152]{1,0:T(8,128)(2,1)} %collective-permute-done.7), channel_id=1, source_target_pairs={{0,1},{1,0},{2,3},{3,2},{4,5},{5,4},{6,7},{7,6},{8,9},{9,8},{10,11... | collective-permute-start | bytes 1990664 | tf_op jit(solution)/shard_map/ppermute | solution.py:22
  30.6 9.6 %collective-permute-start.4 = (bf16[512,288]{0,1:T(8,128)(2,1)S(1)}, bf16[512,288]{0,1:T(8,128)(2,1)}, u32[]{:S(2)}, u32[]{:S(2)}) collective-permute-start(bf16[512,288]{0,1:T(8,128)(2,1)S(1)} %bitcast.67), channel_id=1, source_target_pairs={{0,2},{1,3},{2,0},{3,1},{4,6},{5,7},{6,4},{7,5},{8,10},{9,11},{10,... | collective-permute-start | bytes 884744 | tf_op jit(solution)/shard_map/ppermute | solution.py:22
  32.4 9.7 %collective-permute-start.3 = (bf16[512,288]{0,1:T(8,128)(2,1)S(1)}, bf16[512,288]{0,1:T(8,128)(2,1)}, u32[]{:S(2)}, u32[]{:S(2)}) collective-permute-start(bf16[512,288]{0,1:T(8,128)(2,1)S(1)} %bitcast.68), channel_id=1, source_target_pairs={{0,1},{1,0},{2,3},{3,2},{4,5},{5,4},{6,7},{7,6},{8,9},{9,8},{10,11... | collective-permute-start | bytes 884744 | tf_op jit(solution)/shard_map/ppermute | solution.py:22
  40.2 1.9 %collective-permute-start.5 = (bf16[512,288]{0,1:T(8,128)(2,1)}, bf16[512,288]{0,1:T(8,128)(2,1)}, u32[]{:S(2)}, u32[]{:S(2)}) collective-permute-start(bf16[512,288]{0,1:T(8,128)(2,1)} %collective-permute-done.4), channel_id=1, source_target_pairs={{0,1},{1,0},{2,3},{3,2},{4,5},{5,4},{6,7},{7,6},{8,9},{9,8},{10,11... | collective-permute-start | bytes 884744 | tf_op jit(solution)/shard_map/ppermute | solution.py:22
  42.1 4.2 %copy-start.2 = (bf16[1152,512]{1,0:T(8,128)(2,1)S(1)}, bf16[1152,512]{1,0:T(8,128)(2,1)}, u32[]{:S(2)}) copy-start(bf16[1152,512]{1,0:T(8,128)(2,1)} %param.16) | copy-start | bytes 3538948
  53.4 15.8 %collective-permute-start.9 = (bf16[512,512]{1,0:T(8,128)(2,1)}, bf16[512,512]{1,0:T(8,128)(2,1)}, u32[]{:S(2)}, u32[]{:S(2)}) collective-permute-start(bf16[512,512]{1,0:T(8,128)(2,1)} %slice.36), channel_id=1, source_target_pairs={{0,4},{4,8},{8,12},{12,16},{16,20},{20,24},{24,28},{1,5},{5,9},{9,... | collective-permute-start | bytes 1572872 | tf_op jit(solution)/shard_map/ppermute | solution.py:17
  71.4 13.7 %collective-permute-start.10 = (bf16[512,512]{1,0:T(8,128)(2,1)}, bf16[512,512]{1,0:T(8,128)(2,1)S(1)}, u32[]{:S(2)}, u32[]{:S(2)}) collective-permute-start(bf16[512,512]{1,0:T(8,128)(2,1)} %slice_select_fusion), channel_id=1, source_target_pairs={{0,2},{1,3},{2,0},{3,1},{4,6},{5,7},{6,4},{7,5},{8,10},{9,11},{10,... | collective-permute-start | bytes 1572872 | tf_op jit(solution)/shard_map/ppermute | solution.py:22
  72.9 21.0 %collective-permute-start.12 = (bf16[512,512]{1,0:T(8,128)(2,1)}, bf16[512,512]{1,0:T(8,128)(2,1)S(1)}, u32[]{:S(2)}, u32[]{:S(2)}) collective-permute-start(bf16[512,512]{1,0:T(8,128)(2,1)} %slice_select_fusion), channel_id=1, source_target_pairs={{0,1},{1,0},{2,3},{3,2},{4,5},{5,4},{6,7},{7,6},{8,9},{9,8},{10,11... | collective-permute-start | bytes 1572872 | tf_op jit(solution)/shard_map/ppermute | solution.py:22
  85.1 8.8 %collective-permute-start.11 = (bf16[512,512]{1,0:T(8,128)(2,1)S(1)}, bf16[512,512]{1,0:T(8,128)(2,1)}, u32[]{:S(2)}, u32[]{:S(2)}) collective-permute-start(bf16[512,512]{1,0:T(8,128)(2,1)S(1)} %collective-permute-done.10), channel_id=1, source_target_pairs={{0,1},{1,0},{2,3},{3,2},{4,5},{5,4},{6,7},{7,6},{8,9},{9,8},{10,11... | collective-permute-start | bytes 1572872 | tf_op jit(solution)/shard_map/ppermute | solution.py:22
  93.9 3.1 %copy-start.1 = (bf16[2048,3,512]{0,2,1:T(8,128)(2,1)S(1)}, bf16[2048,3,512]{0,2,1:T(8,128)(2,1)}, u32[]{:S(2)}) copy-start(bf16[2048,3,512]{0,2,1:T(8,128)(2,1)} %copy.21) | copy-start | bytes 18874372
  109.5 26.6 %copy-start.3 = (bf16[512,1,4,128]{0,3,2,1:T(8,128)(2,1)S(1)}, bf16[512,1,4,128]{0,3,2,1:T(8,128)(2,1)}, u32[]{:S(2)}) copy-start(bf16[512,1,4,128]{0,3,2,1:T(8,128)(2,1)} %copy.31) | copy-start | bytes 1572868
  111.0 6.7 %collective-permute-start.13 = (bf16[4,128,128]{2,1,0:T(8,128)(2,1)S(1)}, bf16[4,128,128]{2,1,0:T(8,128)(2,1)S(1)}, u32[]{:S(2)}, u32[]{:S(2)}) collective-permute-start(bf16[4,128,128]{2,1,0:T(8,128)(2,1)S(1)} %convolution_convert_fusion.3), channel_id=1, source_target_pairs={{0,4},{4,0},{8,12},{12,8},{16,20},{20,16},{24,28},{28,24},{1,5},{5... | collective-permute-start | bytes 393224 | tf_op jit(solution)/shard_map/ppermute | solution.py:22
  117.8 7.1 %collective-permute-start.14 = (bf16[4,128,128]{2,1,0:T(8,128)(2,1)S(1)}, bf16[4,128,128]{2,1,0:T(8,128)(2,1)S(1)}, u32[]{:S(2)}, u32[]{:S(2)}) collective-permute-start(bf16[4,128,128]{2,1,0:T(8,128)(2,1)S(1)} %fusion.45), channel_id=1, source_target_pairs={{0,8},{4,12},{8,16},{12,20},{16,24},{20,28},{1,9},{5,13},{9,17},{1... | collective-permute-start | bytes 393224 | tf_op jit(solution)/shard_map/ppermute | solution.py:17
  125.6 8.2 %collective-permute-start.15 = (bf16[4,128,128]{2,1,0:T(8,128)(2,1)}, bf16[4,128,128]{2,1,0:T(8,128)(2,1)S(1)}, u32[]{:S(2)}, u32[]{:S(2)}) collective-permute-start(bf16[4,128,128]{2,1,0:T(8,128)(2,1)} %fusion.43), channel_id=1, source_target_pairs={{0,16},{4,20},{8,24},{12,28},{1,17},{5,21},{9,25},{13,29},{2,18},{... | collective-permute-start | bytes 393224 | tf_op jit(solution)/shard_map/ppermute | solution.py:17
  136.1 3.8 %copy-start.5 = (f32[512]{0:T(512)S(1)}, f32[512]{0:T(512)}, u32[]{:S(2)}) copy-start(f32[512]{0:T(512)} %param.18) | copy-start | bytes 6148

commit v2 on v0

v2 whole, which is shorter than its diff:
```python
import functools
import math

import jax
import jax.numpy as jnp
from jax import lax
from jax.experimental import pallas as pl
from jax.experimental.pallas import tpu as pltpu
from jax.sharding import PartitionSpec as P

VIT_HEADS = 16
VIT_HD = 72
HEADS = 16
HD = 128

EPS = 1e-06
LOW = -1e30
BLOCK = 128
VMEM = pl.BlockSpec(memory_space=pltpu.VMEM)
SMEM = pl.BlockSpec(memory_space=pltpu.SMEM)
F32 = jnp.float32
BF16 = jnp.bfloat16


def dot(left, right):
    return jnp.dot(left, right, preferred_element_type=F32)


def dot_t(left, right):
    return lax.dot_general(left, right, (((1,), (1,)), ((), ())), preferred_element_type=F32)


def shifted(value, axis, steps):
    count = lax.axis_size(axis)
    return lax.ppermute(value, axis, [(source, source + steps) for source in range(count - steps)])


def swapped(value, axis, bit):
    count = lax.axis_size(axis)
    return lax.ppermute(value, axis, [(source, source ^ bit) for source in range(count)])


def spread(value, axis):
    count = lax.axis_size(axis)
    blocks = {0: value}
    stride = count // 2
    while stride >= 1:
        for key in list(blocks):
            blocks[key ^ stride] = swapped(blocks[key], axis, stride)
        stride //= 2
    return [blocks[key] for key in range(count)]


def spread_prior(value):
    count = lax.axis_size("head")
    groups = lax.axis_size("ctx")
    stride = count // 2
    blocks = {0: shifted(value, "ctx", 1)}
    pairs = [
        (group * count + member, (group + 1) * count + (member ^ stride))
        for group in range(groups - 1)
        for member in range(count)
    ]
    blocks[stride] = lax.ppermute(value, ("ctx", "head"), pairs)
    stride //= 2
    while stride >= 1:
        for key in list(blocks):
            blocks[key ^ stride] = swapped(blocks[key], "head", stride)
        stride //= 2
    return [blocks[key] for key in range(count)]


def earlier_sum(value, axis):
    count = lax.axis_size(axis)
    place = lax.axis_index(axis)
    partner = swapped(value, axis, 1)
    total = value.astype(F32) + partner.astype(F32)
    before = jnp.where(place % 2 == 1, partner.astype(F32), 0.0)
    parts = [before]
    step = 1
    while 2 * step < count:
        arrived = shifted(total.astype(BF16), axis, 2 * step).astype(F32)
        parts.append(arrived)
        total = total + arrived
        step *= 2
    return sum(parts)


def clip_span(starts, lens, span, prior):
    place = lax.axis_index("ctx")
    if prior:
        source = jnp.maximum(place - 1, 0)
        shift = span - starts[source]
        length = jnp.where(place > 0, lens[source], 0)
    else:
        shift = -starts[place]
        length = lens[place]
    return shift, length, jnp.maximum(0, -shift), jnp.minimum(span, length - shift)


def clip_rows(rows, count, span):
    me = lax.axis_index("head")
    slot = lax.broadcasted_iota(jnp.int32, (1, span), 1)
    row = slot
    for key in range(count):
        inside = (slot >= key * rows) & (slot < (key + 1) * rows)
        row = jnp.where(inside, slot + ((me ^ key) - key) * rows, row)
    return row


def attend_kernel(prior, heads, block, starts, lens, *refs):
    count = len(refs) - (6 if prior else 5)
    pieces = refs[:count]
    weights, *olds, context, queries, keys, values = refs[count:]
    rows, width = pieces[0].shape
    span = rows * count
    inner = weights.shape[0] // 3
    size = inner // heads
    shift, length, first, last = clip_span(starts, lens, span, prior)
    context[...] = olds[0][...] if prior else jnp.zeros_like(context)
    row = clip_rows(rows, count, span)
    lane = lax.broadcasted_iota(jnp.int32, (1, inner), 1)
    owner = [(lane >= head * size) & (lane < (head + 1) * size) for head in range(heads)]
    groups = {}
    for head in range(heads):
        groups.setdefault(head * size // 128 * 128, []).append(head)

    @pl.when(last > first)
    def _():
        frame = jnp.concatenate([piece[...] for piece in pieces], axis=0)
        wide = frame.astype(F32)
        scale = lax.rsqrt(jnp.sum(wide * wide, axis=-1, keepdims=True) * (1.0 / width) + EPS)
        full = dot_t(frame, weights[...])
        queries[...] = (full[:, :inner] * (scale * (size**-0.5 * math.log2(math.e)))).astype(BF16)
        keys[...] = (full[:, inner : 2 * inner] * scale).astype(BF16)
        values[...] = (full[:, 2 * inner :] * scale).astype(BF16)

    def step(index, _):
        low = pl.multiple_of(index * block, block)
        place = low + lax.broadcasted_iota(jnp.int32, (block, 1), 0)
        live = (place >= first) & (place < last)
        pick = (place + shift == row) & live
        query = dot(jnp.where(pick, 1.0, 0.0).astype(BF16), queries[...])
        total = jnp.zeros((block, inner), F32)
        for base, members in groups.items():
            end = min(inner, base + 256)
            stack = jnp.concatenate(
                [jnp.where(owner[head], query, 0.0)[:, base:end].astype(BF16) for head in members], axis=0
            )
            scores = dot_t(stack, keys[:, base:end])
            scores = jnp.where(row < length, scores, LOW)
            powers = jnp.exp2(scores - jnp.max(scores, axis=-1, keepdims=True))
            mass = jnp.sum(powers, axis=-1, keepdims=True)
            mixed = dot(powers.astype(BF16), values[:, base:end]) / mass
            for place_in, head in enumerate(members):
                part = mixed[place_in * block : (place_in + 1) * block, :]
                sides = [part]
                if base:
                    sides = [jnp.zeros((block, base), F32)] + sides
                if end < inner:
                    sides = sides + [jnp.zeros((block, inner - end), F32)]
                total = jnp.where(owner[head], jnp.concatenate(sides, axis=1), total)
        here = pl.ds(low, block)
        if prior:
            context[here, :] = jnp.where(live, total, context[here, :].astype(F32)).astype(BF16)
        else:
            context[here, :] = total.astype(BF16)
        return 0

    lax.fori_loop(first // block, jnp.where(last > first, (last + block - 1) // block, 0), step, 0)


def attend(pieces, weights, starts, lens, heads, old=None):
    rows, width = pieces[0].shape
    span = rows * len(pieces)
    inner = weights.shape[0] // 3
    olds = [] if old is None else [old]
    return pl.pallas_call(
        functools.partial(attend_kernel, old is not None, heads, min(BLOCK, span)),
        out_shape=jax.ShapeDtypeStruct((span, inner), BF16),
        in_specs=[SMEM, SMEM] + [VMEM] * (len(pieces) + 1 + len(olds)),
        out_specs=VMEM,
        scratch_shapes=[pltpu.VMEM((span, inner), BF16)] * 3,
        compiler_params=pltpu.CompilerParams(vmem_limit_bytes=16 * 2**20),
        cost_estimate=pl.CostEstimate(flops=5 * 10**9, bytes_accessed=4 * 10**6, transcendentals=10**6),
        name="attend_prior" if olds else "attend_own",
    )(starts, lens, *pieces, weights, *olds)


def arrange_kernel(starts, lens, *refs):
    frame_out = refs[-1]
    count = (len(refs) - 1) // 2
    rows, width = refs[0].shape
    span = rows * count
    row = clip_rows(rows, count, span)
    place = lax.broadcasted_iota(jnp.int32, (span, 1), 0)
    total = 0.0
    for prior in (False, True):
        shift, length, _, _ = clip_span(starts, lens, span, prior)
        pick = (place + shift == row) & (row < length)
        frame = jnp.concatenate([piece[...] for piece in refs[prior * count : (prior + 1) * count]], axis=0)
        total = total + dot(jnp.where(pick, 1.0, 0.0).astype(BF16), frame)
    frame_out[...] = total.astype(BF16)


def arrange(own, prior, starts, lens):
    rows, width = own[0].shape
    span = rows * len(own)
    return pl.pallas_call(
        arrange_kernel,
        out_shape=jax.ShapeDtypeStruct((span, width), BF16),
        in_specs=[SMEM, SMEM] + [VMEM] * (2 * len(own)),
        out_specs=VMEM,
        compiler_params=pltpu.CompilerParams(vmem_limit_bytes=12 * 2**20),
        cost_estimate=pl.CostEstimate(flops=2 * 10**9, bytes_accessed=3 * 10**6, transcendentals=0),
        name="arrange",
    )(starts, lens, *own, *prior)


def project_kernel(starts, lens, *refs):
    count = (len(refs) - 4) // 2
    frame, projector, text, *pieces, result = refs
    parts, weights = pieces[:count], pieces[count:]
    span = frame.shape[0]
    _, _, own_first, own_last = clip_span(starts, lens, span, False)
    _, _, prior_first, prior_last = clip_span(starts, lens, span, True)
    context = jnp.concatenate([part[...] for part in parts], axis=1)
    out_weight = jnp.concatenate([weight[...] for weight in weights], axis=0)
    resid = frame[...].astype(F32) + dot(context, out_weight)
    scale = lax.rsqrt(jnp.mean(resid * resid, axis=-1, keepdims=True) + EPS)
    visual = dot((resid * scale).astype(BF16), projector[...]).astype(BF16)
    place = lax.broadcasted_iota(jnp.int32, (span, 1), 0)
    live = ((place >= own_first) & (place < own_last)) | (
        (place >= prior_first) & (place < prior_last)
    )
    result[...] = jnp.where(live, visual, text[...])


def project(frame, parts, outs, projector, text, starts, lens):
    return pl.pallas_call(
        project_kernel,
        out_shape=jax.ShapeDtypeStruct(text.shape, BF16),
        in_specs=[SMEM, SMEM] + [VMEM] * (3 + 2 * len(parts)),
        out_specs=VMEM,
        compiler_params=pltpu.CompilerParams(vmem_limit_bytes=14 * 2**20),
        cost_estimate=pl.CostEstimate(flops=3 * 10**9, bytes_accessed=4 * 10**6, transcendentals=0),
        name="project",
    )(starts, lens, frame, projector, text, *parts, *outs)


def held(weights, part, key, depth):
    start = pl.multiple_of((lax.axis_index("head") ^ key) * depth, depth)
    return weights[part, pl.ds(start, depth), :]


def near_kernel(keys, weights, *refs):
    count = len(keys)
    pieces = refs[:count]
    query_sum, pair_sum, squares = refs[count:]
    norm = 0.0
    for piece in pieces:
        wide = piece[...].astype(F32)
        norm = norm + jnp.sum(wide * wide, axis=-1, keepdims=True)
    squares[...] = jnp.broadcast_to(norm, squares.shape)
    for part in range(3):
        total = 0.0
        for index in range(count):
            total = total + dot(pieces[index][...], held(weights, part, keys[index], pieces[index].shape[1]))
        if part == 0:
            query_sum[...] = total
        else:
            pair_sum[part - 1] = total


def near(pieces, keys, weights):
    span, depth = pieces[0].shape
    columns = weights.shape[2]
    return pl.pallas_call(
        functools.partial(near_kernel, keys),
        out_shape=(
            jax.ShapeDtypeStruct((span, columns), F32),
            jax.ShapeDtypeStruct((2, span, columns), F32),
            jax.ShapeDtypeStruct((span, HD), F32),
        ),
        in_specs=[VMEM] * (1 + len(pieces)),
        out_specs=(VMEM, VMEM, VMEM),
        compiler_params=pltpu.CompilerParams(vmem_limit_bytes=12 * 2**20),
        cost_estimate=pl.CostEstimate(flops=3 * 10**9, bytes_accessed=7 * 10**6, transcendentals=0),
        name="near",
    )(weights, *pieces)


def pair_kernel(keys, total_depth, weights, pair_sum, squares, *refs):
    count = len(keys)
    pieces = refs[:count]
    key_out, value_out, delta, scale_out = refs[count:]
    norm = squares[:, :1]
    for piece in pieces:
        wide = piece[...].astype(F32)
        norm = norm + jnp.sum(wide * wide, axis=-1, keepdims=True)
    scale = lax.rsqrt(norm * (1.0 / total_depth) + EPS)
    scale_out[...] = jnp.broadcast_to(scale, scale_out.shape)
    for part, out in ((0, key_out), (1, value_out)):
        total = pair_sum[part]
        for index in range(count):
            total = total + dot(pieces[index][...], held(weights, part + 1, keys[index], pieces[index].shape[1]))
        out[...] = (total * scale).astype(BF16)
    for head in range(delta.shape[0]):
        lanes = slice(head * HD, (head + 1) * HD)
        delta[head] = lax.dot_general(
            key_out[:, lanes], value_out[:, lanes], (((0,), (0,)), ((), ())), preferred_element_type=F32
        ).astype(BF16)


def pair(pieces, keys, weights, pair_sum, squares):
    span, depth = pieces[0].shape
    columns = weights.shape[2]
    return pl.pallas_call(
        functools.partial(pair_kernel, keys, weights.shape[1]),
        out_shape=(
            jax.ShapeDtypeStruct((span, columns), BF16),
            jax.ShapeDtypeStruct((span, columns), BF16),
            jax.ShapeDtypeStruct((columns // HD, HD, HD), BF16),
            jax.ShapeDtypeStruct((span, HD), F32),
        ),
        in_specs=[VMEM] * (3 + len(pieces)),
        out_specs=(VMEM,) * 4,
        compiler_params=pltpu.CompilerParams(vmem_limit_bytes=12 * 2**20),
        cost_estimate=pl.CostEstimate(flops=3 * 10**9, bytes_accessed=7 * 10**6, transcendentals=0),
        name="pair",
    )(weights, pair_sum, squares, *pieces)


def within_kernel(keys, weights, query_sum, scale, key_in, value_in, *refs):
    count = len(keys)
    pieces = refs[:count]
    query_out, intra = refs[count:]
    span = query_sum.shape[0]
    total = query_sum[...]
    for index in range(count):
        total = total + dot(pieces[index][...], held(weights, 0, keys[index], pieces[index].shape[1]))
    query_out[...] = (total * scale[:, :1]).astype(BF16)
    half = span // 2
    causal = lax.broadcasted_iota(jnp.int32, (half, half), 0) >= lax.broadcasted_iota(
        jnp.int32, (half, half), 1
    )
    for head in range(query_out.shape[1] // HD):
        lanes = slice(head * HD, (head + 1) * HD)
        for top in (0, half):
            query = query_out[top : top + half, lanes]
            corner = dot_t(query, key_in[top : top + half, lanes])
            corner = jnp.where(causal, corner, 0.0).astype(BF16)
            piece = dot(corner, value_in[top : top + half, lanes])
            if top:
                left = dot_t(query, key_in[:top, lanes]).astype(BF16)
                piece = piece + dot(left, value_in[:top, lanes])
            intra[top : top + half, lanes] = piece


def within(pieces, keys, weights, query_sum, scale, key_in, value_in):
    span, depth = pieces[0].shape
    columns = weights.shape[2]
    return pl.pallas_call(
        functools.partial(within_kernel, keys),
        out_shape=(
            jax.ShapeDtypeStruct((span, columns), BF16),
            jax.ShapeDtypeStruct((span, columns), F32),
        ),
        in_specs=[VMEM] * (5 + len(pieces)),
        out_specs=(VMEM,) * 2,
        compiler_params=pltpu.CompilerParams(vmem_limit_bytes=12 * 2**20),
        cost_estimate=pl.CostEstimate(flops=3 * 10**9, bytes_accessed=5 * 10**6, transcendentals=0),
        name="within",
    )(weights, query_sum, scale, key_in, value_in, *pieces)


def finish_kernel(query, intra, carried, state, gain, out):
    for head in range(state.shape[0]):
        lanes = slice(head * HD, (head + 1) * HD)
        whole = (carried[head] + state[head]).astype(BF16)
        lin = intra[:, lanes] + dot(query[:, lanes], whole)
        scale = lax.rsqrt(jnp.mean(lin * lin, axis=-1, keepdims=True) + EPS)
        out[:, lanes] = (lin * scale * gain[:, lanes]).astype(BF16)


def finish(query, intra, carried, state, gain):
    return pl.pallas_call(
        finish_kernel,
        out_shape=jax.ShapeDtypeStruct(query.shape, BF16),
        in_specs=[VMEM] * 5,
        out_specs=VMEM,
        compiler_params=pltpu.CompilerParams(vmem_limit_bytes=8 * 2**20),
        cost_estimate=pl.CostEstimate(flops=10**8, bytes_accessed=3 * 10**6, transcendentals=0),
        name="finish",
    )(query, intra, carried, state, gain.reshape(1, -1))


def local(
    patches,
    clip_start,
    clip_len,
    text_rows,
    vision_qkv,
    vision_out,
    projector,
    layer_qkv,
    head_gain,
    state_in,
):
    groups = lax.axis_size("head")
    heads = VIT_HEADS // groups
    own = spread(patches, "head")
    prior = spread_prior(patches)
    outs = spread(vision_out, "head")
    vision = jnp.transpose(vision_qkv, (1, 2, 0)).reshape(-1, vision_qkv.shape[0])
    layer = jnp.transpose(layer_qkv, (1, 0, 2))
    context = attend(own, vision, clip_start, clip_len, heads)
    context = attend(prior, vision, clip_start, clip_len, heads, context)
    parts = spread(context, "head")
    frame = arrange(own, prior, clip_start, clip_len)
    sequence = project(frame, parts, outs, projector, text_rows, clip_start, clip_len)
    blocks = spread(sequence, "head")
    half = groups // 2
    near_keys, far_keys = tuple(range(half)), tuple(range(half, groups))
    query_sum, pair_sum, squares = near(blocks[:half], near_keys, layer)
    key_rows, value_rows, delta, scale = pair(blocks[half:], far_keys, layer, pair_sum, squares)
    carried = earlier_sum(delta, "ctx")
    query, intra = within(blocks[half:], far_keys, layer, query_sum, scale, key_rows, value_rows)
    return finish(query, intra, carried, state_in, head_gain)


def solution(mesh):
    placed = (
        P(("ctx", "head"), None),
        P(),
        P(),
        P("ctx", "head"),
        P(None, None, "head"),
        P("head", None),
        P(None, "head"),
        P(None, None, "head"),
        P("head"),
        P("head", None, None),
    )
    return jax.shard_map(
        local, mesh=mesh, in_specs=placed, out_specs=P("ctx", "head"), check_vma=False
    )
```

time: 207 us -> 101 us (0.49)
  waiting for transfers between devices: 116 us -> 43.3 us
  matrix products: 33.9 us -> 0 us
  starting transfers between devices: 4.46 us -> 28.8 us
  Pallas kernels: 0 us -> 17.4 us
  local copies, waits for them, and re-layouts: 24.6 us -> 7.33 us
  between operations: 16.5 us -> 0.29 us
  other arithmetic: 10.6 us -> 2.68 us
    all_gather x3 -> x0, waiting for transfers between devices: 72.1 us -> none  [the longest x1 37.7 us: local(): lax.all_gather(delta.astype(jnp.bfloat16), 'ctx', axis=0, tiled=True)]
    ppermute x1 -> x19, waiting for transfers between devices: 7.29 us -> 43.3 us  [the longest x15 33.1 us: swapped(): lax.ppermute(value, axis, [(source, source ^ bit) for source in range(cou...]
    psum x1 -> x0, waiting for transfers between devices: 35.8 us -> none  [local(): lax.psum(partial_value.astype(jnp.bfloat16), 'head').astype(jnp.float32)]
    dot_general x10 -> x0, matrix products: 30.4 us -> none  [the longest x1 8.13 us: local(): jnp.dot(unit, layer_qkv.reshape(layer_qkv.shape[0], -1), preferred_elemen...]
    ppermute x1 -> x19, starting transfers between devices: 4.16 us -> 28.8 us  [the longest x3 16.6 us: shifted(): lax.ppermute(value, axis, [(source, source + steps) for source in range(c...]
    pallas_call x0 -> x8, Pallas kernels: none -> 17.4 us  [the longest x2 5.1 us: attend(): pl.pallas_call(functools.partial(attend_kernel, old is not None, heads, m...]
    reduce_sum x3 -> x0, other arithmetic: 5.53 us -> none  [unit_rows(): jnp.mean(values * values, axis=-1, keepdims=True) + EPS]
    reshape x2 -> x0, local copies, waits for them, and re-layouts: 4.96 us -> none  [the longest x1 3.95 us: local(): layer_mix = layer_mix.astype(jnp.bfloat16).reshape(span, 3, heads, HD)]
  transfers between devices with their start and end apart: 5 -> 19, of which waited for: 5 -> 8; matrix products, arithmetic and copies ran while one was open for 8% -> 0% of each run, Pallas kernels for 0% -> 11%
where the time goes in v2:
time: 101 us; the launch traced here: 99.8 us
  waiting for transfers between devices  43.3 us (43%)
  starting transfers between devices  28.8 us (29%)
  Pallas kernels  17.4 us (17%)
  local copies, waits for them, and re-layouts  7.33 us (7%)
  other arithmetic  2.68 us (3%)
    ppermute x15, waiting for transfers between devices, swapped(): lax.ppermute(value, axis, [(source, source ^ bit) for source in range(cou...  33.1 us
    ppermute x3, starting transfers between devices, shifted(): lax.ppermute(value, axis, [(source, source + steps) for source in range(c...  16.6 us
    ppermute x3, waiting for transfers between devices, shifted(): lax.ppermute(value, axis, [(source, source + steps) for source in range(c...  10.2 us
    ppermute x15, starting transfers between devices, swapped(): lax.ppermute(value, axis, [(source, source ^ bit) for source in range(cou...  8.77 us
    unnamed x34, local copies, waits for them, and re-layouts  7.33 us
    pallas_call x2, Pallas kernels, attend(): pl.pallas_call(functools.partial(attend_kernel, old is not None, heads, m...  5.1 us
    ppermute x1, starting transfers between devices, spread_prior(): blocks[stride] = lax.ppermute(value, ('ctx', 'head'), pairs)  3.4 us
    pallas_call x1, Pallas kernels, project(): pl.pallas_call(project_kernel, out_shape=jax.ShapeDtypeStruct(text.shape,...  3.29 us
  transfers between devices with their start and end apart: 19, of which 8 were waited for; matrix products, arithmetic and copies ran while one was open for 0% of the time, Pallas kernels for 11%

profile of v2, /device:TPU:0, one launch (start us, length us, event | category | flops | bytes accessed | tf_op | source)
XLA Modules:
  0.0 99.8 jit_solution(12248054172825988279)
XLA Ops:
  0.0 3.0 %collective-permute-start.1 = (bf16[128,1152]{1,0:T(8,128)(2,1)}, bf16[128,1152]{1,0:T(8,128)(2,1)S(1)}, u32[]{:S(2)}, u32[]{:S(2)}) collective-permute-start(bf16[128,1152]{1,0:T(8,128)(2,1)} %refs_0_.3), channel_id=1, source_target_pairs={{0,2},{1,3},{2,0},{3,1},{4,6},{5,7},{6,4},{7,5},{8,10},{9,11},{10,... | collective-permute-start | bytes 884744 | tf_op jit(solution)/shard_map/ppermute | solution.py:40
  3.0 3.4 %collective-permute-start.3 = (bf16[128,1152]{1,0:T(8,128)(2,1)}, bf16[128,1152]{1,0:T(8,128)(2,1)S(1)}, u32[]{:S(2)}, u32[]{:S(2)}) collective-permute-start(bf16[128,1152]{1,0:T(8,128)(2,1)} %refs_0_.3), channel_id=1, source_target_pairs={{0,4},{4,8},{8,12},{12,16},{16,20},{20,24},{24,28},{1,5},{5,9},{9,... | collective-permute-start | bytes 884744 | tf_op jit(solution)/shard_map/ppermute | solution.py:35
  6.4 3.4 %collective-permute-start.5 = (bf16[128,1152]{1,0:T(8,128)(2,1)}, bf16[128,1152]{1,0:T(8,128)(2,1)S(1)}, u32[]{:S(2)}, u32[]{:S(2)}) collective-permute-start(bf16[128,1152]{1,0:T(8,128)(2,1)} %refs_0_.3), channel_id=1, source_target_pairs={{0,6},{1,7},{2,4},{3,5},{4,10},{5,11},{6,8},{7,9},{8,14},{9,15},{1... | collective-permute-start | bytes 884744 | tf_op jit(solution)/shard_map/ppermute | solution.py:64
  10.2 1.7 %collective-permute-start.11 = (bf16[288,1152]{1,0:T(8,128)(2,1)}, bf16[288,1152]{1,0:T(8,128)(2,1)S(1)}, u32[]{:S(2)}, u32[]{:S(2)}) collective-permute-start(bf16[288,1152]{1,0:T(8,128)(2,1)} %refs_7_.1), channel_id=1, source_target_pairs={{0,2},{1,3},{2,0},{3,1},{4,6},{5,7},{6,4},{7,5},{8,10},{9,11},{10,... | collective-permute-start | bytes 1990664 | tf_op jit(solution)/shard_map/ppermute | solution.py:40
  12.2 7.8 %collective-permute-done.3.refs_4_.refs_0_ = bf16[128,1152]{1,0:T(8,128)(2,1)S(1)} collective-permute-done((bf16[128,1152]{1,0:T(8,128)(2,1)}, bf16[128,1152]{1,0:T(8,128)(2,1)S(1)}, u32[]{:S(2)}, u32[]{:S(2)}) %collective-permute-start.3) | collective-permute-done | bytes 294944 | tf_op jit(solution)/shard_map/ppermute | solution.py:35
  20.5 1.6 %copy-done.3 = bf16[1152,3,288]{0,2,1:T(8,128)(2,1)S(1)} copy-done((bf16[1152,3,288]{0,2,1:T(8,128)(2,1)S(1)}, bf16[1152,3,288]{0,2,1:T(8,128)(2,1)}, u32[]{:S(2)}) %copy-start.3) | copy-done | bytes 1990680
  22.0 1.0 copy-done.7
  23.0 0.7 copy-done.9
  23.6 0.7 copy-done.11
  24.3 4.5 %attend_own.1.refs_5_ = bf16[512,288]{1,0:T(8,128)(2,1)S(1)} custom-call(s32[8]{0:T(128)S(1)} %copy-done.9, s32[8]{0:T(128)S(1)} %copy-done.11, bf16[128,1152]{1,0:T(8,128)(2,1)S(1)} %copy-done.7, bf16[128,1152]{1,0:T(8,128)(2,1)S(1)} %collective-permute-done.refs_1_, bf16[128,1152]{1,0:T(8,128)(2,1)S(1)} %collective-permute-done.1.refs_2_, ...), custom_call_target="tpu_custom_call" | custom-call | flops 5000000000 | bytes 4000000 | tf_op jit(solution)/shard_map/attend_own/pallas_call | solution.py:178
  28.8 4.0 %collective-permute-done.11.refs_9_ = bf16[288,1152]{1,0:T(8,128)(2,1)S(1)} collective-permute-done((bf16[288,1152]{1,0:T(8,128)(2,1)}, bf16[288,1152]{1,0:T(8,128)(2,1)S(1)}, u32[]{:S(2)}, u32[]{:S(2)}) %collective-permute-start.11) | collective-permute-done | bytes 663584 | tf_op jit(solution)/shard_map/ppermute | solution.py:40
  32.9 0.6 attend_prior.1.refs_3_
  33.5 0.6 collective-permute-start.8
  34.3 10.8 %collective-permute-done.8.refs_5_ = bf16[512,288]{1,0:T(8,128)(2,1)S(1)} collective-permute-done((bf16[512,288]{1,0:T(8,128)(2,1)S(1)}, bf16[512,288]{1,0:T(8,128)(2,1)S(1)}, u32[]{:S(2)}, u32[]{:S(2)}) %collective-permute-start.8) | collective-permute-done | bytes 294944 | tf_op jit(solution)/shard_map/ppermute | solution.py:40
  45.1 2.1 %arrange.1.refs_0_ = bf16[512,1152]{1,0:T(8,128)(2,1)S(1)} custom-call(s32[8]{0:T(128)S(1)} %copy-done.10, s32[8]{0:T(128)S(1)} %copy-done.12, bf16[128,1152]{1,0:T(8,128)(2,1)S(1)} %copy-done.8, bf16[128,1152]{1,0:T(8,128)(2,1)S(1)} %collective-permute-done.refs_1_, bf16[128,1152]{1,0:T(8,128)(2,1)S(1)} %collective-permute-done.1.refs_2_, ...), custom_call_target="tpu_custom_call" | custom-call | flops 2000000000 | bytes 3000000 | tf_op jit(solution)/shard_map/arrange/pallas_call | solution.py:209
  47.3 3.3 %project.1.refs_0_ = bf16[512,512]{1,0:T(8,128)(2,1)S(1)} custom-call(s32[8]{0:T(128)S(1)} %copy-done.10, s32[8]{0:T(128)S(1)} %copy-done.12, bf16[512,1152]{1,0:T(8,128)(2,1)S(1)} %arrange.1.refs_0_, bf16[1152,512]{1,0:T(8,128)(2,1)S(1)} %copy-done.4, bf16[512,512]{1,0:T(8,128)(2,1)S(1)} %copy-done.6, bf16[512,288]{1,0:T(8,128)(2,1)S(1)} %attend_prior.1.refs_3_, ...), custom_call_target="tpu_custom_call" | custom-call | flops 3000000000 | bytes 4000000 | tf_op jit(solution)/shard_map/project/pallas_call | solution.py:240
  50.6 0.6 collective-permute-start.14
  51.4 13.6 %collective-permute-done.14.refs_0_ = bf16[512,512]{1,0:T(8,128)(2,1)S(1)} collective-permute-done((bf16[512,512]{1,0:T(8,128)(2,1)S(1)}, bf16[512,512]{1,0:T(8,128)(2,1)S(1)}, u32[]{:S(2)}, u32[]{:S(2)}) %collective-permute-start.14) | collective-permute-done | bytes 524320 | tf_op jit(solution)/shard_map/ppermute | solution.py:40
  65.0 1.8 %near.1 = (f32[512,512]{1,0:T(8,128)S(1)}, f32[2,512,512]{2,1,0:T(8,128)S(1)}, f32[512,128]{1,0:T(8,128)S(1)}) custom-call(bf16[3,2048,512]{2,1,0:T(8,128)(2,1)S(1)} %bitcast.8, bf16[512,512]{1,0:T(8,128)(2,1)S(1)} %project.1.refs_0_, bf16[512,512]{1,0:T(8,128)(2,1)S(1)} %collective-permute-done.13.refs_1_), custom_call_target="tpu_custom_call" | custom-call | flops 3000000000 | bytes 7000000 | tf_op jit(solution)/shard_map/near/pallas_call | solution.py:278
  66.9 1.6 %pair.1 = (bf16[512,512]{1,0:T(8,128)(2,1)S(1)}, bf16[512,512]{1,0:T(8,128)(2,1)S(1)}, bf16[4,128,128]{2,1,0:T(8,128)(2,1)S(1)}, f32[512,128]{1,0:T(8,128)S(1)}) custom-call(bf16[3,2048,512]{2,1,0:T(8,128)(2,1)S(1)} %bitcast.9, f32[2,512,512]{2,1,0:T(8,128)S(1)} %get-tuple-element.15.pair_sum, f32[512,128]{1,0:T(8,128)S(1)} %get-tuple-element.16.squares, ...), custom_call_target="tpu_custom_call" | custom-call | flops 3000000000 | bytes 7000000 | tf_op jit(solution)/shard_map/pair/pallas_call | solution.py:318
  68.6 1.7 %collective-permute-start.16 = (bf16[4,128,128]{2,1,0:T(8,128)(2,1)S(1)}, bf16[4,128,128]{2,1,0:T(8,128)(2,1)S(1)}, u32[]{:S(2)}, u32[]{:S(2)}) collective-permute-start(bf16[4,128,128]{2,1,0:T(8,128)(2,1)S(1)} %get-tuple-element.22), channel_id=1, source_target_pairs={{0,4},{4,0},{8,12},{12,8},{16,20},{20,16},{24,28},{28,24},{1,5},{5... | collective-permute-start | bytes 393224 | tf_op jit(solution)/shard_map/ppermute | solution.py:40
  70.2 4.2 %collective-permute-done.16 = bf16[4,128,128]{2,1,0:T(8,128)(2,1)S(1)} collective-permute-done((bf16[4,128,128]{2,1,0:T(8,128)(2,1)S(1)}, bf16[4,128,128]{2,1,0:T(8,128)(2,1)S(1)}, u32[]{:S(2)}, u32[]{:S(2)}) %collective-permute-start.16) | collective-permute-done | bytes 131104 | tf_op jit(solution)/shard_map/ppermute | solution.py:40
  74.5 0.7 copy-done.13
  75.1 0.7 fusion.2
  75.8 5.3 %collective-permute-start.17 = (bf16[4,128,128]{2,1,0:T(8,128)(2,1)}, bf16[4,128,128]{2,1,0:T(8,128)(2,1)}, u32[]{:S(2)}, u32[]{:S(2)}) collective-permute-start(bf16[4,128,128]{2,1,0:T(8,128)(2,1)} %fusion.2), channel_id=1, source_target_pairs={{0,8},{4,12},{8,16},{12,20},{16,24},{20,28},{1,9},{5,13},{9,17},{1... | collective-permute-start | bytes 393224 | tf_op jit(solution)/shard_map/ppermute | solution.py:35
  81.2 2.4 %collective-permute-done.17 = bf16[4,128,128]{2,1,0:T(8,128)(2,1)} collective-permute-done((bf16[4,128,128]{2,1,0:T(8,128)(2,1)}, bf16[4,128,128]{2,1,0:T(8,128)(2,1)}, u32[]{:S(2)}, u32[]{:S(2)}) %collective-permute-start.17) | collective-permute-done | bytes 131104 | tf_op jit(solution)/shard_map/ppermute | solution.py:35
  83.6 1.0 %fusion.1 = bf16[4,128,128]{2,1,0:T(8,128)(2,1)S(1)} fusion(bf16[4,128,128]{2,1,0:T(8,128)(2,1)} %collective-permute-done.17, bf16[4,128,128]{2,1,0:T(8,128)(2,1)} %copy-done.13, bf16[4,128,128]{2,1,0:T(8,128)(2,1)S(1)} %get-tuple-element.22), kind=kLoop, calls=%fused_computation.5 | loop fusion | flops 393216 | bytes 524288 | tf_op jit(solution)/shard_map/convert_element_type | solution.py:82
  84.6 7.8 %collective-permute-start.18 = (bf16[4,128,128]{2,1,0:T(8,128)(2,1)S(1)}, bf16[4,128,128]{2,1,0:T(8,128)(2,1)S(1)}, u32[]{:S(2)}, u32[]{:S(2)}) collective-permute-start(bf16[4,128,128]{2,1,0:T(8,128)(2,1)S(1)} %fusion.1), channel_id=1, source_target_pairs={{0,16},{4,20},{8,24},{12,28},{1,17},{5,21},{9,25},{13,29},{2,18},{... | collective-permute-start | bytes 393224 | tf_op jit(solution)/shard_map/ppermute | solution.py:35
  92.5 2.8 %copy-done.2 = bf16[2048,3,512]{2,0,1:T(8,128)(2,1)S(1)} copy-done((bf16[2048,3,512]{2,0,1:T(8,128)(2,1)S(1)}, bf16[2048,3,512]{2,0,1:T(8,128)(2,1)}, u32[]{:S(2)}) %copy-start.2) | copy-done | bytes 6291480
  95.2 2.2 %within.1 = (bf16[512,512]{1,0:T(8,128)(2,1)S(1)}, f32[512,512]{1,0:T(8,128)S(1)}) custom-call(bf16[3,2048,512]{2,1,0:T(8,128)(2,1)S(1)} %bitcast.10, f32[512,512]{1,0:T(8,128)S(1)} %get-tuple-element.14.query_sum, f32[512,128]{1,0:T(8,128)S(1)} %get-tuple-element.17.scale, bf16[512,512]{1,0:T(8,128)(2,1)S(1)} %get-tuple-element.18.key_in, ...), custom_call_target="tpu_custom_call" | custom-call | flops 3000000000 | bytes 5000000 | tf_op jit(solution)/shard_map/within/pallas_call | solution.py:363
  97.5 1.0 fusion.carried
  98.5 1.3 %finish.1 = bf16[512,512]{1,0:T(8,128)(2,1)} custom-call(bf16[512,512]{1,0:T(8,128)(2,1)S(1)} %get-tuple-element.20.query, f32[512,512]{1,0:T(8,128)S(1)} %get-tuple-element.21.intra, f32[4,128,128]{2,1,0:T(8,128)S(1)} %fusion.carried, f32[4,128,128]{2,1,0:T(8,128)S(1)} %copy-done, f32[1,512]{1,0:T(1,128)S(1)} %bitcast.5), custom_call_target="tpu_custom_call" | custom-call | flops 100000000 | bytes 3000000 | tf_op jit(solution)/shard_map/finish/pallas_call | solution.py:387
  (52 shorter events, 1.7 us)
Async XLA Ops:
  0.0 10.2 %collective-permute-start.1 = (bf16[128,1152]{1,0:T(8,128)(2,1)}, bf16[128,1152]{1,0:T(8,128)(2,1)S(1)}, u32[]{:S(2)}, u32[]{:S(2)}) collective-permute-start(bf16[128,1152]{1,0:T(8,128)(2,1)} %refs_0_.3), channel_id=1, source_target_pairs={{0,2},{1,3},{2,0},{3,1},{4,6},{5,7},{6,4},{7,5},{8,10},{9,11},{10,... | collective-permute-start | bytes 884744 | tf_op jit(solution)/shard_map/ppermute | solution.py:40
  3.0 9.0 %collective-permute-start = (bf16[128,1152]{1,0:T(8,128)(2,1)}, bf16[128,1152]{1,0:T(8,128)(2,1)S(1)}, u32[]{:S(2)}, u32[]{:S(2)}) collective-permute-start(bf16[128,1152]{1,0:T(8,128)(2,1)} %refs_0_.3), channel_id=1, source_target_pairs={{0,1},{1,0},{2,3},{3,2},{4,5},{5,4},{6,7},{7,6},{8,9},{9,8},{10,11... | collective-permute-start | bytes 884744 | tf_op jit(solution)/shard_map/ppermute | solution.py:40
  3.0 17.0 %collective-permute-start.3 = (bf16[128,1152]{1,0:T(8,128)(2,1)}, bf16[128,1152]{1,0:T(8,128)(2,1)S(1)}, u32[]{:S(2)}, u32[]{:S(2)}) collective-permute-start(bf16[128,1152]{1,0:T(8,128)(2,1)} %refs_0_.3), channel_id=1, source_target_pairs={{0,4},{4,8},{8,12},{12,16},{16,20},{20,24},{24,28},{1,5},{5,9},{9,... | collective-permute-start | bytes 884744 | tf_op jit(solution)/shard_map/ppermute | solution.py:35
  6.4 13.5 %collective-permute-start.5 = (bf16[128,1152]{1,0:T(8,128)(2,1)}, bf16[128,1152]{1,0:T(8,128)(2,1)S(1)}, u32[]{:S(2)}, u32[]{:S(2)}) collective-permute-start(bf16[128,1152]{1,0:T(8,128)(2,1)} %refs_0_.3), channel_id=1, source_target_pairs={{0,6},{1,7},{2,4},{3,5},{4,10},{5,11},{6,8},{7,9},{8,14},{9,15},{1... | collective-permute-start | bytes 884744 | tf_op jit(solution)/shard_map/ppermute | solution.py:64
  10.2 10.3 %collective-permute-start.2 = (bf16[128,1152]{1,0:T(8,128)(2,1)S(1)}, bf16[128,1152]{1,0:T(8,128)(2,1)S(1)}, u32[]{:S(2)}, u32[]{:S(2)}) collective-permute-start(bf16[128,1152]{1,0:T(8,128)(2,1)S(1)} %collective-permute-done.1.refs_2_), channel_id=1, source_target_pairs={{0,1},{1,0},{2,3},{3,2},{4,5},{5,4},{6,7},{7,6},{8,9},{9,8},{10,11... | collective-permute-start | bytes 884744 | tf_op jit(solution)/shard_map/ppermute | solution.py:40
  10.2 22.7 %collective-permute-start.11 = (bf16[288,1152]{1,0:T(8,128)(2,1)}, bf16[288,1152]{1,0:T(8,128)(2,1)S(1)}, u32[]{:S(2)}, u32[]{:S(2)}) collective-permute-start(bf16[288,1152]{1,0:T(8,128)(2,1)} %refs_7_.1), channel_id=1, source_target_pairs={{0,2},{1,3},{2,0},{3,1},{4,6},{5,7},{6,4},{7,5},{8,10},{9,11},{10,... | collective-permute-start | bytes 1990664 | tf_op jit(solution)/shard_map/ppermute | solution.py:40
  11.9 35.3 %collective-permute-start.10 = (bf16[288,1152]{1,0:T(8,128)(2,1)}, bf16[288,1152]{1,0:T(8,128)(2,1)S(1)}, u32[]{:S(2)}, u32[]{:S(2)}) collective-permute-start(bf16[288,1152]{1,0:T(8,128)(2,1)} %refs_7_.1), channel_id=1, source_target_pairs={{0,1},{1,0},{2,3},{3,2},{4,5},{5,4},{6,7},{7,6},{8,9},{9,8},{10,11... | collective-permute-start | bytes 1990664 | tf_op jit(solution)/shard_map/ppermute | solution.py:40
  19.9 12.9 %collective-permute-start.4 = (bf16[128,1152]{1,0:T(8,128)(2,1)S(1)}, bf16[128,1152]{1,0:T(8,128)(2,1)S(1)}, u32[]{:S(2)}, u32[]{:S(2)}) collective-permute-start(bf16[128,1152]{1,0:T(8,128)(2,1)S(1)} %collective-permute-done.3.refs_4_.refs_0_), channel_id=1, source_target_pairs={{0,1},{1,0},{2,3},{3,2},{4,5},{5,4},{6,7},{7,6},{8,9},{9,8},{10,11... | collective-permute-start | bytes 884744 | tf_op jit(solution)/shard_map/ppermute | solution.py:40
  20.0 12.9 %collective-permute-start.6 = (bf16[128,1152]{1,0:T(8,128)(2,1)S(1)}, bf16[128,1152]{1,0:T(8,128)(2,1)S(1)}, u32[]{:S(2)}, u32[]{:S(2)}) collective-permute-start(bf16[128,1152]{1,0:T(8,128)(2,1)S(1)} %collective-permute-done.5.refs_6_.refs_2_), channel_id=1, source_target_pairs={{0,1},{1,0},{2,3},{3,2},{4,5},{5,4},{6,7},{7,6},{8,9},{9,8},{10,11... | collective-permute-start | bytes 884744 | tf_op jit(solution)/shard_map/ppermute | solution.py:40
  20.5 1.6 %copy-start.3 = (bf16[1152,3,288]{0,2,1:T(8,128)(2,1)S(1)}, bf16[1152,3,288]{0,2,1:T(8,128)(2,1)}, u32[]{:S(2)}) copy-start(bf16[1152,3,288]{0,2,1:T(8,128)(2,1)} %param.14) | copy-start | bytes 5971972
  28.8 16.3 %copy-start.8 = (bf16[128,1152]{1,0:T(8,128)(2,1)S(1)}, bf16[128,1152]{1,0:T(8,128)(2,1)}, u32[]{:S(2)}) copy-start(bf16[128,1152]{1,0:T(8,128)(2,1)} %refs_0_.3) | copy-start | bytes 884740
  28.8 16.3 %copy-start.10 = (s32[8]{0:T(128)S(1)}, s32[8]{0:T(128)}, u32[]{:S(2)}) copy-start(s32[8]{0:T(128)} %starts.7) | copy-start | bytes 100
  28.8 16.3 %copy-start.12 = (s32[8]{0:T(128)S(1)}, s32[8]{0:T(128)}, u32[]{:S(2)}) copy-start(s32[8]{0:T(128)} %lens.7) | copy-start | bytes 100
  32.9 14.4 %collective-permute-start.12 = (bf16[288,1152]{1,0:T(8,128)(2,1)S(1)}, bf16[288,1152]{1,0:T(8,128)(2,1)S(1)}, u32[]{:S(2)}, u32[]{:S(2)}) collective-permute-start(bf16[288,1152]{1,0:T(8,128)(2,1)S(1)} %collective-permute-done.11.refs_9_), channel_id=1, source_target_pairs={{0,1},{1,0},{2,3},{3,2},{4,5},{5,4},{6,7},{7,6},{8,9},{9,8},{10,11... | collective-permute-start | bytes 1990664 | tf_op jit(solution)/shard_map/ppermute | solution.py:40
  33.5 13.8 %copy-start.4 = (bf16[1152,512]{1,0:T(8,128)(2,1)S(1)}, bf16[1152,512]{1,0:T(8,128)(2,1)}, u32[]{:S(2)}) copy-start(bf16[1152,512]{1,0:T(8,128)(2,1)} %refs_1_.1) | copy-start | bytes 3538948
  33.5 13.8 %copy-start.5 = (bf16[288,1152]{1,0:T(8,128)(2,1)S(1)}, bf16[288,1152]{1,0:T(8,128)(2,1)}, u32[]{:S(2)}) copy-start(bf16[288,1152]{1,0:T(8,128)(2,1)} %refs_7_.1) | copy-start | bytes 1990660
  33.5 13.8 %copy-start.6 = (bf16[512,512]{1,0:T(8,128)(2,1)S(1)}, bf16[512,512]{1,0:T(8,128)(2,1)}, u32[]{:S(2)}) copy-start(bf16[512,512]{1,0:T(8,128)(2,1)} %refs_2_.1) | copy-start | bytes 1572868
  33.5 11.6 %collective-permute-start.8 = (bf16[512,288]{1,0:T(8,128)(2,1)S(1)}, bf16[512,288]{1,0:T(8,128)(2,1)S(1)}, u32[]{:S(2)}, u32[]{:S(2)}) collective-permute-start(bf16[512,288]{1,0:T(8,128)(2,1)S(1)} %attend_prior.1.refs_3_), channel_id=1, source_target_pairs={{0,2},{1,3},{2,0},{3,1},{4,6},{5,7},{6,4},{7,5},{8,10},{9,11},{10,... | collective-permute-start | bytes 884744 | tf_op jit(solution)/shard_map/ppermute | solution.py:40
  34.1 13.1 %collective-permute-start.7 = (bf16[512,288]{1,0:T(8,128)(2,1)S(1)}, bf16[512,288]{1,0:T(8,128)(2,1)S(1)}, u32[]{:S(2)}, u32[]{:S(2)}) collective-permute-start(bf16[512,288]{1,0:T(8,128)(2,1)S(1)} %attend_prior.1.refs_3_), channel_id=1, source_target_pairs={{0,1},{1,0},{2,3},{3,2},{4,5},{5,4},{6,7},{7,6},{8,9},{9,8},{10,11... | collective-permute-start | bytes 884744 | tf_op jit(solution)/shard_map/ppermute | solution.py:40
  45.1 2.2 %collective-permute-start.9 = (bf16[512,288]{1,0:T(8,128)(2,1)S(1)}, bf16[512,288]{1,0:T(8,128)(2,1)S(1)}, u32[]{:S(2)}, u32[]{:S(2)}) collective-permute-start(bf16[512,288]{1,0:T(8,128)(2,1)S(1)} %collective-permute-done.8.refs_5_), channel_id=1, source_target_pairs={{0,1},{1,0},{2,3},{3,2},{4,5},{5,4},{6,7},{7,6},{8,9},{9,8},{10,11... | collective-permute-start | bytes 884744 | tf_op jit(solution)/shard_map/ppermute | solution.py:40
  45.1 19.9 %slice-start = ((s8[6291456]{0:T(1024)(128)(4,1)}), s8[4194304]{0:T(1024)(128)(4,1)S(1)}, s32[]{:S(2)}) async-start(s8[6291456]{0:T(1024)(128)(4,1)} %bitcast.6), calls=%async_computation | async-start | bytes 8388608
  47.2 17.8 %slice-start.1 = ((s8[6291456]{0:T(1024)(128)(4,1)}), s8[2097152]{0:T(1024)(128)(4,1)S(1)}, s32[]{:S(2)}) async-start(s8[6291456]{0:T(1024)(128)(4,1)} %bitcast.6), calls=%async_computation.1 | async-start | bytes 4194304
  50.6 14.4 %collective-permute-start.14 = (bf16[512,512]{1,0:T(8,128)(2,1)S(1)}, bf16[512,512]{1,0:T(8,128)(2,1)S(1)}, u32[]{:S(2)}, u32[]{:S(2)}) collective-permute-start(bf16[512,512]{1,0:T(8,128)(2,1)S(1)} %project.1.refs_0_), channel_id=1, source_target_pairs={{0,2},{1,3},{2,0},{3,1},{4,6},{5,7},{6,4},{7,5},{8,10},{9,11},{10,... | collective-permute-start | bytes 1572872 | tf_op jit(solution)/shard_map/ppermute | solution.py:40
  51.2 13.8 %collective-permute-start.13 = (bf16[512,512]{1,0:T(8,128)(2,1)S(1)}, bf16[512,512]{1,0:T(8,128)(2,1)S(1)}, u32[]{:S(2)}, u32[]{:S(2)}) collective-permute-start(bf16[512,512]{1,0:T(8,128)(2,1)S(1)} %project.1.refs_0_), channel_id=1, source_target_pairs={{0,1},{1,0},{2,3},{3,2},{4,5},{5,4},{6,7},{7,6},{8,9},{9,8},{10,11... | collective-permute-start | bytes 1572872 | tf_op jit(solution)/shard_map/ppermute | solution.py:40
  65.0 1.9 %collective-permute-start.15 = (bf16[512,512]{1,0:T(8,128)(2,1)S(1)}, bf16[512,512]{1,0:T(8,128)(2,1)S(1)}, u32[]{:S(2)}, u32[]{:S(2)}) collective-permute-start(bf16[512,512]{1,0:T(8,128)(2,1)S(1)} %collective-permute-done.14.refs_0_), channel_id=1, source_target_pairs={{0,1},{1,0},{2,3},{3,2},{4,5},{5,4},{6,7},{7,6},{8,9},{9,8},{10,11... | collective-permute-start | bytes 1572872 | tf_op jit(solution)/shard_map/ppermute | solution.py:40
  68.6 5.9 %collective-permute-start.16 = (bf16[4,128,128]{2,1,0:T(8,128)(2,1)S(1)}, bf16[4,128,128]{2,1,0:T(8,128)(2,1)S(1)}, u32[]{:S(2)}, u32[]{:S(2)}) collective-permute-start(bf16[4,128,128]{2,1,0:T(8,128)(2,1)S(1)} %get-tuple-element.22), channel_id=1, source_target_pairs={{0,4},{4,0},{8,12},{12,8},{16,20},{20,16},{24,28},{28,24},{1,5},{5... | collective-permute-start | bytes 393224 | tf_op jit(solution)/shard_map/ppermute | solution.py:40
  75.8 7.8 %collective-permute-start.17 = (bf16[4,128,128]{2,1,0:T(8,128)(2,1)}, bf16[4,128,128]{2,1,0:T(8,128)(2,1)}, u32[]{:S(2)}, u32[]{:S(2)}) collective-permute-start(bf16[4,128,128]{2,1,0:T(8,128)(2,1)} %fusion.2), channel_id=1, source_target_pairs={{0,8},{4,12},{8,16},{12,20},{16,24},{20,28},{1,9},{5,13},{9,17},{1... | collective-permute-start | bytes 393224 | tf_op jit(solution)/shard_map/ppermute | solution.py:35
  84.6 12.8 %collective-permute-start.18 = (bf16[4,128,128]{2,1,0:T(8,128)(2,1)S(1)}, bf16[4,128,128]{2,1,0:T(8,128)(2,1)S(1)}, u32[]{:S(2)}, u32[]{:S(2)}) collective-permute-start(bf16[4,128,128]{2,1,0:T(8,128)(2,1)S(1)} %fusion.1), channel_id=1, source_target_pairs={{0,16},{4,20},{8,24},{12,28},{1,17},{5,21},{9,25},{13,29},{2,18},{... | collective-permute-start | bytes 393224 | tf_op jit(solution)/shard_map/ppermute | solution.py:35
  92.4 2.8 %copy-start.2 = (bf16[2048,3,512]{2,0,1:T(8,128)(2,1)S(1)}, bf16[2048,3,512]{2,0,1:T(8,128)(2,1)}, u32[]{:S(2)}) copy-start(bf16[2048,3,512]{2,0,1:T(8,128)(2,1)} %param.17) | copy-start | bytes 18874372
  95.2 2.2 %copy-start.14 = (bf16[4,128,128]{2,1,0:T(8,128)(2,1)S(1)}, bf16[4,128,128]{2,1,0:T(8,128)(2,1)}, u32[]{:S(2)}) copy-start(bf16[4,128,128]{2,1,0:T(8,128)(2,1)} %copy-done.13) | copy-start | bytes 393220
  95.2 3.2 %copy-start = (f32[4,128,128]{2,1,0:T(8,128)S(1)}, f32[4,128,128]{2,1,0:T(8,128)}, u32[]{:S(2)}) copy-start(f32[4,128,128]{2,1,0:T(8,128)} %state.1) | copy-start | bytes 786436
  95.2 3.2 %copy-start.1 = (f32[512]{0:T(512)S(1)}, f32[512]{0:T(512)}, u32[]{:S(2)}) copy-start(f32[512]{0:T(512)} %param.18) | copy-start | bytes 6148
  (4 other events, 2.9 us)

commit v3 on v2

v3 whole, which is shorter than its diff:
```python
import functools
import math

import jax
import jax.numpy as jnp
from jax import lax
from jax.experimental import pallas as pl
from jax.experimental.pallas import tpu as pltpu
from jax.sharding import PartitionSpec as P

VIT_HEADS = 16
HD = 128

EPS = 1e-06
LOW = -1e30
BLOCK = 128
SPLIT = 2
VMEM = pl.BlockSpec(memory_space=pltpu.VMEM)
HBM = pl.BlockSpec(memory_space=pltpu.HBM)
F32 = jnp.float32
BF16 = jnp.bfloat16


def dot(left, right):
    return jnp.dot(left, right, preferred_element_type=F32)


def dot_t(left, right):
    return lax.dot_general(left, right, (((1,), (1,)), ((), ())), preferred_element_type=F32)


def shifted(value, axis, steps):
    count = lax.axis_size(axis)
    return lax.ppermute(value, axis, [(source, source + steps) for source in range(count - steps)])


def swapped(value, axis, bit):
    count = lax.axis_size(axis)
    return lax.ppermute(value, axis, [(source, source ^ bit) for source in range(count)])


def widen(blocks, stride):
    count = lax.axis_size("head")
    while stride >= 1:
        for key in list(blocks):
            blocks[key ^ stride] = swapped(blocks[key], "head", stride)
        stride //= 2
    return [blocks[key] for key in range(count)]


def spread(value):
    return widen({0: value}, lax.axis_size("head") // 2)


def spread_prior(blocks):
    stride = lax.axis_size("head") // 2
    handed = {0: shifted(blocks[0], "ctx", 1), stride: shifted(blocks[stride], "ctx", 1)}
    return widen(handed, stride // 2)


def earlier_sum(value, axis):
    count = lax.axis_size(axis)
    place = lax.axis_index(axis)
    partner = swapped(value, axis, 1)
    total = value.astype(F32) + partner.astype(F32)
    before = jnp.where(place % 2 == 1, partner.astype(F32), 0.0)
    parts = [before]
    step = 1
    while 2 * step < count:
        arrived = shifted(total.astype(BF16), axis, 2 * step).astype(F32)
        parts.append(arrived)
        total = total + arrived
        step *= 2
    return sum(parts)


def fetch(tables, copies, semaphores):
    moves = [
        pltpu.make_async_copy(table, copy, semaphores.at[index])
        for index, (table, copy) in enumerate(zip(tables, copies))
    ]
    for move in moves:
        move.start()
    return moves


def table_scratch(*tables):
    return [pltpu.SMEM(table.shape, table.dtype) for table in tables] + [
        pltpu.SemaphoreType.DMA((len(tables),))
    ]


def clip_span(starts, lens, span, prior):
    place = lax.axis_index("ctx")
    if prior:
        source = jnp.maximum(place - 1, 0)
        shift = span - starts[source]
        length = jnp.where(place > 0, lens[source], 0)
    else:
        shift = -starts[place]
        length = lens[place]
    return shift, length, jnp.maximum(0, -shift), jnp.minimum(span, length - shift)


def clip_rows(rows, count, span):
    me = lax.axis_index("head")
    slot = lax.broadcasted_iota(jnp.int32, (1, span), 1)
    row = slot
    for key in range(count):
        inside = (slot >= key * rows) & (slot < (key + 1) * rows)
        row = jnp.where(inside, slot + ((me ^ key) - key) * rows, row)
    return row


def packed_shape(span, inner):
    whole = inner // 256 * 256
    return span + span * (inner - whole) // whole, whole


def pack(value):
    span, inner = value.shape
    whole = inner // 256 * 256
    groups = whole // (inner - whole)
    rows = span // groups
    tail = jnp.concatenate(
        [value[group * rows : (group + 1) * rows, whole:] for group in range(groups)], axis=1
    )
    return jnp.concatenate([value[:, :whole], tail], axis=0)


def unpack_tail(value, span):
    whole = value.shape[1]
    rows = value.shape[0] - span
    width = rows * whole // span
    return jnp.concatenate(
        [value[span:, group * width : (group + 1) * width] for group in range(span // rows)], axis=0
    )


def output_product(parts, weights, span):
    whole = parts[0].shape[1]
    left = jnp.concatenate(
        [part[:span, :] for part in parts] + [unpack_tail(part[...], span) for part in parts], axis=1
    )
    right = jnp.concatenate(
        [weight[:whole, :] for weight in weights] + [weight[whole:, :] for weight in weights], axis=0
    )
    return dot(left, right)


def attend_kernel(prior, heads, block, far_starts, far_lens, *refs):
    *refs, starts, lens, semaphores = refs
    moves = fetch((far_starts, far_lens), (starts, lens), semaphores)
    if prior:
        *refs, held_context = refs
    count = len(refs) - (6 if prior else 5)
    pieces = refs[:count]
    weights, *olds, result, queries, keys, values = refs[count:]
    context = olds[0] if prior else result
    rows, width = pieces[0].shape
    span = rows * count
    inner = weights.shape[0] // 3
    size = inner // heads
    if not prior:
        context[...] = jnp.zeros_like(context)
    row = clip_rows(rows, count, span)
    lane = lax.broadcasted_iota(jnp.int32, (1, inner), 1)
    owner = [(lane >= head * size) & (lane < (head + 1) * size) for head in range(heads)]
    groups = {}
    for head in range(heads):
        groups.setdefault(head * size // 128 * 128, []).append(head)

    if prior:
        for move in moves:
            move.wait()
        shift, length, first, last = clip_span(starts, lens, span, prior)

    @pl.when(last > first if prior else True)
    def _():
        frame = jnp.concatenate([piece[...] for piece in pieces], axis=0)
        wide = frame.astype(F32)
        scale = lax.rsqrt(jnp.sum(wide * wide, axis=-1, keepdims=True) * (1.0 / width) + EPS)
        full = dot_t(frame, weights[...])
        queries[...] = (full[:, :inner] * (scale * (size**-0.5 * math.log2(math.e)))).astype(BF16)
        keys[...] = (full[:, inner : 2 * inner] * scale).astype(BF16)
        values[...] = (full[:, 2 * inner :] * scale).astype(BF16)

    if not prior:
        for move in moves:
            move.wait()
        shift, length, first, last = clip_span(starts, lens, span, prior)

    def step(index, _):
        low = pl.multiple_of(index * block, block)
        place = low + lax.broadcasted_iota(jnp.int32, (block, 1), 0)
        live = (place >= first) & (place < last)
        pick = (place + shift == row) & live
        query = dot(jnp.where(pick, 1.0, 0.0).astype(BF16), queries[...])
        total = jnp.zeros((block, inner), F32)
        for base, members in groups.items():
            end = min(inner, base + 256)
            stack = jnp.concatenate(
                [jnp.where(owner[head], query, 0.0)[:, base:end].astype(BF16) for head in members], axis=0
            )
            scores = dot_t(stack, keys[:, base:end])
            scores = jnp.where(row < length, scores, LOW)
            powers = jnp.exp2(scores - jnp.max(scores, axis=-1, keepdims=True))
            mass = jnp.sum(powers, axis=-1, keepdims=True)
            mixed = dot(powers.astype(BF16), values[:, base:end]) / mass
            for place_in, head in enumerate(members):
                part = mixed[place_in * block : (place_in + 1) * block, :]
                sides = [part]
                if base:
                    sides = [jnp.zeros((block, base), F32)] + sides
                if end < inner:
                    sides = sides + [jnp.zeros((block, inner - end), F32)]
                total = jnp.where(owner[head], jnp.concatenate(sides, axis=1), total)
        here = pl.ds(low, block)
        if prior:
            context[here, :] = jnp.where(live, total, context[here, :].astype(F32)).astype(BF16)
        else:
            context[here, :] = total.astype(BF16)
        return 0

    if prior:
        held_context[...] = context[...]
        context = held_context
    lax.fori_loop(first // block, jnp.where(last > first, (last + block - 1) // block, 0), step, 0)
    if prior:
        result[...] = pack(context[...])


def attend(pieces, weights, starts, lens, heads, old=None):
    rows, _ = pieces[0].shape
    span = rows * len(pieces)
    inner = weights.shape[0] // 3
    olds = [] if old is None else [old]
    return pl.pallas_call(
        functools.partial(attend_kernel, old is not None, heads, min(BLOCK, span)),
        out_shape=jax.ShapeDtypeStruct(packed_shape(span, inner) if olds else (span, inner), BF16),
        in_specs=[HBM, HBM] + [VMEM] * (len(pieces) + 1 + len(olds)),
        out_specs=VMEM,
        scratch_shapes=[pltpu.VMEM((span, inner), BF16)] * (3 + len(olds)) + table_scratch(starts, lens),
        compiler_params=pltpu.CompilerParams(vmem_limit_bytes=16 * 2**20),
        cost_estimate=pl.CostEstimate(flops=5 * 10**9, bytes_accessed=4 * 10**6, transcendentals=10**6),
        name="attend_prior" if olds else "attend_own",
    )(starts, lens, *pieces, weights, *olds)


def warm_kernel(source, target):
    target[...] = source[...]


def warm(weights):
    return pl.pallas_call(
        warm_kernel,
        out_shape=jax.ShapeDtypeStruct(weights.shape, weights.dtype),
        in_specs=[VMEM],
        out_specs=VMEM,
        compiler_params=pltpu.CompilerParams(vmem_limit_bytes=6 * 2**20),
        cost_estimate=pl.CostEstimate(flops=10**9, bytes_accessed=4 * 10**6, transcendentals=0),
        name="warm",
    )(weights)


def arrange_kernel(far_starts, far_lens, *refs):
    *refs, starts, lens, semaphores = refs
    for move in fetch((far_starts, far_lens), (starts, lens), semaphores):
        move.wait()
    near_count = len(refs) - 1 - 2 * lax.axis_size("head")
    near_refs, refs = refs[: near_count], refs[near_count:]
    frame_out = refs[-1]
    count = (len(refs) - 1) // 2
    rows, _ = refs[0].shape
    span = rows * count
    row = clip_rows(rows, count, span)
    place = lax.broadcasted_iota(jnp.int32, (span, 1), 0)
    total = output_product(near_refs[: near_count // 2], near_refs[near_count // 2 :], span)
    for prior in (False, True):
        shift, length, _, _ = clip_span(starts, lens, span, prior)
        pick = (place + shift == row) & (row < length)
        frame = jnp.concatenate([piece[...] for piece in refs[prior * count : (prior + 1) * count]], axis=0)
        total = total + dot(jnp.where(pick, 1.0, 0.0).astype(BF16), frame)
    frame_out[...] = total


def arrange(own, prior, parts, outs, starts, lens):
    rows, width = own[0].shape
    span = rows * len(own)
    return pl.pallas_call(
        arrange_kernel,
        out_shape=jax.ShapeDtypeStruct((span, width), F32),
        in_specs=[HBM, HBM] + [VMEM] * (2 * len(own) + 2 * len(parts)),
        out_specs=VMEM,
        scratch_shapes=table_scratch(starts, lens),
        compiler_params=pltpu.CompilerParams(vmem_limit_bytes=16 * 2**20),
        cost_estimate=pl.CostEstimate(flops=2 * 10**9, bytes_accessed=3 * 10**6, transcendentals=0),
        name="arrange",
    )(starts, lens, *parts, *outs, *own, *prior)


def project_kernel(low, span, far_starts, far_lens, *refs):
    *refs, starts, lens, semaphores = refs
    moves = fetch((far_starts, far_lens), (starts, lens), semaphores)
    base, projector, text, *pieces, result = refs
    parts, weights = pieces[: len(pieces) // 2], pieces[len(pieces) // 2 :]
    rows = result.shape[0]
    here = slice(low, low + rows)
    whole = parts[0].shape[1]
    left = jnp.concatenate(
        [part[here, :] for part in parts] + [unpack_tail(part[...], span)[here] for part in parts], axis=1
    )
    right = jnp.concatenate(
        [weight[:whole, :] for weight in weights] + [weight[whole:, :] for weight in weights], axis=0
    )
    resid = base[here, :] + dot(left, right)
    scale = lax.rsqrt(jnp.mean(resid * resid, axis=-1, keepdims=True) + EPS)
    visual = dot((resid * scale).astype(BF16), projector[...]).astype(BF16)
    for move in moves:
        move.wait()
    _, _, own_first, own_last = clip_span(starts, lens, span, False)
    _, _, prior_first, prior_last = clip_span(starts, lens, span, True)
    place = low + lax.broadcasted_iota(jnp.int32, (rows, 1), 0)
    live = ((place >= own_first) & (place < own_last)) | (
        (place >= prior_first) & (place < prior_last)
    )
    result[...] = jnp.where(live, visual, text[here, :])


def project(index, count, base, parts, outs, projector, text, starts, lens):
    span, columns = text.shape
    rows = span // count
    return pl.pallas_call(
        functools.partial(project_kernel, index * rows, span),
        out_shape=jax.ShapeDtypeStruct((rows, columns), BF16),
        in_specs=[HBM, HBM] + [VMEM] * (3 + 2 * len(parts)),
        out_specs=VMEM,
        scratch_shapes=table_scratch(starts, lens),
        compiler_params=pltpu.CompilerParams(vmem_limit_bytes=12 * 2**20),
        cost_estimate=pl.CostEstimate(flops=10**9, bytes_accessed=2 * 10**6, transcendentals=0),
    )(starts, lens, base, projector, text, *parts, *outs)


def held(weights, part, key, depth):
    start = pl.multiple_of((lax.axis_index("head") ^ key) * depth, depth)
    return weights[part, pl.ds(start, depth), :]


def near_kernel(keys, weights, *refs):
    count = len(keys)
    pieces = refs[:count]
    query_sum, pair_sum, squares = refs[count:]
    norm = 0.0
    for piece in pieces:
        wide = piece[...].astype(F32)
        norm = norm + jnp.sum(wide * wide, axis=-1, keepdims=True)
    squares[...] = jnp.broadcast_to(norm, squares.shape)
    for part in range(3):
        total = 0.0
        for index in range(count):
            total = total + dot(pieces[index][...], held(weights, part, keys[index], pieces[index].shape[1]))
        if part == 0:
            query_sum[...] = total
        else:
            pair_sum[part - 1] = total


def near(pieces, keys, weights):
    span, _ = pieces[0].shape
    columns = weights.shape[2]
    return pl.pallas_call(
        functools.partial(near_kernel, keys),
        out_shape=(
            jax.ShapeDtypeStruct((span, columns), F32),
            jax.ShapeDtypeStruct((2, span, columns), F32),
            jax.ShapeDtypeStruct((span, HD), F32),
        ),
        in_specs=[VMEM] * (1 + len(pieces)),
        out_specs=(VMEM, VMEM, VMEM),
        compiler_params=pltpu.CompilerParams(vmem_limit_bytes=12 * 2**20),
        cost_estimate=pl.CostEstimate(flops=3 * 10**9, bytes_accessed=7 * 10**6, transcendentals=0),
    )(weights, *pieces)


def pair_kernel(keys, total_depth, weights, pair_sum, squares, *refs):
    count = len(keys)
    pieces = refs[:count]
    *olds, key_out, value_out, delta, scale_out = refs[count:]
    norm = squares[:, :1]
    for piece in pieces:
        wide = piece[...].astype(F32)
        norm = norm + jnp.sum(wide * wide, axis=-1, keepdims=True)
    scale = lax.rsqrt(norm * (1.0 / total_depth) + EPS)
    scale_out[...] = jnp.broadcast_to(scale, scale_out.shape)
    for part, out in ((0, key_out), (1, value_out)):
        total = pair_sum[part]
        for index in range(count):
            total = total + dot(pieces[index][...], held(weights, part + 1, keys[index], pieces[index].shape[1]))
        out[...] = (total * scale).astype(BF16)
    for head in range(delta.shape[0]):
        lanes = slice(head * HD, (head + 1) * HD)
        product = lax.dot_general(
            key_out[:, lanes], value_out[:, lanes], (((0,), (0,)), ((), ())), preferred_element_type=F32
        )
        if olds:
            product = product + olds[0][head]
        delta[head] = product.astype(delta.dtype)


def pair(kind, pieces, keys, weights, pair_sum, squares, olds):
    span, _ = pieces[0].shape
    columns = weights.shape[2]
    return pl.pallas_call(
        functools.partial(pair_kernel, keys, weights.shape[1]),
        out_shape=(
            jax.ShapeDtypeStruct((span, columns), BF16),
            jax.ShapeDtypeStruct((span, columns), BF16),
            jax.ShapeDtypeStruct((columns // HD, HD, HD), kind),
            jax.ShapeDtypeStruct((span, HD), F32),
        ),
        in_specs=[VMEM] * (3 + len(pieces) + len(olds)),
        out_specs=(VMEM,) * 4,
        compiler_params=pltpu.CompilerParams(vmem_limit_bytes=12 * 2**20),
        cost_estimate=pl.CostEstimate(flops=3 * 10**9, bytes_accessed=7 * 10**6, transcendentals=0),
    )(weights, pair_sum, squares, *pieces, *olds)


def within_kernel(keys, groups, weights, *refs):
    count = len(keys)
    sizes = (groups, groups, groups, groups, groups * count)
    lists, at = [], 0
    for size in sizes:
        lists.append(refs[at : at + size])
        at += size
    query_sums, scales, key_ins, value_ins, pieces = lists
    query_out, intra, buffers, semaphores = refs[at:]
    rows, depth = pieces[0].shape
    starts = [pl.multiple_of((lax.axis_index("head") ^ key) * depth, depth) for key in keys]
    moves = fetch(
        [weights.at[0, pl.ds(start, depth), :] for start in starts],
        [buffers.at[index] for index in range(count)],
        semaphores,
    )
    for move in moves:
        move.wait()
    causal = lax.broadcasted_iota(jnp.int32, (rows, rows), 0) >= lax.broadcasted_iota(
        jnp.int32, (rows, rows), 1
    )
    for group in range(groups):
        here = slice(group * rows, (group + 1) * rows)
        total = query_sums[group][...]
        for index in range(count):
            total = total + dot(pieces[group * count + index][...], buffers[index])
        query_out[here, :] = (total * scales[group][:, :1]).astype(BF16)
        for head in range(query_out.shape[1] // HD):
            lanes = slice(head * HD, (head + 1) * HD)
            query = query_out[here, lanes]
            corner = dot_t(query, key_ins[group][:, lanes])
            corner = jnp.where(causal, corner, 0.0).astype(BF16)
            total = dot(corner, value_ins[group][:, lanes])
            for earlier in range(group):
                left = dot_t(query, key_ins[earlier][:, lanes]).astype(BF16)
                total = total + dot(left, value_ins[earlier][:, lanes])
            intra[here, lanes] = total


def within(pieces, keys, weights, query_sums, scales, key_ins, value_ins):
    rows, depth = pieces[0].shape
    groups = len(query_sums)
    columns = weights.shape[2]
    return pl.pallas_call(
        functools.partial(within_kernel, keys, groups),
        out_shape=(
            jax.ShapeDtypeStruct((groups * rows, columns), BF16),
            jax.ShapeDtypeStruct((groups * rows, columns), F32),
        ),
        in_specs=[HBM] + [VMEM] * (4 * groups + len(pieces)),
        out_specs=(VMEM,) * 2,
        scratch_shapes=[
            pltpu.VMEM((len(keys), depth, columns), BF16),
            pltpu.SemaphoreType.DMA((len(keys),)),
        ],
        compiler_params=pltpu.CompilerParams(vmem_limit_bytes=12 * 2**20),
        cost_estimate=pl.CostEstimate(flops=3 * 10**9, bytes_accessed=5 * 10**6, transcendentals=0),
        name="within",
    )(weights, *query_sums, *scales, *key_ins, *value_ins, *pieces)


def finish_kernel(query, intra, carried, state, gain, out):
    for head in range(state.shape[0]):
        lanes = slice(head * HD, (head + 1) * HD)
        whole = (carried[head] + state[head]).astype(BF16)
        lin = intra[:, lanes] + dot(query[:, lanes], whole)
        scale = lax.rsqrt(jnp.mean(lin * lin, axis=-1, keepdims=True) + EPS)
        out[:, lanes] = (lin * scale * gain[:, lanes]).astype(BF16)


def finish(query, intra, carried, state, gain):
    return pl.pallas_call(
        finish_kernel,
        out_shape=jax.ShapeDtypeStruct(query.shape, BF16),
        in_specs=[VMEM] * 5,
        out_specs=VMEM,
        compiler_params=pltpu.CompilerParams(vmem_limit_bytes=8 * 2**20),
        cost_estimate=pl.CostEstimate(flops=10**8, bytes_accessed=3 * 10**6, transcendentals=0),
        name="finish",
    )(query, intra, carried, state, gain.reshape(1, -1))


def program(
    patches,
    clip_start,
    clip_len,
    text_rows,
    vision_qkv,
    vision_out,
    projector,
    layer_qkv,
    head_gain,
    state_in,
):
    groups = lax.axis_size("head")
    heads = VIT_HEADS // groups
    own = spread(patches)
    prior = spread_prior(own)
    outs = spread(vision_out)
    vision = jnp.transpose(vision_qkv, (1, 2, 0)).reshape(-1, vision_qkv.shape[0])
    layer = jnp.transpose(layer_qkv, (1, 0, 2))
    vision = warm(vision)
    context = attend(own, vision, clip_start, clip_len, heads)
    context = attend(prior, vision, clip_start, clip_len, heads, context)
    parts = spread(context)
    half = groups // 2
    near_keys, far_keys = tuple(range(half)), tuple(range(half, groups))
    base = arrange(own, prior, parts[:half], outs[:half], clip_start, clip_len)
    query_sums, scales, key_rows, value_rows, pieces, old = [], [], [], [], [], []
    for index in range(SPLIT):
        sequence = project(
            index, SPLIT, base, parts[half:], outs[half:], projector, text_rows, clip_start, clip_len
        )
        blocks = spread(sequence)
        query_sum, pair_sum, squares = near(blocks[:half], near_keys, layer)
        kind = BF16 if index == SPLIT - 1 else F32
        key_row, value_row, delta, scale = pair(kind, blocks[half:], far_keys, layer, pair_sum, squares, old)
        old = [delta]
        query_sums.append(query_sum)
        scales.append(scale)
        key_rows.append(key_row)
        value_rows.append(value_row)
        pieces += blocks[half:]
    carried = earlier_sum(delta, "ctx")
    query, intra = within(pieces, far_keys, layer, query_sums, scales, key_rows, value_rows)
    return finish(query, intra, carried, state_in, head_gain)


def solution(mesh):
    placed = (
        P(("ctx", "head"), None),
        P(),
        P(),
        P("ctx", "head"),
        P(None, None, "head"),
        P("head", None),
        P(None, "head"),
        P(None, None, "head"),
        P("head"),
        P("head", None, None),
    )
    return jax.shard_map(program, mesh=mesh, in_specs=placed, out_specs=P("ctx", "head"), check_vma=False)
```

time: 101 us -> 94.9 us (0.940)
  waiting for transfers between devices: 43.3 us -> 37.3 us
  starting transfers between devices: 28.8 us -> 30.3 us
  local copies, waits for them, and re-layouts: 7.33 us -> 5.95 us
    ppermute x3 -> x4, waiting for transfers between devices: 10.2 us -> 2.8 us  [shifted(): lax.ppermute(value, axis, [(source, source + steps) for source in range(c...]
    ppermute x1 -> x0, starting transfers between devices: 3.4 us -> none  [spread_prior(): blocks[stride] = lax.ppermute(value, ('ctx', 'head'), pairs)]
    ppermute x3 -> x4, starting transfers between devices: 16.6 us -> 19.1 us  [shifted(): lax.ppermute(value, axis, [(source, source + steps) for source in range(c...]
    ppermute x15 -> x18, starting transfers between devices: 8.77 us -> 11.2 us  [swapped(): lax.ppermute(value, axis, [(source, source ^ bit) for source in range(cou...]
    ppermute x15 -> x18, waiting for transfers between devices: 33.1 us -> 34.5 us  [swapped(): lax.ppermute(value, axis, [(source, source ^ bit) for source in range(cou...]
    unnamed x34 -> x28, local copies, waits for them, and re-layouts: 7.33 us -> 5.95 us
    pallas_call x1, Pallas kernels: 2.08 us -> 3.09 us  [arrange(): pl.pallas_call(arrange_kernel, out_shape=jax.ShapeDtypeStruct((span, widt...]
    pallas_call x2 -> x4, Pallas kernels: 5.5 us -> 5.09 us  [the longest x2 2.9 us: project(): pl.pallas_call(functools.partial(project_kernel, index * rows, span), out...]
  transfers between devices with their start and end apart: 19 -> 22, of which waited for: 8 -> 8; matrix products, arithmetic and copies ran while one was open for 0% -> 0% of each run, Pallas kernels for 11% -> 15%
where the time goes in v3:
time: 94.9 us; the launch traced here: 94.6 us
  waiting for transfers between devices  37.3 us (39%)
  starting transfers between devices  30.3 us (32%)
  Pallas kernels  18 us (19%)
  local copies, waits for them, and re-layouts  5.95 us (6%)
  other arithmetic  2.68 us (3%)
    ppermute x18, waiting for transfers between devices, swapped(): lax.ppermute(value, axis, [(source, source ^ bit) for source in range(cou...  34.5 us
    ppermute x4, starting transfers between devices, shifted(): lax.ppermute(value, axis, [(source, source + steps) for source in range(c...  19.1 us
    ppermute x18, starting transfers between devices, swapped(): lax.ppermute(value, axis, [(source, source ^ bit) for source in range(cou...  11.2 us
    unnamed x28, local copies, waits for them, and re-layouts  5.95 us
    pallas_call x2, Pallas kernels, attend(): pl.pallas_call(functools.partial(attend_kernel, old is not None, heads, m...  4.62 us
    pallas_call x1, Pallas kernels, arrange(): pl.pallas_call(arrange_kernel, out_shape=jax.ShapeDtypeStruct((span, widt...  3.09 us
    pallas_call x2, Pallas kernels, project(): pl.pallas_call(functools.partial(project_kernel, index * rows, span), out...  2.9 us
    ppermute x4, waiting for transfers between devices, shifted(): lax.ppermute(value, axis, [(source, source + steps) for source in range(c...  2.8 us
  transfers between devices with their start and end apart: 22, of which 8 were waited for; matrix products, arithmetic and copies ran while one was open for 0% of the time, Pallas kernels for 15%

profile of v3, /device:TPU:0, one launch (start us, length us, event | category | flops | bytes accessed | tf_op | source)
XLA Modules:
  0.0 94.6 jit_solution(5981017828732302843)
XLA Ops:
  0.0 3.0 %collective-permute-start.2 = (bf16[128,1152]{1,0:T(8,128)(2,1)}, bf16[128,1152]{1,0:T(8,128)(2,1)S(1)}, u32[]{:S(2)}, u32[]{:S(2)}) collective-permute-start(bf16[128,1152]{1,0:T(8,128)(2,1)} %refs_4_.1), channel_id=1, source_target_pairs={{0,2},{1,3},{2,0},{3,1},{4,6},{5,7},{6,4},{7,5},{8,10},{9,11},{10,... | collective-permute-start | bytes 884744 | tf_op jit(solution)/shard_map/ppermute | solution.py:39
  3.0 3.4 %collective-permute-start = (bf16[128,1152]{1,0:T(8,128)(2,1)}, bf16[128,1152]{1,0:T(8,128)(2,1)S(1)}, u32[]{:S(2)}, u32[]{:S(2)}) collective-permute-start(bf16[128,1152]{1,0:T(8,128)(2,1)} %refs_4_.1), channel_id=1, source_target_pairs={{0,4},{4,8},{8,12},{12,16},{16,20},{20,24},{24,28},{1,5},{5,9},{9,... | collective-permute-start | bytes 884744 | tf_op jit(solution)/shard_map/ppermute | solution.py:34
  6.5 3.7 %collective-permute-done.2.refs_2_.refs_6_ = bf16[128,1152]{1,0:T(8,128)(2,1)S(1)} collective-permute-done((bf16[128,1152]{1,0:T(8,128)(2,1)}, bf16[128,1152]{1,0:T(8,128)(2,1)S(1)}, u32[]{:S(2)}, u32[]{:S(2)}) %collective-permute-start.2) | collective-permute-done | bytes 294944 | tf_op jit(solution)/shard_map/ppermute | solution.py:39
  10.2 3.7 %collective-permute-start.3 = (bf16[128,1152]{1,0:T(8,128)(2,1)S(1)}, bf16[128,1152]{1,0:T(8,128)(2,1)S(1)}, u32[]{:S(2)}, u32[]{:S(2)}) collective-permute-start(bf16[128,1152]{1,0:T(8,128)(2,1)S(1)} %collective-permute-done.2.refs_2_.refs_6_), channel_id=1, source_target_pairs={{0,4},{4,8},{8,12},{12,16},{16,20},{20,24},{24,28},{1,5},{5,9},{9,... | collective-permute-start | bytes 884744 | tf_op jit(solution)/shard_map/ppermute | solution.py:34
  14.0 1.6 %collective-permute-start.11 = (bf16[288,1152]{1,0:T(8,128)(2,1)}, bf16[288,1152]{1,0:T(8,128)(2,1)S(1)}, u32[]{:S(2)}, u32[]{:S(2)}) collective-permute-start(bf16[288,1152]{1,0:T(8,128)(2,1)} %refs_2_.3), channel_id=1, source_target_pairs={{0,2},{1,3},{2,0},{3,1},{4,6},{5,7},{6,4},{7,5},{8,10},{9,11},{10,... | collective-permute-start | bytes 1990664 | tf_op jit(solution)/shard_map/ppermute | solution.py:39
  15.5 1.6 %copy-done.2 = bf16[1152,3,288]{0,2,1:T(8,128)(2,1)S(1)} copy-done((bf16[1152,3,288]{0,2,1:T(8,128)(2,1)S(1)}, bf16[1152,3,288]{0,2,1:T(8,128)(2,1)}, u32[]{:S(2)}) %copy-start.2) | copy-done | bytes 1990680
  17.2 0.9 copy-done.8
  19.3 3.7 %attend_own.1.refs_5_ = bf16[512,288]{1,0:T(8,128)(2,1)S(1)} custom-call(s32[8]{0:T(128)S(1)} %copy-done.5, s32[8]{0:T(128)S(1)} %copy-done.6, bf16[128,1152]{1,0:T(8,128)(2,1)S(1)} %copy-done.9, bf16[128,1152]{1,0:T(8,128)(2,1)S(1)} %collective-permute-done.5.refs_1_.refs_5_, bf16[128,1152]{1,0:T(8,128)(2,1)S(1)} %collective-permute-done.2.refs_2_.refs_6_, ...), custom_call_target="tpu_custom_call" | custom-call | flops 5000000000 | bytes 4000000 | tf_op jit(solution)/shard_map/attend_own/pallas_call | solution.py:238
  23.0 8.5 %collective-permute-done.11.refs_5_ = bf16[288,1152]{1,0:T(8,128)(2,1)S(1)} collective-permute-done((bf16[288,1152]{1,0:T(8,128)(2,1)}, bf16[288,1152]{1,0:T(8,128)(2,1)S(1)}, u32[]{:S(2)}, u32[]{:S(2)}) %collective-permute-start.11) | collective-permute-done | bytes 663584 | tf_op jit(solution)/shard_map/ppermute | solution.py:39
  31.5 0.9 attend_prior.1.refs_0_
  32.4 1.6 %collective-permute-start.9 = (bf16[576,256]{1,0:T(8,128)(2,1)S(1)}, bf16[576,256]{1,0:T(8,128)(2,1)S(1)}, u32[]{:S(2)}, u32[]{:S(2)}) collective-permute-start(bf16[576,256]{1,0:T(8,128)(2,1)S(1)} %attend_prior.1.refs_0_), channel_id=1, source_target_pairs={{0,2},{1,3},{2,0},{3,1},{4,6},{5,7},{6,4},{7,5},{8,10},{9,11},{10,... | collective-permute-start | bytes 884744 | tf_op jit(solution)/shard_map/ppermute | solution.py:39
  34.2 7.7 %collective-permute-done.9.refs_3_ = bf16[576,256]{1,0:T(8,128)(2,1)S(1)} collective-permute-done((bf16[576,256]{1,0:T(8,128)(2,1)S(1)}, bf16[576,256]{1,0:T(8,128)(2,1)S(1)}, u32[]{:S(2)}, u32[]{:S(2)}) %collective-permute-start.9) | collective-permute-done | bytes 294944 | tf_op jit(solution)/shard_map/ppermute | solution.py:39
  41.9 3.1 %arrange.1.refs_0_ = f32[512,1152]{1,0:T(8,128)S(1)} custom-call(s32[8]{0:T(128)S(1)} %copy-done.5, s32[8]{0:T(128)S(1)} %copy-done.6, bf16[576,256]{1,0:T(8,128)(2,1)S(1)} %attend_prior.1.refs_0_, bf16[576,256]{1,0:T(8,128)(2,1)S(1)} %collective-permute-done.7.refs_1_, bf16[288,1152]{1,0:T(8,128)(2,1)S(1)} %copy-done.8, ...), custom_call_target="tpu_custom_call" | custom-call | flops 2000000000 | bytes 3000000 | tf_op jit(solution)/shard_map/arrange/pallas_call | solution.py:290
  45.1 1.5 %shard_map.100.refs_0_ = bf16[256,512]{1,0:T(8,128)(2,1)S(1)} custom-call(s32[8]{0:T(128)S(1)} %copy-done.5, s32[8]{0:T(128)S(1)} %copy-done.6, f32[512,1152]{1,0:T(8,128)S(1)} %arrange.1.refs_0_, bf16[1152,512]{1,0:T(8,128)(2,1)S(1)} %copy-done, bf16[512,512]{1,0:T(8,128)(2,1)S(1)} %copy-done.1, bf16[576,256]{1,0:T(8,128)(2,1)S(1)} %collective-permute-done.9.refs_3_, ...), custom_call_target="tpu_custom_call" | custom-call | flops 1000000000 | bytes 2000000 | tf_op jit(solution)/shard_map/pallas_call | solution.py:333
  46.5 1.6 %collective-permute-start.15 = (bf16[256,512]{1,0:T(8,128)(2,1)S(1)}, bf16[256,512]{1,0:T(8,128)(2,1)S(1)}, u32[]{:S(2)}, u32[]{:S(2)}) collective-permute-start(bf16[256,512]{1,0:T(8,128)(2,1)S(1)} %shard_map.100.refs_0_), channel_id=1, source_target_pairs={{0,2},{1,3},{2,0},{3,1},{4,6},{5,7},{6,4},{7,5},{8,10},{9,11},{10,... | collective-permute-start | bytes 786440 | tf_op jit(solution)/shard_map/ppermute | solution.py:39
  48.1 1.4 %shard_map.102.refs_0_ = bf16[256,512]{1,0:T(8,128)(2,1)S(1)} custom-call(s32[8]{0:T(128)S(1)} %copy-done.5, s32[8]{0:T(128)S(1)} %copy-done.6, f32[512,1152]{1,0:T(8,128)S(1)} %arrange.1.refs_0_, bf16[1152,512]{1,0:T(8,128)(2,1)S(1)} %copy-done, bf16[512,512]{1,0:T(8,128)(2,1)S(1)} %copy-done.1, bf16[576,256]{1,0:T(8,128)(2,1)S(1)} %collective-permute-done.9.refs_3_, ...), custom_call_target="tpu_custom_call" | custom-call | flops 1000000000 | bytes 2000000 | tf_op jit(solution)/shard_map/pallas_call | solution.py:333
  50.7 5.1 %collective-permute-done.15.refs_0_.refs_8_ = bf16[256,512]{1,0:T(8,128)(2,1)S(1)} collective-permute-done((bf16[256,512]{1,0:T(8,128)(2,1)S(1)}, bf16[256,512]{1,0:T(8,128)(2,1)S(1)}, u32[]{:S(2)}, u32[]{:S(2)}) %collective-permute-start.15) | collective-permute-done | bytes 262176 | tf_op jit(solution)/shard_map/ppermute | solution.py:39
  55.8 5.1 %collective-permute-done.17.refs_0_.refs_10_ = bf16[256,512]{1,0:T(8,128)(2,1)S(1)} collective-permute-done((bf16[256,512]{1,0:T(8,128)(2,1)S(1)}, bf16[256,512]{1,0:T(8,128)(2,1)S(1)}, u32[]{:S(2)}, u32[]{:S(2)}) %collective-permute-start.17) | collective-permute-done | bytes 262176 | tf_op jit(solution)/shard_map/ppermute | solution.py:39
  61.0 1.0 %shard_map.101 = (f32[256,512]{1,0:T(8,128)S(1)}, f32[2,256,512]{2,1,0:T(8,128)S(1)}, f32[256,128]{1,0:T(8,128)S(1)}) custom-call(bf16[3,2048,512]{2,1,0:T(8,128)(2,1)S(1)} %bitcast.9, bf16[256,512]{1,0:T(8,128)(2,1)S(1)} %shard_map.100.refs_0_, bf16[256,512]{1,0:T(8,128)(2,1)S(1)} %collective-permute-done.13.refs_1_), custom_call_target="tpu_custom_call" | custom-call | flops 3000000000 | bytes 7000000 | tf_op jit(solution)/shard_map/pallas_call | solution.py:371
  62.0 1.0 %shard_map.103 = (f32[256,512]{1,0:T(8,128)S(1)}, f32[2,256,512]{2,1,0:T(8,128)S(1)}, f32[256,128]{1,0:T(8,128)S(1)}) custom-call(bf16[3,2048,512]{2,1,0:T(8,128)(2,1)S(1)} %bitcast.10, bf16[256,512]{1,0:T(8,128)(2,1)S(1)} %shard_map.102.refs_0_, bf16[256,512]{1,0:T(8,128)(2,1)S(1)} %collective-permute-done.14.refs_1_), custom_call_target="tpu_custom_call" | custom-call | flops 3000000000 | bytes 7000000 | tf_op jit(solution)/shard_map/pallas_call | solution.py:371
  63.0 1.0 %shard_map.104 = (bf16[256,512]{1,0:T(8,128)(2,1)S(1)}, bf16[256,512]{1,0:T(8,128)(2,1)S(1)}, f32[4,128,128]{2,1,0:T(8,128)S(1)}, f32[256,128]{1,0:T(8,128)S(1)}) custom-call(bf16[3,2048,512]{2,1,0:T(8,128)(2,1)S(1)} %bitcast.11, f32[2,256,512]{2,1,0:T(8,128)S(1)} %get-tuple-element.23.pair_sum, f32[256,128]{1,0:T(8,128)S(1)} %get-tuple-element.24.squares, ...), custom_call_target="tpu_custom_call" | custom-call | flops 3000000000 | bytes 7000000 | tf_op jit(solution)/shard_map/pallas_call | solution.py:413
  63.9 1.0 %shard_map.105 = (bf16[256,512]{1,0:T(8,128)(2,1)S(1)}, bf16[256,512]{1,0:T(8,128)(2,1)S(1)}, bf16[4,128,128]{2,1,0:T(8,128)(2,1)S(1)}, f32[256,128]{1,0:T(8,128)S(1)}) custom-call(bf16[3,2048,512]{2,1,0:T(8,128)(2,1)S(1)} %bitcast.12, f32[2,256,512]{2,1,0:T(8,128)S(1)} %get-tuple-element.26.pair_sum, f32[256,128]{1,0:T(8,128)S(1)} %get-tuple-element.27.squares, ...), custom_call_target="tpu_custom_call" | custom-call | flops 3000000000 | bytes 7000000 | tf_op jit(solution)/shard_map/pallas_call | solution.py:413
  64.9 1.6 %collective-permute-start.19 = (bf16[4,128,128]{2,1,0:T(8,128)(2,1)S(1)}, bf16[4,128,128]{2,1,0:T(8,128)(2,1)S(1)}, u32[]{:S(2)}, u32[]{:S(2)}) collective-permute-start(bf16[4,128,128]{2,1,0:T(8,128)(2,1)S(1)} %get-tuple-element.36), channel_id=1, source_target_pairs={{0,4},{4,0},{8,12},{12,8},{16,20},{20,16},{24,28},{28,24},{1,5},{5... | collective-permute-start | bytes 393224 | tf_op jit(solution)/shard_map/ppermute | solution.py:39
  66.5 4.4 %collective-permute-done.19 = bf16[4,128,128]{2,1,0:T(8,128)(2,1)S(1)} collective-permute-done((bf16[4,128,128]{2,1,0:T(8,128)(2,1)S(1)}, bf16[4,128,128]{2,1,0:T(8,128)(2,1)S(1)}, u32[]{:S(2)}, u32[]{:S(2)}) %collective-permute-start.19) | collective-permute-done | bytes 131104 | tf_op jit(solution)/shard_map/ppermute | solution.py:39
  72.2 4.1 %collective-permute-start.20 = (bf16[4,128,128]{2,1,0:T(8,128)(2,1)}, bf16[4,128,128]{2,1,0:T(8,128)(2,1)}, u32[]{:S(2)}, u32[]{:S(2)}) collective-permute-start(bf16[4,128,128]{2,1,0:T(8,128)(2,1)} %fusion.2), channel_id=1, source_target_pairs={{0,8},{4,12},{8,16},{12,20},{16,24},{20,28},{1,9},{5,13},{9,17},{1... | collective-permute-start | bytes 393224 | tf_op jit(solution)/shard_map/ppermute | solution.py:34
  76.3 2.2 %collective-permute-done.20 = bf16[4,128,128]{2,1,0:T(8,128)(2,1)} collective-permute-done((bf16[4,128,128]{2,1,0:T(8,128)(2,1)}, bf16[4,128,128]{2,1,0:T(8,128)(2,1)}, u32[]{:S(2)}, u32[]{:S(2)}) %collective-permute-start.20) | collective-permute-done | bytes 131104 | tf_op jit(solution)/shard_map/ppermute | solution.py:34
  78.5 1.0 %fusion.1 = bf16[4,128,128]{2,1,0:T(8,128)(2,1)S(1)} fusion(bf16[4,128,128]{2,1,0:T(8,128)(2,1)} %collective-permute-done.20, bf16[4,128,128]{2,1,0:T(8,128)(2,1)} %copy-done.10, bf16[4,128,128]{2,1,0:T(8,128)(2,1)S(1)} %get-tuple-element.36), kind=kLoop, calls=%fused_computation.5 | loop fusion | flops 393216 | bytes 524288 | tf_op jit(solution)/shard_map/convert_element_type | solution.py:70
  79.6 7.8 %collective-permute-start.21 = (bf16[4,128,128]{2,1,0:T(8,128)(2,1)S(1)}, bf16[4,128,128]{2,1,0:T(8,128)(2,1)S(1)}, u32[]{:S(2)}, u32[]{:S(2)}) collective-permute-start(bf16[4,128,128]{2,1,0:T(8,128)(2,1)S(1)} %fusion.1), channel_id=1, source_target_pairs={{0,16},{4,20},{8,24},{12,28},{1,17},{5,21},{9,25},{13,29},{2,18},{... | collective-permute-start | bytes 393224 | tf_op jit(solution)/shard_map/ppermute | solution.py:34
  87.4 2.8 %copy-done.7 = bf16[2048,3,512]{2,0,1:T(8,128)(2,1)S(1)} copy-done((bf16[2048,3,512]{2,0,1:T(8,128)(2,1)S(1)}, bf16[2048,3,512]{2,0,1:T(8,128)(2,1)}, u32[]{:S(2)}) %copy-start.7) | copy-done | bytes 6291480
  90.2 2.0 %within.1 = (bf16[512,512]{1,0:T(8,128)(2,1)S(1)}, f32[512,512]{1,0:T(8,128)S(1)}) custom-call(bf16[3,2048,512]{2,1,0:T(8,128)(2,1)S(1)} %bitcast.13, f32[256,512]{1,0:T(8,128)S(1)} %get-tuple-element.21.refs_0_, f32[256,512]{1,0:T(8,128)S(1)} %get-tuple-element.22.refs_1_, f32[256,128]{1,0:T(8,128)S(1)} %get-tuple-element.25.refs_2_, ...), custom_call_target="tpu_custom_call" | custom-call | flops 3000000000 | bytes 5000000 | tf_op jit(solution)/shard_map/within/pallas_call | solution.py:471
  92.3 1.0 %fusion.carried = f32[4,128,128]{2,1,0:T(8,128)S(1)} fusion(bf16[4,128,128]{2,1,0:T(8,128)(2,1)} %collective-permute-done.20, bf16[4,128,128]{2,1,0:T(8,128)(2,1)S(1)} %copy-done.11, bf16[4,128,128]{2,1,0:T(8,128)(2,1)S(1)} %collective-permute-done.21, pred[]{:T(512)S(6)} %eq.5), kind=kLoop, calls=%fused_computation.4 | loop fusion | flops 393216 | bytes 655361 | tf_op jit(solution)/shard_map/add | solution.py:74
  93.3 1.3 %finish.1 = bf16[512,512]{1,0:T(8,128)(2,1)} custom-call(bf16[512,512]{1,0:T(8,128)(2,1)S(1)} %get-tuple-element.34.query, f32[512,512]{1,0:T(8,128)S(1)} %get-tuple-element.35.intra, f32[4,128,128]{2,1,0:T(8,128)S(1)} %fusion.carried, f32[4,128,128]{2,1,0:T(8,128)S(1)} %copy-done.3, f32[1,512]{1,0:T(1,128)S(1)} %bitcast.6), custom_call_target="tpu_custom_call" | custom-call | flops 100000000 | bytes 3000000 | tf_op jit(solution)/shard_map/finish/pallas_call | solution.py:499
  (56 shorter events, 4.2 us)
Async XLA Ops:
  0.0 10.2 %collective-permute-start.2 = (bf16[128,1152]{1,0:T(8,128)(2,1)}, bf16[128,1152]{1,0:T(8,128)(2,1)S(1)}, u32[]{:S(2)}, u32[]{:S(2)}) collective-permute-start(bf16[128,1152]{1,0:T(8,128)(2,1)} %refs_4_.1), channel_id=1, source_target_pairs={{0,2},{1,3},{2,0},{3,1},{4,6},{5,7},{6,4},{7,5},{8,10},{9,11},{10,... | collective-permute-start | bytes 884744 | tf_op jit(solution)/shard_map/ppermute | solution.py:39
  3.0 14.3 %collective-permute-start = (bf16[128,1152]{1,0:T(8,128)(2,1)}, bf16[128,1152]{1,0:T(8,128)(2,1)S(1)}, u32[]{:S(2)}, u32[]{:S(2)}) collective-permute-start(bf16[128,1152]{1,0:T(8,128)(2,1)} %refs_4_.1), channel_id=1, source_target_pairs={{0,4},{4,8},{8,12},{12,16},{16,20},{20,24},{24,28},{1,5},{5,9},{9,... | collective-permute-start | bytes 884744 | tf_op jit(solution)/shard_map/ppermute | solution.py:34
  6.4 11.9 %collective-permute-start.5 = (bf16[128,1152]{1,0:T(8,128)(2,1)}, bf16[128,1152]{1,0:T(8,128)(2,1)S(1)}, u32[]{:S(2)}, u32[]{:S(2)}) collective-permute-start(bf16[128,1152]{1,0:T(8,128)(2,1)} %refs_4_.1), channel_id=1, source_target_pairs={{0,1},{1,0},{2,3},{3,2},{4,5},{5,4},{6,7},{7,6},{8,9},{9,8},{10,11... | collective-permute-start | bytes 884744 | tf_op jit(solution)/shard_map/ppermute | solution.py:39
  10.2 9.1 %collective-permute-start.3 = (bf16[128,1152]{1,0:T(8,128)(2,1)S(1)}, bf16[128,1152]{1,0:T(8,128)(2,1)S(1)}, u32[]{:S(2)}, u32[]{:S(2)}) collective-permute-start(bf16[128,1152]{1,0:T(8,128)(2,1)S(1)} %collective-permute-done.2.refs_2_.refs_6_), channel_id=1, source_target_pairs={{0,4},{4,8},{8,12},{12,16},{16,20},{20,24},{24,28},{1,5},{5,9},{9,... | collective-permute-start | bytes 884744 | tf_op jit(solution)/shard_map/ppermute | solution.py:34
  13.9 5.4 %collective-permute-start.6 = (bf16[128,1152]{1,0:T(8,128)(2,1)S(1)}, bf16[128,1152]{1,0:T(8,128)(2,1)S(1)}, u32[]{:S(2)}, u32[]{:S(2)}) collective-permute-start(bf16[128,1152]{1,0:T(8,128)(2,1)S(1)} %collective-permute-done.2.refs_2_.refs_6_), channel_id=1, source_target_pairs={{0,1},{1,0},{2,3},{3,2},{4,5},{5,4},{6,7},{7,6},{8,9},{9,8},{10,11... | collective-permute-start | bytes 884744 | tf_op jit(solution)/shard_map/ppermute | solution.py:39
  14.0 17.5 %collective-permute-start.11 = (bf16[288,1152]{1,0:T(8,128)(2,1)}, bf16[288,1152]{1,0:T(8,128)(2,1)S(1)}, u32[]{:S(2)}, u32[]{:S(2)}) collective-permute-start(bf16[288,1152]{1,0:T(8,128)(2,1)} %refs_2_.3), channel_id=1, source_target_pairs={{0,2},{1,3},{2,0},{3,1},{4,6},{5,7},{6,4},{7,5},{8,10},{9,11},{10,... | collective-permute-start | bytes 1990664 | tf_op jit(solution)/shard_map/ppermute | solution.py:39
  17.1 2.2 %copy-start.5 = (s32[8]{0:T(128)S(1)}, s32[8]{0:T(128)}, u32[]{:S(2)}) copy-start(s32[8]{0:T(128)} %far_starts.9) | copy-start | bytes 100
  17.1 2.2 %copy-start.6 = (s32[8]{0:T(128)S(1)}, s32[8]{0:T(128)}, u32[]{:S(2)}) copy-start(s32[8]{0:T(128)} %far_lens.9) | copy-start | bytes 100
  17.1 2.2 %copy-start.9 = (bf16[128,1152]{1,0:T(8,128)(2,1)S(1)}, bf16[128,1152]{1,0:T(8,128)(2,1)}, u32[]{:S(2)}) copy-start(bf16[128,1152]{1,0:T(8,128)(2,1)} %refs_4_.1) | copy-start | bytes 884740
  18.2 23.8 %collective-permute-start.8 = (bf16[288,1152]{1,0:T(8,128)(2,1)S(1)}, bf16[288,1152]{1,0:T(8,128)(2,1)S(1)}, u32[]{:S(2)}, u32[]{:S(2)}) collective-permute-start(bf16[288,1152]{1,0:T(8,128)(2,1)S(1)} %copy-done.8), channel_id=1, source_target_pairs={{0,1},{1,0},{2,3},{3,2},{4,5},{5,4},{6,7},{7,6},{8,9},{9,8},{10,11... | collective-permute-start | bytes 1990664 | tf_op jit(solution)/shard_map/ppermute | solution.py:39
  18.3 13.2 %collective-permute-start.1 = (bf16[128,1152]{1,0:T(8,128)(2,1)S(1)}, bf16[128,1152]{1,0:T(8,128)(2,1)S(1)}, u32[]{:S(2)}, u32[]{:S(2)}) collective-permute-start(bf16[128,1152]{1,0:T(8,128)(2,1)S(1)} %collective-permute-done.refs_0_.refs_8_), channel_id=1, source_target_pairs={{0,1},{1,0},{2,3},{3,2},{4,5},{5,4},{6,7},{7,6},{8,9},{9,8},{10,11... | collective-permute-start | bytes 884744 | tf_op jit(solution)/shard_map/ppermute | solution.py:39
  19.2 12.2 %collective-permute-start.4 = (bf16[128,1152]{1,0:T(8,128)(2,1)S(1)}, bf16[128,1152]{1,0:T(8,128)(2,1)S(1)}, u32[]{:S(2)}, u32[]{:S(2)}) collective-permute-start(bf16[128,1152]{1,0:T(8,128)(2,1)S(1)} %collective-permute-done.3.refs_2_.refs_10_), channel_id=1, source_target_pairs={{0,1},{1,0},{2,3},{3,2},{4,5},{5,4},{6,7},{7,6},{8,9},{9,8},{10,11... | collective-permute-start | bytes 884744 | tf_op jit(solution)/shard_map/ppermute | solution.py:39
  31.5 13.6 %collective-permute-start.12 = (bf16[288,1152]{1,0:T(8,128)(2,1)S(1)}, bf16[288,1152]{1,0:T(8,128)(2,1)S(1)}, u32[]{:S(2)}, u32[]{:S(2)}) collective-permute-start(bf16[288,1152]{1,0:T(8,128)(2,1)S(1)} %collective-permute-done.11.refs_5_), channel_id=1, source_target_pairs={{0,1},{1,0},{2,3},{3,2},{4,5},{5,4},{6,7},{7,6},{8,9},{9,8},{10,11... | collective-permute-start | bytes 1990664 | tf_op jit(solution)/shard_map/ppermute | solution.py:39
  32.4 12.7 %copy-start = (bf16[1152,512]{1,0:T(8,128)(2,1)S(1)}, bf16[1152,512]{1,0:T(8,128)(2,1)}, u32[]{:S(2)}) copy-start(bf16[1152,512]{1,0:T(8,128)(2,1)} %refs_1_.3) | copy-start | bytes 3538948
  32.4 12.7 %copy-start.1 = (bf16[512,512]{1,0:T(8,128)(2,1)S(1)}, bf16[512,512]{1,0:T(8,128)(2,1)}, u32[]{:S(2)}) copy-start(bf16[512,512]{1,0:T(8,128)(2,1)} %refs_2_.5) | copy-start | bytes 1572868
  32.4 9.5 %collective-permute-start.9 = (bf16[576,256]{1,0:T(8,128)(2,1)S(1)}, bf16[576,256]{1,0:T(8,128)(2,1)S(1)}, u32[]{:S(2)}, u32[]{:S(2)}) collective-permute-start(bf16[576,256]{1,0:T(8,128)(2,1)S(1)} %attend_prior.1.refs_0_), channel_id=1, source_target_pairs={{0,2},{1,3},{2,0},{3,1},{4,6},{5,7},{6,4},{7,5},{8,10},{9,11},{10,... | collective-permute-start | bytes 884744 | tf_op jit(solution)/shard_map/ppermute | solution.py:39
  34.0 7.9 %collective-permute-start.7 = (bf16[576,256]{1,0:T(8,128)(2,1)S(1)}, bf16[576,256]{1,0:T(8,128)(2,1)S(1)}, u32[]{:S(2)}, u32[]{:S(2)}) collective-permute-start(bf16[576,256]{1,0:T(8,128)(2,1)S(1)} %attend_prior.1.refs_0_), channel_id=1, source_target_pairs={{0,1},{1,0},{2,3},{3,2},{4,5},{5,4},{6,7},{7,6},{8,9},{9,8},{10,11... | collective-permute-start | bytes 884744 | tf_op jit(solution)/shard_map/ppermute | solution.py:39
  41.9 3.2 %collective-permute-start.10 = (bf16[576,256]{1,0:T(8,128)(2,1)S(1)}, bf16[576,256]{1,0:T(8,128)(2,1)S(1)}, u32[]{:S(2)}, u32[]{:S(2)}) collective-permute-start(bf16[576,256]{1,0:T(8,128)(2,1)S(1)} %collective-permute-done.9.refs_3_), channel_id=1, source_target_pairs={{0,1},{1,0},{2,3},{3,2},{4,5},{5,4},{6,7},{7,6},{8,9},{9,8},{10,11... | collective-permute-start | bytes 884744 | tf_op jit(solution)/shard_map/ppermute | solution.py:39
  41.9 19.0 %slice-start = ((s8[6291456]{0:T(1024)(128)(4,1)}), s8[4194304]{0:T(1024)(128)(4,1)S(1)}, s32[]{:S(2)}) async-start(s8[6291456]{0:T(1024)(128)(4,1)} %bitcast.7), calls=%async_computation | async-start | bytes 8388608
  45.0 15.9 %slice-start.1 = ((s8[6291456]{0:T(1024)(128)(4,1)}), s8[2097152]{0:T(1024)(128)(4,1)S(1)}, s32[]{:S(2)}) async-start(s8[6291456]{0:T(1024)(128)(4,1)} %bitcast.7), calls=%async_computation.1 | async-start | bytes 4194304
  46.5 9.2 %collective-permute-start.15 = (bf16[256,512]{1,0:T(8,128)(2,1)S(1)}, bf16[256,512]{1,0:T(8,128)(2,1)S(1)}, u32[]{:S(2)}, u32[]{:S(2)}) collective-permute-start(bf16[256,512]{1,0:T(8,128)(2,1)S(1)} %shard_map.100.refs_0_), channel_id=1, source_target_pairs={{0,2},{1,3},{2,0},{3,1},{4,6},{5,7},{6,4},{7,5},{8,10},{9,11},{10,... | collective-permute-start | bytes 786440 | tf_op jit(solution)/shard_map/ppermute | solution.py:39
  49.6 11.4 %collective-permute-start.17 = (bf16[256,512]{1,0:T(8,128)(2,1)S(1)}, bf16[256,512]{1,0:T(8,128)(2,1)S(1)}, u32[]{:S(2)}, u32[]{:S(2)}) collective-permute-start(bf16[256,512]{1,0:T(8,128)(2,1)S(1)} %shard_map.102.refs_0_), channel_id=1, source_target_pairs={{0,2},{1,3},{2,0},{3,1},{4,6},{5,7},{6,4},{7,5},{8,10},{9,11},{10,... | collective-permute-start | bytes 786440 | tf_op jit(solution)/shard_map/ppermute | solution.py:39
  50.2 10.8 %collective-permute-start.13 = (bf16[256,512]{1,0:T(8,128)(2,1)S(1)}, bf16[256,512]{1,0:T(8,128)(2,1)S(1)}, u32[]{:S(2)}, u32[]{:S(2)}) collective-permute-start(bf16[256,512]{1,0:T(8,128)(2,1)S(1)} %shard_map.100.refs_0_), channel_id=1, source_target_pairs={{0,1},{1,0},{2,3},{3,2},{4,5},{5,4},{6,7},{7,6},{8,9},{9,8},{10,11... | collective-permute-start | bytes 786440 | tf_op jit(solution)/shard_map/ppermute | solution.py:39
  50.2 11.8 %collective-permute-start.14 = (bf16[256,512]{1,0:T(8,128)(2,1)S(1)}, bf16[256,512]{1,0:T(8,128)(2,1)S(1)}, u32[]{:S(2)}, u32[]{:S(2)}) collective-permute-start(bf16[256,512]{1,0:T(8,128)(2,1)S(1)} %shard_map.102.refs_0_), channel_id=1, source_target_pairs={{0,1},{1,0},{2,3},{3,2},{4,5},{5,4},{6,7},{7,6},{8,9},{9,8},{10,11... | collective-permute-start | bytes 786440 | tf_op jit(solution)/shard_map/ppermute | solution.py:39
  55.8 7.2 %collective-permute-start.16 = (bf16[256,512]{1,0:T(8,128)(2,1)S(1)}, bf16[256,512]{1,0:T(8,128)(2,1)S(1)}, u32[]{:S(2)}, u32[]{:S(2)}) collective-permute-start(bf16[256,512]{1,0:T(8,128)(2,1)S(1)} %collective-permute-done.15.refs_0_.refs_8_), channel_id=1, source_target_pairs={{0,1},{1,0},{2,3},{3,2},{4,5},{5,4},{6,7},{7,6},{8,9},{9,8},{10,11... | collective-permute-start | bytes 786440 | tf_op jit(solution)/shard_map/ppermute | solution.py:39
  60.9 3.0 %collective-permute-start.18 = (bf16[256,512]{1,0:T(8,128)(2,1)S(1)}, bf16[256,512]{1,0:T(8,128)(2,1)S(1)}, u32[]{:S(2)}, u32[]{:S(2)}) collective-permute-start(bf16[256,512]{1,0:T(8,128)(2,1)S(1)} %collective-permute-done.17.refs_0_.refs_10_), channel_id=1, source_target_pairs={{0,1},{1,0},{2,3},{3,2},{4,5},{5,4},{6,7},{7,6},{8,9},{9,8},{10,11... | collective-permute-start | bytes 786440 | tf_op jit(solution)/shard_map/ppermute | solution.py:39
  64.9 6.0 %collective-permute-start.19 = (bf16[4,128,128]{2,1,0:T(8,128)(2,1)S(1)}, bf16[4,128,128]{2,1,0:T(8,128)(2,1)S(1)}, u32[]{:S(2)}, u32[]{:S(2)}) collective-permute-start(bf16[4,128,128]{2,1,0:T(8,128)(2,1)S(1)} %get-tuple-element.36), channel_id=1, source_target_pairs={{0,4},{4,0},{8,12},{12,8},{16,20},{20,16},{24,28},{28,24},{1,5},{5... | collective-permute-start | bytes 393224 | tf_op jit(solution)/shard_map/ppermute | solution.py:39
  72.2 6.3 %collective-permute-start.20 = (bf16[4,128,128]{2,1,0:T(8,128)(2,1)}, bf16[4,128,128]{2,1,0:T(8,128)(2,1)}, u32[]{:S(2)}, u32[]{:S(2)}) collective-permute-start(bf16[4,128,128]{2,1,0:T(8,128)(2,1)} %fusion.2), channel_id=1, source_target_pairs={{0,8},{4,12},{8,16},{12,20},{16,24},{20,28},{1,9},{5,13},{9,17},{1... | collective-permute-start | bytes 393224 | tf_op jit(solution)/shard_map/ppermute | solution.py:34
  79.6 12.7 %collective-permute-start.21 = (bf16[4,128,128]{2,1,0:T(8,128)(2,1)S(1)}, bf16[4,128,128]{2,1,0:T(8,128)(2,1)S(1)}, u32[]{:S(2)}, u32[]{:S(2)}) collective-permute-start(bf16[4,128,128]{2,1,0:T(8,128)(2,1)S(1)} %fusion.1), channel_id=1, source_target_pairs={{0,16},{4,20},{8,24},{12,28},{1,17},{5,21},{9,25},{13,29},{2,18},{... | collective-permute-start | bytes 393224 | tf_op jit(solution)/shard_map/ppermute | solution.py:34
  87.4 2.8 %copy-start.7 = (bf16[2048,3,512]{2,0,1:T(8,128)(2,1)S(1)}, bf16[2048,3,512]{2,0,1:T(8,128)(2,1)}, u32[]{:S(2)}) copy-start(bf16[2048,3,512]{2,0,1:T(8,128)(2,1)} %param.17) | copy-start | bytes 18874372
  90.2 3.0 %copy-start.3 = (f32[4,128,128]{2,1,0:T(8,128)S(1)}, f32[4,128,128]{2,1,0:T(8,128)}, u32[]{:S(2)}) copy-start(f32[4,128,128]{2,1,0:T(8,128)} %state.1) | copy-start | bytes 786436
  90.2 3.1 %copy-start.4 = (f32[512]{0:T(512)S(1)}, f32[512]{0:T(512)}, u32[]{:S(2)}) copy-start(f32[512]{0:T(512)} %param.18) | copy-start | bytes 6148
  (4 other events, 5.4 us)

commit v4 on v3

--- a/solution.py
+++ b/solution.py
@@ -14,7 +14,7 @@
 EPS = 1e-06
 LOW = -1e30
 BLOCK = 128
-SPLIT = 2
+SHARES = (2, 2)
 VMEM = pl.BlockSpec(memory_space=pltpu.VMEM)
 HBM = pl.BlockSpec(memory_space=pltpu.HBM)
 F32 = jnp.float32
@@ -61,17 +61,20 @@
 def earlier_sum(value, axis):
     count = lax.axis_size(axis)
     place = lax.axis_index(axis)
-    partner = swapped(value, axis, 1)
-    total = value.astype(F32) + partner.astype(F32)
-    before = jnp.where(place % 2 == 1, partner.astype(F32), 0.0)
-    parts = [before]
-    step = 1
-    while 2 * step < count:
-        arrived = shifted(total.astype(BF16), axis, 2 * step).astype(F32)
-        parts.append(arrived)
-        total = total + arrived
-        step *= 2
-    return sum(parts)
+    total = value.astype(F32)
+    before = jnp.zeros_like(total)
+    bit = 1
+    while bit < count:
+        slim = total.astype(BF16)
+        if 2 * bit < count:
+            other = swapped(slim, axis, bit).astype(F32)
+        else:
+            ahead = [(source, source + bit) for source in range(count - bit)]
+            other = lax.ppermute(slim, axis, ahead).astype(F32)
+        before = before + jnp.where(place & bit != 0, other, 0.0)
+        total = total + other
+        bit *= 2
+    return before
 
 
 def fetch(tables, copies, semaphores):
@@ -148,21 +151,50 @@
     return dot(left, right)
 
 
-def attend_kernel(prior, heads, block, far_starts, far_lens, *refs):
+def mix(pieces, weights, size):
+    frame = jnp.concatenate([piece[...] for piece in pieces], axis=0)
+    inner = weights.shape[0] // 3
+    wide = frame.astype(F32)
+    scale = lax.rsqrt(jnp.mean(wide * wide, axis=-1, keepdims=True) + EPS)
+    full = dot_t(frame, weights[...])
+    return (
+        (full[:, :inner] * (scale * (size**-0.5 * math.log2(math.e)))).astype(BF16),
+        (full[:, inner : 2 * inner] * scale).astype(BF16),
+        (full[:, 2 * inner :] * scale).astype(BF16),
+    )
+
+
+def mix_kernel(size, *refs):
+    *pieces, weights, queries, keys, values = refs
+    queries[...], keys[...], values[...] = mix(pieces, weights, size)
+
+
+def mix_rows(pieces, weights, heads):
+    rows = pieces[0].shape[0] * len(pieces)
+    inner = weights.shape[0] // 3
+    return pl.pallas_call(
+        functools.partial(mix_kernel, inner // heads),
+        out_shape=(jax.ShapeDtypeStruct((rows, inner), BF16),) * 3,
+        in_specs=[VMEM] * (len(pieces) + 1),
+        out_specs=(VMEM,) * 3,
+        compiler_params=pltpu.CompilerParams(vmem_limit_bytes=10 * 2**20),
+        cost_estimate=pl.CostEstimate(flops=10**9, bytes_accessed=4 * 10**6, transcendentals=0),
+        name="prior_mix",
+    )(*pieces, weights)
+
+
+def attend_kernel(prior, count, heads, block, far_starts, far_lens, *refs):
     *refs, starts, lens, semaphores = refs
     moves = fetch((far_starts, far_lens), (starts, lens), semaphores)
     if prior:
-        *refs, held_context = refs
-    count = len(refs) - (6 if prior else 5)
-    pieces = refs[:count]
-    weights, *olds, result, queries, keys, values = refs[count:]
-    context = olds[0] if prior else result
-    rows, width = pieces[0].shape
+        *refs, old, result, queries, keys, values, context = refs
+        *pieces, weights, near_queries, near_keys, near_values = refs
+    else:
+        *pieces, weights, context, queries, keys, values = refs
+    rows, _ = pieces[0].shape
     span = rows * count
     inner = weights.shape[0] // 3
     size = inner // heads
-    if not prior:
-        context[...] = jnp.zeros_like(context)
     row = clip_rows(rows, count, span)
     lane = lax.broadcasted_iota(jnp.int32, (1, inner), 1)
     owner = [(lane >= head * size) & (lane < (head + 1) * size) for head in range(heads)]
@@ -170,22 +202,26 @@
     for head in range(heads):
         groups.setdefault(head * size // 128 * 128, []).append(head)
 
+    def fill(first_row):
+        queries[first_row:, :], keys[first_row:, :], values[first_row:, :] = mix(pieces, weights, size)
+
     if prior:
+        context[...] = old[...]
         for move in moves:
             move.wait()
         shift, length, first, last = clip_span(starts, lens, span, prior)
 
-    @pl.when(last > first if prior else True)
-    def _():
-        frame = jnp.concatenate([piece[...] for piece in pieces], axis=0)
-        wide = frame.astype(F32)
-        scale = lax.rsqrt(jnp.sum(wide * wide, axis=-1, keepdims=True) * (1.0 / width) + EPS)
-        full = dot_t(frame, weights[...])
-        queries[...] = (full[:, :inner] * (scale * (size**-0.5 * math.log2(math.e)))).astype(BF16)
-        keys[...] = (full[:, inner : 2 * inner] * scale).astype(BF16)
-        values[...] = (full[:, 2 * inner :] * scale).astype(BF16)
-
-    if not prior:
+        @pl.when(last > first)
+        def _():
+            held_rows = near_queries.shape[0]
+            queries[:held_rows, :] = near_queries[...]
+            keys[:held_rows, :] = near_keys[...]
+            values[:held_rows, :] = near_values[...]
+            fill(held_rows)
+
+    else:
+        context[...] = jnp.zeros_like(context)
+        fill(0)
         for move in moves:
             move.wait()
         shift, length, first, last = clip_span(starts, lens, span, prior)
@@ -222,29 +258,27 @@
             context[here, :] = total.astype(BF16)
         return 0
 
-    if prior:
-        held_context[...] = context[...]
-        context = held_context
     lax.fori_loop(first // block, jnp.where(last > first, (last + block - 1) // block, 0), step, 0)
     if prior:
         result[...] = pack(context[...])
 
 
-def attend(pieces, weights, starts, lens, heads, old=None):
+def attend(pieces, weights, starts, lens, heads, near_rows=(), old=()):
     rows, _ = pieces[0].shape
-    span = rows * len(pieces)
+    held_rows = near_rows[0].shape[0] if near_rows else 0
+    span = rows * len(pieces) + held_rows
     inner = weights.shape[0] // 3
-    olds = [] if old is None else [old]
-    return pl.pallas_call(
-        functools.partial(attend_kernel, old is not None, heads, min(BLOCK, span)),
-        out_shape=jax.ShapeDtypeStruct(packed_shape(span, inner) if olds else (span, inner), BF16),
-        in_specs=[HBM, HBM] + [VMEM] * (len(pieces) + 1 + len(olds)),
+    extra = [*near_rows, *old]
+    return pl.pallas_call(
+        functools.partial(attend_kernel, len(old) > 0, span // rows, heads, min(BLOCK, span)),
+        out_shape=jax.ShapeDtypeStruct(packed_shape(span, inner) if old else (span, inner), BF16),
+        in_specs=[HBM, HBM] + [VMEM] * (len(pieces) + 1 + len(extra)),
         out_specs=VMEM,
-        scratch_shapes=[pltpu.VMEM((span, inner), BF16)] * (3 + len(olds)) + table_scratch(starts, lens),
+        scratch_shapes=[pltpu.VMEM((span, inner), BF16)] * (3 + len(old)) + table_scratch(starts, lens),
         compiler_params=pltpu.CompilerParams(vmem_limit_bytes=16 * 2**20),
         cost_estimate=pl.CostEstimate(flops=5 * 10**9, bytes_accessed=4 * 10**6, transcendentals=10**6),
-        name="attend_prior" if olds else "attend_own",
-    )(starts, lens, *pieces, weights, *olds)
+        name="attend_prior" if old else "attend_own",
+    )(starts, lens, *pieces, weights, *extra)
 
 
 def warm_kernel(source, target):
@@ -327,11 +361,10 @@
     result[...] = jnp.where(live, visual, text[here, :])
 
 
-def project(index, count, base, parts, outs, projector, text, starts, lens):
+def project(low, rows, base, parts, outs, projector, text, starts, lens):
     span, columns = text.shape
-    rows = span // count
-    return pl.pallas_call(
-        functools.partial(project_kernel, index * rows, span),
+    return pl.pallas_call(
+        functools.partial(project_kernel, low, span),
         out_shape=jax.ShapeDtypeStruct((rows, columns), BF16),
         in_specs=[HBM, HBM] + [VMEM] * (3 + 2 * len(parts)),
         out_specs=VMEM,
@@ -434,7 +467,7 @@
         at += size
     query_sums, scales, key_ins, value_ins, pieces = lists
     query_out, intra, buffers, semaphores = refs[at:]
-    rows, depth = pieces[0].shape
+    depth = pieces[0].shape[1]
     starts = [pl.multiple_of((lax.axis_index("head") ^ key) * depth, depth) for key in keys]
     moves = fetch(
         [weights.at[0, pl.ds(start, depth), :] for start in starts],
@@ -443,11 +476,14 @@
     )
     for move in moves:
         move.wait()
-    causal = lax.broadcasted_iota(jnp.int32, (rows, rows), 0) >= lax.broadcasted_iota(
-        jnp.int32, (rows, rows), 1
-    )
+    low = 0
     for group in range(groups):
-        here = slice(group * rows, (group + 1) * rows)
+        rows = query_sums[group].shape[0]
+        here = slice(low, low + rows)
+        low += rows
+        causal = lax.broadcasted_iota(jnp.int32, (rows, rows), 0) >= lax.broadcasted_iota(
+            jnp.int32, (rows, rows), 1
+        )
         total = query_sums[group][...]
         for index in range(count):
             total = total + dot(pieces[group * count + index][...], buffers[index])
@@ -465,14 +501,15 @@
 
 
 def within(pieces, keys, weights, query_sums, scales, key_ins, value_ins):
-    rows, depth = pieces[0].shape
+    depth = pieces[0].shape[1]
     groups = len(query_sums)
     columns = weights.shape[2]
+    span = sum(query_sum.shape[0] for query_sum in query_sums)
     return pl.pallas_call(
         functools.partial(within_kernel, keys, groups),
         out_shape=(
-            jax.ShapeDtypeStruct((groups * rows, columns), BF16),
-            jax.ShapeDtypeStruct((groups * rows, columns), F32),
+            jax.ShapeDtypeStruct((span, columns), BF16),
+            jax.ShapeDtypeStruct((span, columns), F32),
         ),
         in_specs=[HBM] + [VMEM] * (4 * groups + len(pieces)),
         out_specs=(VMEM,) * 2,
@@ -528,19 +565,21 @@
     layer = jnp.transpose(layer_qkv, (1, 0, 2))
     vision = warm(vision)
     context = attend(own, vision, clip_start, clip_len, heads)
-    context = attend(prior, vision, clip_start, clip_len, heads, context)
+    half = groups // 2
+    near_rows = mix_rows(prior[:half], vision, heads)
+    context = attend(prior[half:], vision, clip_start, clip_len, heads, near_rows, [context])
     parts = spread(context)
-    half = groups // 2
     near_keys, far_keys = tuple(range(half)), tuple(range(half, groups))
     base = arrange(own, prior, parts[:half], outs[:half], clip_start, clip_len)
     query_sums, scales, key_rows, value_rows, pieces, old = [], [], [], [], [], []
-    for index in range(SPLIT):
-        sequence = project(
-            index, SPLIT, base, parts[half:], outs[half:], projector, text_rows, clip_start, clip_len
-        )
+    low = 0
+    for index, share in enumerate(SHARES):
+        rows = text_rows.shape[0] // share
+        sequence = project(low, rows, base, parts[half:], outs[half:], projector, text_rows, clip_start, clip_len)
+        low += rows
         blocks = spread(sequence)
         query_sum, pair_sum, squares = near(blocks[:half], near_keys, layer)
-        kind = BF16 if index == SPLIT - 1 else F32
+        kind = BF16 if index == len(SHARES) - 1 else F32
         key_row, value_row, delta, scale = pair(kind, blocks[half:], far_keys, layer, pair_sum, squares, old)
         old = [delta]
         query_sums.append(query_sum)

time: 94.9 us -> 93.3 us (0.983)
  starting transfers between devices: 30.3 us -> 27.3 us
  waiting for transfers between devices: 37.3 us -> 38.7 us
  Pallas kernels: 18 us -> 19 us
    ppermute x4 -> x2, starting transfers between devices: 19.1 us -> 7.11 us  [shifted(): lax.ppermute(value, axis, [(source, source + steps) for source in range(c...]
    ppermute x0 -> x1, starting transfers between devices: none -> 6.44 us  [earlier_sum(): other = lax.ppermute(slim, axis, ahead).astype(F32)]
    ppermute x18 -> x19, waiting for transfers between devices: 34.5 us -> 37.2 us  [swapped(): lax.ppermute(value, axis, [(source, source ^ bit) for source in range(cou...]
    ppermute x18 -> x19, starting transfers between devices: 11.2 us -> 13.7 us  [swapped(): lax.ppermute(value, axis, [(source, source ^ bit) for source in range(cou...]
    ppermute x4 -> x2, waiting for transfers between devices: 2.8 us -> 1.48 us  [shifted(): lax.ppermute(value, axis, [(source, source + steps) for source in range(c...]
    pallas_call x4 -> x5, Pallas kernels: 7.53 us -> 8.51 us  [the longest x2 4.59 us: attend(): pl.pallas_call(functools.partial(attend_kernel, len(old) > 0, span // row...]
  transfers between devices with their start and end apart: 22 -> 22, of which waited for: 8 -> 8; matrix products, arithmetic and copies ran while one was open for 0% -> 0% of each run, Pallas kernels for 15% -> 16%
where the time goes in v4:
time: 93.3 us; the launch traced here: 93.1 us
  waiting for transfers between devices  38.7 us (41%)
  starting transfers between devices  27.3 us (29%)
  Pallas kernels  19 us (20%)
  local copies, waits for them, and re-layouts  5.05 us (5%)
  other arithmetic  2.69 us (3%)
    ppermute x19, waiting for transfers between devices, swapped(): lax.ppermute(value, axis, [(source, source ^ bit) for source in range(cou...  37.2 us
    ppermute x19, starting transfers between devices, swapped(): lax.ppermute(value, axis, [(source, source ^ bit) for source in range(cou...  13.7 us
    ppermute x2, starting transfers between devices, shifted(): lax.ppermute(value, axis, [(source, source + steps) for source in range(c...  7.11 us
    ppermute x1, starting transfers between devices, earlier_sum(): other = lax.ppermute(slim, axis, ahead).astype(F32)  6.44 us
    unnamed x28, local copies, waits for them, and re-layouts  5.05 us
    pallas_call x2, Pallas kernels, attend(): pl.pallas_call(functools.partial(attend_kernel, len(old) > 0, span // row...  4.59 us
    pallas_call x1, Pallas kernels, arrange(): pl.pallas_call(arrange_kernel, out_shape=jax.ShapeDtypeStruct((span, widt...  3.09 us
    pallas_call x2, Pallas kernels, project(): pl.pallas_call(functools.partial(project_kernel, low, span), out_shape=ja...  2.9 us
  transfers between devices with their start and end apart: 22, of which 8 were waited for; matrix products, arithmetic and copies ran while one was open for 0% of the time, Pallas kernels for 16%

profile of v4, /device:TPU:0, one launch (start us, length us, event | category | flops | bytes accessed | tf_op | source)
XLA Modules:
  0.0 93.1 jit_solution(13417426151509521032)
XLA Ops:
  0.0 3.0 %collective-permute-start = (bf16[128,1152]{1,0:T(8,128)(2,1)}, bf16[128,1152]{1,0:T(8,128)(2,1)S(1)}, u32[]{:S(2)}, u32[]{:S(2)}) collective-permute-start(bf16[128,1152]{1,0:T(8,128)(2,1)} %refs_4_.1), channel_id=1, source_target_pairs={{0,2},{1,3},{2,0},{3,1},{4,6},{5,7},{6,4},{7,5},{8,10},{9,11},{10,... | collective-permute-start | bytes 884744 | tf_op jit(solution)/shard_map/ppermute | solution.py:39
  3.0 3.4 %collective-permute-start.3 = (bf16[128,1152]{1,0:T(8,128)(2,1)}, bf16[128,1152]{1,0:T(8,128)(2,1)S(1)}, u32[]{:S(2)}, u32[]{:S(2)}) collective-permute-start(bf16[128,1152]{1,0:T(8,128)(2,1)} %refs_4_.1), channel_id=1, source_target_pairs={{0,4},{4,8},{8,12},{12,16},{16,20},{20,24},{24,28},{1,5},{5,9},{9,... | collective-permute-start | bytes 884744 | tf_op jit(solution)/shard_map/ppermute | solution.py:34
  6.4 3.8 %collective-permute-done.refs_2_.refs_6_ = bf16[128,1152]{1,0:T(8,128)(2,1)S(1)} collective-permute-done((bf16[128,1152]{1,0:T(8,128)(2,1)}, bf16[128,1152]{1,0:T(8,128)(2,1)S(1)}, u32[]{:S(2)}, u32[]{:S(2)}) %collective-permute-start) | collective-permute-done | bytes 294944 | tf_op jit(solution)/shard_map/ppermute | solution.py:39
  10.2 3.7 %collective-permute-start.1 = (bf16[128,1152]{1,0:T(8,128)(2,1)S(1)}, bf16[128,1152]{1,0:T(8,128)(2,1)S(1)}, u32[]{:S(2)}, u32[]{:S(2)}) collective-permute-start(bf16[128,1152]{1,0:T(8,128)(2,1)S(1)} %collective-permute-done.refs_2_.refs_6_), channel_id=1, source_target_pairs={{0,4},{4,8},{8,12},{12,16},{16,20},{20,24},{24,28},{1,5},{5,9},{9,... | collective-permute-start | bytes 884744 | tf_op jit(solution)/shard_map/ppermute | solution.py:34
  14.5 1.5 %collective-permute-start.11 = (bf16[288,1152]{1,0:T(8,128)(2,1)}, bf16[288,1152]{1,0:T(8,128)(2,1)S(1)}, u32[]{:S(2)}, u32[]{:S(2)}) collective-permute-start(bf16[288,1152]{1,0:T(8,128)(2,1)} %refs_2_.3), channel_id=1, source_target_pairs={{0,2},{1,3},{2,0},{3,1},{4,6},{5,7},{6,4},{7,5},{8,10},{9,11},{10,... | collective-permute-start | bytes 1990664 | tf_op jit(solution)/shard_map/ppermute | solution.py:39
  16.0 1.6 %copy-done.2 = bf16[1152,3,288]{0,2,1:T(8,128)(2,1)S(1)} copy-done((bf16[1152,3,288]{0,2,1:T(8,128)(2,1)S(1)}, bf16[1152,3,288]{0,2,1:T(8,128)(2,1)}, u32[]{:S(2)}) %copy-start.2) | copy-done | bytes 1990680
  17.8 1.5 %collective-permute-done.1.refs_0_.refs_10_ = bf16[128,1152]{1,0:T(8,128)(2,1)S(1)} collective-permute-done((bf16[128,1152]{1,0:T(8,128)(2,1)S(1)}, bf16[128,1152]{1,0:T(8,128)(2,1)S(1)}, u32[]{:S(2)}, u32[]{:S(2)}) %collective-permute-start.1) | collective-permute-done | bytes 294944 | tf_op jit(solution)/shard_map/ppermute | solution.py:34
  19.8 1.0 %prior_mix.1 = (bf16[256,288]{1,0:T(8,128)(2,1)S(1)}, bf16[256,288]{1,0:T(8,128)(2,1)S(1)}, bf16[256,288]{1,0:T(8,128)(2,1)S(1)}) custom-call(bf16[128,1152]{1,0:T(8,128)(2,1)S(1)} %collective-permute-done.3.refs_0_.refs_8_, bf16[128,1152]{1,0:T(8,128)(2,1)S(1)} %collective-permute-done.4.refs_1_.refs_9_, bf16[864,1152]{1,0:T(8,128)(2,1)S(1)} %warm.1.refs_2_.refs_4_), custom_call_target="tpu_custom_call" | custom-call | flops 1000000000 | bytes 4000000 | tf_op jit(solution)/shard_map/prior_mix/pallas_call | solution.py:175
  20.8 3.7 %attend_own.1.refs_6_ = bf16[512,288]{1,0:T(8,128)(2,1)S(1)} custom-call(s32[8]{0:T(128)S(1)} %copy-done.5, s32[8]{0:T(128)S(1)} %copy-done.6, bf16[128,1152]{1,0:T(8,128)(2,1)S(1)} %copy-done.9, bf16[128,1152]{1,0:T(8,128)(2,1)S(1)} %collective-permute-done.5.refs_1_.refs_5_, bf16[128,1152]{1,0:T(8,128)(2,1)S(1)} %collective-permute-done.refs_2_.refs_6_, ...), custom_call_target="tpu_custom_call" | custom-call | flops 5000000000 | bytes 4000000 | tf_op jit(solution)/shard_map/attend_own/pallas_call | solution.py:272
  24.6 7.4 %collective-permute-done.11.refs_5_ = bf16[288,1152]{1,0:T(8,128)(2,1)S(1)} collective-permute-done((bf16[288,1152]{1,0:T(8,128)(2,1)}, bf16[288,1152]{1,0:T(8,128)(2,1)S(1)}, u32[]{:S(2)}, u32[]{:S(2)}) %collective-permute-start.11) | collective-permute-done | bytes 663584 | tf_op jit(solution)/shard_map/ppermute | solution.py:39
  32.9 1.6 %collective-permute-start.9 = (bf16[576,256]{1,0:T(8,128)(2,1)S(1)}, bf16[576,256]{1,0:T(8,128)(2,1)S(1)}, u32[]{:S(2)}, u32[]{:S(2)}) collective-permute-start(bf16[576,256]{1,0:T(8,128)(2,1)S(1)} %attend_prior.1.refs_0_), channel_id=1, source_target_pairs={{0,2},{1,3},{2,0},{3,1},{4,6},{5,7},{6,4},{7,5},{8,10},{9,11},{10,... | collective-permute-start | bytes 884744 | tf_op jit(solution)/shard_map/ppermute | solution.py:39
  34.7 7.7 %collective-permute-done.9.refs_3_ = bf16[576,256]{1,0:T(8,128)(2,1)S(1)} collective-permute-done((bf16[576,256]{1,0:T(8,128)(2,1)S(1)}, bf16[576,256]{1,0:T(8,128)(2,1)S(1)}, u32[]{:S(2)}, u32[]{:S(2)}) %collective-permute-start.9) | collective-permute-done | bytes 294944 | tf_op jit(solution)/shard_map/ppermute | solution.py:39
  42.4 3.1 %arrange.1.refs_0_ = f32[512,1152]{1,0:T(8,128)S(1)} custom-call(s32[8]{0:T(128)S(1)} %copy-done.5, s32[8]{0:T(128)S(1)} %copy-done.6, bf16[576,256]{1,0:T(8,128)(2,1)S(1)} %attend_prior.1.refs_0_, bf16[576,256]{1,0:T(8,128)(2,1)S(1)} %collective-permute-done.7.refs_1_, bf16[288,1152]{1,0:T(8,128)(2,1)S(1)} %copy-done.8, ...), custom_call_target="tpu_custom_call" | custom-call | flops 2000000000 | bytes 3000000 | tf_op jit(solution)/shard_map/arrange/pallas_call | solution.py:324
  45.6 1.4 %shard_map.100.refs_0_ = bf16[256,512]{1,0:T(8,128)(2,1)S(1)} custom-call(s32[8]{0:T(128)S(1)} %copy-done.5, s32[8]{0:T(128)S(1)} %copy-done.6, f32[512,1152]{1,0:T(8,128)S(1)} %arrange.1.refs_0_, bf16[1152,512]{1,0:T(8,128)(2,1)S(1)} %copy-done, bf16[512,512]{1,0:T(8,128)(2,1)S(1)} %copy-done.1, bf16[576,256]{1,0:T(8,128)(2,1)S(1)} %collective-permute-done.9.refs_3_, ...), custom_call_target="tpu_custom_call" | custom-call | flops 1000000000 | bytes 2000000 | tf_op jit(solution)/shard_map/pallas_call | solution.py:366
  47.0 1.6 %collective-permute-start.15 = (bf16[256,512]{1,0:T(8,128)(2,1)S(1)}, bf16[256,512]{1,0:T(8,128)(2,1)S(1)}, u32[]{:S(2)}, u32[]{:S(2)}) collective-permute-start(bf16[256,512]{1,0:T(8,128)(2,1)S(1)} %shard_map.100.refs_0_), channel_id=1, source_target_pairs={{0,2},{1,3},{2,0},{3,1},{4,6},{5,7},{6,4},{7,5},{8,10},{9,11},{10,... | collective-permute-start | bytes 786440 | tf_op jit(solution)/shard_map/ppermute | solution.py:39
  48.6 1.4 %shard_map.102.refs_0_ = bf16[256,512]{1,0:T(8,128)(2,1)S(1)} custom-call(s32[8]{0:T(128)S(1)} %copy-done.5, s32[8]{0:T(128)S(1)} %copy-done.6, f32[512,1152]{1,0:T(8,128)S(1)} %arrange.1.refs_0_, bf16[1152,512]{1,0:T(8,128)(2,1)S(1)} %copy-done, bf16[512,512]{1,0:T(8,128)(2,1)S(1)} %copy-done.1, bf16[576,256]{1,0:T(8,128)(2,1)S(1)} %collective-permute-done.9.refs_3_, ...), custom_call_target="tpu_custom_call" | custom-call | flops 1000000000 | bytes 2000000 | tf_op jit(solution)/shard_map/pallas_call | solution.py:366
  51.2 5.1 %collective-permute-done.15.refs_0_.refs_8_ = bf16[256,512]{1,0:T(8,128)(2,1)S(1)} collective-permute-done((bf16[256,512]{1,0:T(8,128)(2,1)S(1)}, bf16[256,512]{1,0:T(8,128)(2,1)S(1)}, u32[]{:S(2)}, u32[]{:S(2)}) %collective-permute-start.15) | collective-permute-done | bytes 262176 | tf_op jit(solution)/shard_map/ppermute | solution.py:39
  56.3 5.1 %collective-permute-done.17.refs_0_.refs_10_ = bf16[256,512]{1,0:T(8,128)(2,1)S(1)} collective-permute-done((bf16[256,512]{1,0:T(8,128)(2,1)S(1)}, bf16[256,512]{1,0:T(8,128)(2,1)S(1)}, u32[]{:S(2)}, u32[]{:S(2)}) %collective-permute-start.17) | collective-permute-done | bytes 262176 | tf_op jit(solution)/shard_map/ppermute | solution.py:39
  61.5 1.0 %shard_map.101 = (f32[256,512]{1,0:T(8,128)S(1)}, f32[2,256,512]{2,1,0:T(8,128)S(1)}, f32[256,128]{1,0:T(8,128)S(1)}) custom-call(bf16[3,2048,512]{2,1,0:T(8,128)(2,1)S(1)} %bitcast.9, bf16[256,512]{1,0:T(8,128)(2,1)S(1)} %shard_map.100.refs_0_, bf16[256,512]{1,0:T(8,128)(2,1)S(1)} %collective-permute-done.13.refs_1_), custom_call_target="tpu_custom_call" | custom-call | flops 3000000000 | bytes 7000000 | tf_op jit(solution)/shard_map/pallas_call | solution.py:404
  62.5 1.0 %shard_map.103 = (f32[256,512]{1,0:T(8,128)S(1)}, f32[2,256,512]{2,1,0:T(8,128)S(1)}, f32[256,128]{1,0:T(8,128)S(1)}) custom-call(bf16[3,2048,512]{2,1,0:T(8,128)(2,1)S(1)} %bitcast.10, bf16[256,512]{1,0:T(8,128)(2,1)S(1)} %shard_map.102.refs_0_, bf16[256,512]{1,0:T(8,128)(2,1)S(1)} %collective-permute-done.14.refs_1_), custom_call_target="tpu_custom_call" | custom-call | flops 3000000000 | bytes 7000000 | tf_op jit(solution)/shard_map/pallas_call | solution.py:404
  63.5 1.0 %shard_map.104 = (bf16[256,512]{1,0:T(8,128)(2,1)S(1)}, bf16[256,512]{1,0:T(8,128)(2,1)S(1)}, f32[4,128,128]{2,1,0:T(8,128)S(1)}, f32[256,128]{1,0:T(8,128)S(1)}) custom-call(bf16[3,2048,512]{2,1,0:T(8,128)(2,1)S(1)} %bitcast.11, f32[2,256,512]{2,1,0:T(8,128)S(1)} %get-tuple-element.29.pair_sum, f32[256,128]{1,0:T(8,128)S(1)} %get-tuple-element.30.squares, ...), custom_call_target="tpu_custom_call" | custom-call | flops 3000000000 | bytes 7000000 | tf_op jit(solution)/shard_map/pallas_call | solution.py:446
  64.4 1.0 %shard_map.105 = (bf16[256,512]{1,0:T(8,128)(2,1)S(1)}, bf16[256,512]{1,0:T(8,128)(2,1)S(1)}, bf16[4,128,128]{2,1,0:T(8,128)(2,1)S(1)}, f32[256,128]{1,0:T(8,128)S(1)}) custom-call(bf16[3,2048,512]{2,1,0:T(8,128)(2,1)S(1)} %bitcast.12, f32[2,256,512]{2,1,0:T(8,128)S(1)} %get-tuple-element.32.pair_sum, f32[256,128]{1,0:T(8,128)S(1)} %get-tuple-element.33.squares, ...), custom_call_target="tpu_custom_call" | custom-call | flops 3000000000 | bytes 7000000 | tf_op jit(solution)/shard_map/pallas_call | solution.py:446
  65.4 1.6 %collective-permute-start.19 = (bf16[4,128,128]{2,1,0:T(8,128)(2,1)S(1)}, bf16[4,128,128]{2,1,0:T(8,128)(2,1)S(1)}, u32[]{:S(2)}, u32[]{:S(2)}) collective-permute-start(bf16[4,128,128]{2,1,0:T(8,128)(2,1)S(1)} %get-tuple-element.42), channel_id=1, source_target_pairs={{0,4},{4,0},{8,12},{12,8},{16,20},{20,16},{24,28},{28,24},{1,5},{5... | collective-permute-start | bytes 393224 | tf_op jit(solution)/shard_map/ppermute | solution.py:39
  67.0 4.4 %collective-permute-done.19 = bf16[4,128,128]{2,1,0:T(8,128)(2,1)S(1)} collective-permute-done((bf16[4,128,128]{2,1,0:T(8,128)(2,1)S(1)}, bf16[4,128,128]{2,1,0:T(8,128)(2,1)S(1)}, u32[]{:S(2)}, u32[]{:S(2)}) %collective-permute-start.19) | collective-permute-done | bytes 131104 | tf_op jit(solution)/shard_map/ppermute | solution.py:39
  72.7 2.1 %collective-permute-start.20 = (bf16[4,128,128]{2,1,0:T(8,128)(2,1)}, bf16[4,128,128]{2,1,0:T(8,128)(2,1)}, u32[]{:S(2)}, u32[]{:S(2)}) collective-permute-start(bf16[4,128,128]{2,1,0:T(8,128)(2,1)} %fusion.3), channel_id=1, source_target_pairs={{0,8},{4,12},{8,0},{12,4},{16,24},{20,28},{24,16},{28,20},{1,9},{5... | collective-permute-start | bytes 393224 | tf_op jit(solution)/shard_map/ppermute | solution.py:39
  74.8 3.6 %collective-permute-done.20 = bf16[4,128,128]{2,1,0:T(8,128)(2,1)} collective-permute-done((bf16[4,128,128]{2,1,0:T(8,128)(2,1)}, bf16[4,128,128]{2,1,0:T(8,128)(2,1)}, u32[]{:S(2)}, u32[]{:S(2)}) %collective-permute-start.20) | collective-permute-done | bytes 131104 | tf_op jit(solution)/shard_map/ppermute | solution.py:39
  78.4 1.0 %fusion.2 = bf16[4,128,128]{2,1,0:T(8,128)(2,1)S(1)} fusion(bf16[4,128,128]{2,1,0:T(8,128)(2,1)} %collective-permute-done.20, bf16[4,128,128]{2,1,0:T(8,128)(2,1)} %copy-done.10, bf16[4,128,128]{2,1,0:T(8,128)(2,1)S(1)} %get-tuple-element.42), kind=kLoop, calls=%fused_computation.6 | loop fusion | flops 393216 | bytes 524288 | tf_op jit(solution)/shard_map/convert_element_type | solution.py:68
  79.4 6.4 %collective-permute-start.21 = (bf16[4,128,128]{2,1,0:T(8,128)(2,1)S(1)}, bf16[4,128,128]{2,1,0:T(8,128)(2,1)S(1)}, u32[]{:S(2)}, u32[]{:S(2)}) collective-permute-start(bf16[4,128,128]{2,1,0:T(8,128)(2,1)S(1)} %fusion.2), channel_id=1, source_target_pairs={{0,16},{4,20},{8,24},{12,28},{1,17},{5,21},{9,25},{13,29},{2,18},{... | collective-permute-start | bytes 393224 | tf_op jit(solution)/shard_map/ppermute | solution.py:73
  85.9 2.8 %copy-done.7 = bf16[2048,3,512]{2,0,1:T(8,128)(2,1)S(1)} copy-done((bf16[2048,3,512]{2,0,1:T(8,128)(2,1)S(1)}, bf16[2048,3,512]{2,0,1:T(8,128)(2,1)}, u32[]{:S(2)}) %copy-start.7) | copy-done | bytes 6291480
  88.7 2.0 %within.1 = (bf16[512,512]{1,0:T(8,128)(2,1)S(1)}, f32[512,512]{1,0:T(8,128)S(1)}) custom-call(bf16[3,2048,512]{2,1,0:T(8,128)(2,1)S(1)} %bitcast.13, f32[256,512]{1,0:T(8,128)S(1)} %get-tuple-element.27.refs_0_, f32[256,512]{1,0:T(8,128)S(1)} %get-tuple-element.28.refs_1_, f32[256,128]{1,0:T(8,128)S(1)} %get-tuple-element.31.refs_2_, ...), custom_call_target="tpu_custom_call" | custom-call | flops 3000000000 | bytes 5000000 | tf_op jit(solution)/shard_map/within/pallas_call | solution.py:508
  90.7 1.0 %fusion.1.carried = f32[4,128,128]{2,1,0:T(8,128)S(1)} fusion(bf16[4,128,128]{2,1,0:T(8,128)(2,1)S(1)} %copy-done.11, bf16[4,128,128]{2,1,0:T(8,128)(2,1)} %collective-permute-done.20, bf16[4,128,128]{2,1,0:T(8,128)(2,1)S(1)} %collective-permute-done.21, pred[]{:T(512)S(6)} %ne.11, pred[]{:T(512)S(6)} %ne.10, pred[]{:T(512)S(6)} %ne.9), kind=kLoop, calls=%fused_computation.5 | loop fusion | flops 524288 | bytes 655363 | tf_op jit(solution)/shard_map/add | solution.py:74
  91.7 1.3 %finish.1 = bf16[512,512]{1,0:T(8,128)(2,1)} custom-call(bf16[512,512]{1,0:T(8,128)(2,1)S(1)} %get-tuple-element.40.query, f32[512,512]{1,0:T(8,128)S(1)} %get-tuple-element.41.intra, f32[4,128,128]{2,1,0:T(8,128)S(1)} %fusion.1.carried, f32[4,128,128]{2,1,0:T(8,128)S(1)} %copy-done.3, f32[1,512]{1,0:T(1,128)S(1)} %bitcast.6), custom_call_target="tpu_custom_call" | custom-call | flops 100000000 | bytes 3000000 | tf_op jit(solution)/shard_map/finish/pallas_call | solution.py:536
  (57 shorter events, 5.0 us)
Async XLA Ops:
  0.0 10.2 %collective-permute-start = (bf16[128,1152]{1,0:T(8,128)(2,1)}, bf16[128,1152]{1,0:T(8,128)(2,1)S(1)}, u32[]{:S(2)}, u32[]{:S(2)}) collective-permute-start(bf16[128,1152]{1,0:T(8,128)(2,1)} %refs_4_.1), channel_id=1, source_target_pairs={{0,2},{1,3},{2,0},{3,1},{4,6},{5,7},{6,4},{7,5},{8,10},{9,11},{10,... | collective-permute-start | bytes 884744 | tf_op jit(solution)/shard_map/ppermute | solution.py:39
  3.0 10.9 %collective-permute-start.3 = (bf16[128,1152]{1,0:T(8,128)(2,1)}, bf16[128,1152]{1,0:T(8,128)(2,1)S(1)}, u32[]{:S(2)}, u32[]{:S(2)}) collective-permute-start(bf16[128,1152]{1,0:T(8,128)(2,1)} %refs_4_.1), channel_id=1, source_target_pairs={{0,4},{4,8},{8,12},{12,16},{16,20},{20,24},{24,28},{1,5},{5,9},{9,... | collective-permute-start | bytes 884744 | tf_op jit(solution)/shard_map/ppermute | solution.py:34
  10.2 9.1 %collective-permute-start.1 = (bf16[128,1152]{1,0:T(8,128)(2,1)S(1)}, bf16[128,1152]{1,0:T(8,128)(2,1)S(1)}, u32[]{:S(2)}, u32[]{:S(2)}) collective-permute-start(bf16[128,1152]{1,0:T(8,128)(2,1)S(1)} %collective-permute-done.refs_2_.refs_6_), channel_id=1, source_target_pairs={{0,4},{4,8},{8,12},{12,16},{16,20},{20,24},{24,28},{1,5},{5,9},{9,... | collective-permute-start | bytes 884744 | tf_op jit(solution)/shard_map/ppermute | solution.py:34
  13.9 5.4 %collective-permute-start.4 = (bf16[128,1152]{1,0:T(8,128)(2,1)S(1)}, bf16[128,1152]{1,0:T(8,128)(2,1)S(1)}, u32[]{:S(2)}, u32[]{:S(2)}) collective-permute-start(bf16[128,1152]{1,0:T(8,128)(2,1)S(1)} %collective-permute-done.3.refs_0_.refs_8_), channel_id=1, source_target_pairs={{0,1},{1,0},{2,3},{3,2},{4,5},{5,4},{6,7},{7,6},{8,9},{9,8},{10,11... | collective-permute-start | bytes 884744 | tf_op jit(solution)/shard_map/ppermute | solution.py:39
  14.0 6.8 %collective-permute-start.5 = (bf16[128,1152]{1,0:T(8,128)(2,1)}, bf16[128,1152]{1,0:T(8,128)(2,1)S(1)}, u32[]{:S(2)}, u32[]{:S(2)}) collective-permute-start(bf16[128,1152]{1,0:T(8,128)(2,1)} %refs_4_.1), channel_id=1, source_target_pairs={{0,1},{1,0},{2,3},{3,2},{4,5},{5,4},{6,7},{7,6},{8,9},{9,8},{10,11... | collective-permute-start | bytes 884744 | tf_op jit(solution)/shard_map/ppermute | solution.py:39
  14.5 6.3 %collective-permute-start.6 = (bf16[128,1152]{1,0:T(8,128)(2,1)S(1)}, bf16[128,1152]{1,0:T(8,128)(2,1)S(1)}, u32[]{:S(2)}, u32[]{:S(2)}) collective-permute-start(bf16[128,1152]{1,0:T(8,128)(2,1)S(1)} %collective-permute-done.refs_2_.refs_6_), channel_id=1, source_target_pairs={{0,1},{1,0},{2,3},{3,2},{4,5},{5,4},{6,7},{7,6},{8,9},{9,8},{10,11... | collective-permute-start | bytes 884744 | tf_op jit(solution)/shard_map/ppermute | solution.py:39
  14.5 17.5 %collective-permute-start.11 = (bf16[288,1152]{1,0:T(8,128)(2,1)}, bf16[288,1152]{1,0:T(8,128)(2,1)S(1)}, u32[]{:S(2)}, u32[]{:S(2)}) collective-permute-start(bf16[288,1152]{1,0:T(8,128)(2,1)} %refs_2_.3), channel_id=1, source_target_pairs={{0,2},{1,3},{2,0},{3,1},{4,6},{5,7},{6,4},{7,5},{8,10},{9,11},{10,... | collective-permute-start | bytes 1990664 | tf_op jit(solution)/shard_map/ppermute | solution.py:39
  17.7 3.1 %copy-start.5 = (s32[8]{0:T(128)S(1)}, s32[8]{0:T(128)}, u32[]{:S(2)}) copy-start(s32[8]{0:T(128)} %far_starts.9) | copy-start | bytes 100
  17.7 3.1 %copy-start.6 = (s32[8]{0:T(128)S(1)}, s32[8]{0:T(128)}, u32[]{:S(2)}) copy-start(s32[8]{0:T(128)} %far_lens.9) | copy-start | bytes 100
  17.8 3.1 %copy-start.9 = (bf16[128,1152]{1,0:T(8,128)(2,1)S(1)}, bf16[128,1152]{1,0:T(8,128)(2,1)}, u32[]{:S(2)}) copy-start(bf16[128,1152]{1,0:T(8,128)(2,1)} %refs_4_.1) | copy-start | bytes 884740
  19.3 23.1 %collective-permute-start.8 = (bf16[288,1152]{1,0:T(8,128)(2,1)S(1)}, bf16[288,1152]{1,0:T(8,128)(2,1)S(1)}, u32[]{:S(2)}, u32[]{:S(2)}) collective-permute-start(bf16[288,1152]{1,0:T(8,128)(2,1)S(1)} %copy-done.8), channel_id=1, source_target_pairs={{0,1},{1,0},{2,3},{3,2},{4,5},{5,4},{6,7},{7,6},{8,9},{9,8},{10,11... | collective-permute-start | bytes 1990664 | tf_op jit(solution)/shard_map/ppermute | solution.py:39
  19.3 12.7 %collective-permute-start.2 = (bf16[128,1152]{1,0:T(8,128)(2,1)S(1)}, bf16[128,1152]{1,0:T(8,128)(2,1)S(1)}, u32[]{:S(2)}, u32[]{:S(2)}) collective-permute-start(bf16[128,1152]{1,0:T(8,128)(2,1)S(1)} %collective-permute-done.1.refs_0_.refs_10_), channel_id=1, source_target_pairs={{0,1},{1,0},{2,3},{3,2},{4,5},{5,4},{6,7},{7,6},{8,9},{9,8},{10,11... | collective-permute-start | bytes 884744 | tf_op jit(solution)/shard_map/ppermute | solution.py:39
  32.0 13.5 %collective-permute-start.12 = (bf16[288,1152]{1,0:T(8,128)(2,1)S(1)}, bf16[288,1152]{1,0:T(8,128)(2,1)S(1)}, u32[]{:S(2)}, u32[]{:S(2)}) collective-permute-start(bf16[288,1152]{1,0:T(8,128)(2,1)S(1)} %collective-permute-done.11.refs_5_), channel_id=1, source_target_pairs={{0,1},{1,0},{2,3},{3,2},{4,5},{5,4},{6,7},{7,6},{8,9},{9,8},{10,11... | collective-permute-start | bytes 1990664 | tf_op jit(solution)/shard_map/ppermute | solution.py:39
  32.9 12.7 %copy-start = (bf16[1152,512]{1,0:T(8,128)(2,1)S(1)}, bf16[1152,512]{1,0:T(8,128)(2,1)}, u32[]{:S(2)}) copy-start(bf16[1152,512]{1,0:T(8,128)(2,1)} %refs_1_.3) | copy-start | bytes 3538948
  32.9 12.7 %copy-start.1 = (bf16[512,512]{1,0:T(8,128)(2,1)S(1)}, bf16[512,512]{1,0:T(8,128)(2,1)}, u32[]{:S(2)}) copy-start(bf16[512,512]{1,0:T(8,128)(2,1)} %refs_2_.5) | copy-start | bytes 1572868
  32.9 9.5 %collective-permute-start.9 = (bf16[576,256]{1,0:T(8,128)(2,1)S(1)}, bf16[576,256]{1,0:T(8,128)(2,1)S(1)}, u32[]{:S(2)}, u32[]{:S(2)}) collective-permute-start(bf16[576,256]{1,0:T(8,128)(2,1)S(1)} %attend_prior.1.refs_0_), channel_id=1, source_target_pairs={{0,2},{1,3},{2,0},{3,1},{4,6},{5,7},{6,4},{7,5},{8,10},{9,11},{10,... | collective-permute-start | bytes 884744 | tf_op jit(solution)/shard_map/ppermute | solution.py:39
  34.5 7.9 %collective-permute-start.7 = (bf16[576,256]{1,0:T(8,128)(2,1)S(1)}, bf16[576,256]{1,0:T(8,128)(2,1)S(1)}, u32[]{:S(2)}, u32[]{:S(2)}) collective-permute-start(bf16[576,256]{1,0:T(8,128)(2,1)S(1)} %attend_prior.1.refs_0_), channel_id=1, source_target_pairs={{0,1},{1,0},{2,3},{3,2},{4,5},{5,4},{6,7},{7,6},{8,9},{9,8},{10,11... | collective-permute-start | bytes 884744 | tf_op jit(solution)/shard_map/ppermute | solution.py:39
  42.4 3.2 %collective-permute-start.10 = (bf16[576,256]{1,0:T(8,128)(2,1)S(1)}, bf16[576,256]{1,0:T(8,128)(2,1)S(1)}, u32[]{:S(2)}, u32[]{:S(2)}) collective-permute-start(bf16[576,256]{1,0:T(8,128)(2,1)S(1)} %collective-permute-done.9.refs_3_), channel_id=1, source_target_pairs={{0,1},{1,0},{2,3},{3,2},{4,5},{5,4},{6,7},{7,6},{8,9},{9,8},{10,11... | collective-permute-start | bytes 884744 | tf_op jit(solution)/shard_map/ppermute | solution.py:39
  42.4 19.0 %slice-start = ((s8[6291456]{0:T(1024)(128)(4,1)}), s8[4194304]{0:T(1024)(128)(4,1)S(1)}, s32[]{:S(2)}) async-start(s8[6291456]{0:T(1024)(128)(4,1)} %bitcast.7), calls=%async_computation | async-start | bytes 8388608
  45.5 15.9 %slice-start.1 = ((s8[6291456]{0:T(1024)(128)(4,1)}), s8[2097152]{0:T(1024)(128)(4,1)S(1)}, s32[]{:S(2)}) async-start(s8[6291456]{0:T(1024)(128)(4,1)} %bitcast.7), calls=%async_computation.1 | async-start | bytes 4194304
  47.0 9.2 %collective-permute-start.15 = (bf16[256,512]{1,0:T(8,128)(2,1)S(1)}, bf16[256,512]{1,0:T(8,128)(2,1)S(1)}, u32[]{:S(2)}, u32[]{:S(2)}) collective-permute-start(bf16[256,512]{1,0:T(8,128)(2,1)S(1)} %shard_map.100.refs_0_), channel_id=1, source_target_pairs={{0,2},{1,3},{2,0},{3,1},{4,6},{5,7},{6,4},{7,5},{8,10},{9,11},{10,... | collective-permute-start | bytes 786440 | tf_op jit(solution)/shard_map/ppermute | solution.py:39
  50.0 11.4 %collective-permute-start.17 = (bf16[256,512]{1,0:T(8,128)(2,1)S(1)}, bf16[256,512]{1,0:T(8,128)(2,1)S(1)}, u32[]{:S(2)}, u32[]{:S(2)}) collective-permute-start(bf16[256,512]{1,0:T(8,128)(2,1)S(1)} %shard_map.102.refs_0_), channel_id=1, source_target_pairs={{0,2},{1,3},{2,0},{3,1},{4,6},{5,7},{6,4},{7,5},{8,10},{9,11},{10,... | collective-permute-start | bytes 786440 | tf_op jit(solution)/shard_map/ppermute | solution.py:39
  50.6 10.8 %collective-permute-start.13 = (bf16[256,512]{1,0:T(8,128)(2,1)S(1)}, bf16[256,512]{1,0:T(8,128)(2,1)S(1)}, u32[]{:S(2)}, u32[]{:S(2)}) collective-permute-start(bf16[256,512]{1,0:T(8,128)(2,1)S(1)} %shard_map.100.refs_0_), channel_id=1, source_target_pairs={{0,1},{1,0},{2,3},{3,2},{4,5},{5,4},{6,7},{7,6},{8,9},{9,8},{10,11... | collective-permute-start | bytes 786440 | tf_op jit(solution)/shard_map/ppermute | solution.py:39
  50.6 11.8 %collective-permute-start.14 = (bf16[256,512]{1,0:T(8,128)(2,1)S(1)}, bf16[256,512]{1,0:T(8,128)(2,1)S(1)}, u32[]{:S(2)}, u32[]{:S(2)}) collective-permute-start(bf16[256,512]{1,0:T(8,128)(2,1)S(1)} %shard_map.102.refs_0_), channel_id=1, source_target_pairs={{0,1},{1,0},{2,3},{3,2},{4,5},{5,4},{6,7},{7,6},{8,9},{9,8},{10,11... | collective-permute-start | bytes 786440 | tf_op jit(solution)/shard_map/ppermute | solution.py:39
  56.3 7.2 %collective-permute-start.16 = (bf16[256,512]{1,0:T(8,128)(2,1)S(1)}, bf16[256,512]{1,0:T(8,128)(2,1)S(1)}, u32[]{:S(2)}, u32[]{:S(2)}) collective-permute-start(bf16[256,512]{1,0:T(8,128)(2,1)S(1)} %collective-permute-done.15.refs_0_.refs_8_), channel_id=1, source_target_pairs={{0,1},{1,0},{2,3},{3,2},{4,5},{5,4},{6,7},{7,6},{8,9},{9,8},{10,11... | collective-permute-start | bytes 786440 | tf_op jit(solution)/shard_map/ppermute | solution.py:39
  61.4 3.0 %collective-permute-start.18 = (bf16[256,512]{1,0:T(8,128)(2,1)S(1)}, bf16[256,512]{1,0:T(8,128)(2,1)S(1)}, u32[]{:S(2)}, u32[]{:S(2)}) collective-permute-start(bf16[256,512]{1,0:T(8,128)(2,1)S(1)} %collective-permute-done.17.refs_0_.refs_10_), channel_id=1, source_target_pairs={{0,1},{1,0},{2,3},{3,2},{4,5},{5,4},{6,7},{7,6},{8,9},{9,8},{10,11... | collective-permute-start | bytes 786440 | tf_op jit(solution)/shard_map/ppermute | solution.py:39
  65.4 6.0 %collective-permute-start.19 = (bf16[4,128,128]{2,1,0:T(8,128)(2,1)S(1)}, bf16[4,128,128]{2,1,0:T(8,128)(2,1)S(1)}, u32[]{:S(2)}, u32[]{:S(2)}) collective-permute-start(bf16[4,128,128]{2,1,0:T(8,128)(2,1)S(1)} %get-tuple-element.42), channel_id=1, source_target_pairs={{0,4},{4,0},{8,12},{12,8},{16,20},{20,16},{24,28},{28,24},{1,5},{5... | collective-permute-start | bytes 393224 | tf_op jit(solution)/shard_map/ppermute | solution.py:39
  72.7 5.7 %collective-permute-start.20 = (bf16[4,128,128]{2,1,0:T(8,128)(2,1)}, bf16[4,128,128]{2,1,0:T(8,128)(2,1)}, u32[]{:S(2)}, u32[]{:S(2)}) collective-permute-start(bf16[4,128,128]{2,1,0:T(8,128)(2,1)} %fusion.3), channel_id=1, source_target_pairs={{0,8},{4,12},{8,0},{12,4},{16,24},{20,28},{24,16},{28,20},{1,9},{5... | collective-permute-start | bytes 393224 | tf_op jit(solution)/shard_map/ppermute | solution.py:39
  79.4 11.3 %collective-permute-start.21 = (bf16[4,128,128]{2,1,0:T(8,128)(2,1)S(1)}, bf16[4,128,128]{2,1,0:T(8,128)(2,1)S(1)}, u32[]{:S(2)}, u32[]{:S(2)}) collective-permute-start(bf16[4,128,128]{2,1,0:T(8,128)(2,1)S(1)} %fusion.2), channel_id=1, source_target_pairs={{0,16},{4,20},{8,24},{12,28},{1,17},{5,21},{9,25},{13,29},{2,18},{... | collective-permute-start | bytes 393224 | tf_op jit(solution)/shard_map/ppermute | solution.py:73
  85.9 2.8 %copy-start.7 = (bf16[2048,3,512]{2,0,1:T(8,128)(2,1)S(1)}, bf16[2048,3,512]{2,0,1:T(8,128)(2,1)}, u32[]{:S(2)}) copy-start(bf16[2048,3,512]{2,0,1:T(8,128)(2,1)} %param.17) | copy-start | bytes 18874372
  88.7 3.1 %copy-start.3 = (f32[4,128,128]{2,1,0:T(8,128)S(1)}, f32[4,128,128]{2,1,0:T(8,128)}, u32[]{:S(2)}) copy-start(f32[4,128,128]{2,1,0:T(8,128)} %state.1) | copy-start | bytes 786436
  88.7 3.1 %copy-start.4 = (f32[512]{0:T(512)S(1)}, f32[512]{0:T(512)}, u32[]{:S(2)}) copy-start(f32[512]{0:T(512)} %param.18) | copy-start | bytes 6148
  (4 other events, 6.0 us)

commit v5 on v4

--- a/solution.py
+++ b/solution.py
@@ -187,7 +187,7 @@
     *refs, starts, lens, semaphores = refs
     moves = fetch((far_starts, far_lens), (starts, lens), semaphores)
     if prior:
-        *refs, old, result, queries, keys, values, context = refs
+        *refs, old, top, bottom, queries, keys, values, context = refs
         *pieces, weights, near_queries, near_keys, near_values = refs
     else:
         *pieces, weights, context, queries, keys, values = refs
@@ -260,7 +260,8 @@
 
     lax.fori_loop(first // block, jnp.where(last > first, (last + block - 1) // block, 0), step, 0)
     if prior:
-        result[...] = pack(context[...])
+        top[...] = pack(context[: span // 2, :])
+        bottom[...] = pack(context[span // 2 :, :])
 
 
 def attend(pieces, weights, starts, lens, heads, near_rows=(), old=()):
@@ -271,9 +272,11 @@
     extra = [*near_rows, *old]
     return pl.pallas_call(
         functools.partial(attend_kernel, len(old) > 0, span // rows, heads, min(BLOCK, span)),
-        out_shape=jax.ShapeDtypeStruct(packed_shape(span, inner) if old else (span, inner), BF16),
+        out_shape=(jax.ShapeDtypeStruct(packed_shape(span // 2, inner), BF16),) * 2
+        if old
+        else jax.ShapeDtypeStruct((span, inner), BF16),
         in_specs=[HBM, HBM] + [VMEM] * (len(pieces) + 1 + len(extra)),
-        out_specs=VMEM,
+        out_specs=(VMEM,) * 2 if old else VMEM,
         scratch_shapes=[pltpu.VMEM((span, inner), BF16)] * (3 + len(old)) + table_scratch(starts, lens),
         compiler_params=pltpu.CompilerParams(vmem_limit_bytes=16 * 2**20),
         cost_estimate=pl.CostEstimate(flops=5 * 10**9, bytes_accessed=4 * 10**6, transcendentals=10**6),
@@ -297,40 +300,41 @@
     )(weights)
 
 
-def arrange_kernel(far_starts, far_lens, *refs):
-    *refs, starts, lens, semaphores = refs
+def arrange_kernel(sizes, far_starts, far_lens, *refs):
+    *refs, base, starts, lens, semaphores = refs
     for move in fetch((far_starts, far_lens), (starts, lens), semaphores):
         move.wait()
-    near_count = len(refs) - 1 - 2 * lax.axis_size("head")
-    near_refs, refs = refs[: near_count], refs[near_count:]
-    frame_out = refs[-1]
-    count = (len(refs) - 1) // 2
-    rows, _ = refs[0].shape
-    span = rows * count
-    row = clip_rows(rows, count, span)
+    lists, at = [], 0
+    for size in sizes:
+        lists.append(refs[at : at + size])
+        at += size
+    top, bottom, outs, own, prior = lists
+    span = base.shape[0]
+    count = lax.axis_size("head")
+    row = clip_rows(span // count, count, span)
     place = lax.broadcasted_iota(jnp.int32, (span, 1), 0)
-    total = output_product(near_refs[: near_count // 2], near_refs[near_count // 2 :], span)
-    for prior in (False, True):
-        shift, length, _, _ = clip_span(starts, lens, span, prior)
+    total = jnp.concatenate([output_product(parts, outs, span // 2) for parts in (top, bottom)], axis=0)
+    for pieces, earlier in ((own, False), (prior, True)):
+        shift, length, _, _ = clip_span(starts, lens, span, earlier)
         pick = (place + shift == row) & (row < length)
-        frame = jnp.concatenate([piece[...] for piece in refs[prior * count : (prior + 1) * count]], axis=0)
+        frame = jnp.concatenate([piece[...] for piece in pieces], axis=0)
         total = total + dot(jnp.where(pick, 1.0, 0.0).astype(BF16), frame)
-    frame_out[...] = total
-
-
-def arrange(own, prior, parts, outs, starts, lens):
-    rows, width = own[0].shape
-    span = rows * len(own)
-    return pl.pallas_call(
-        arrange_kernel,
-        out_shape=jax.ShapeDtypeStruct((span, width), F32),
-        in_specs=[HBM, HBM] + [VMEM] * (2 * len(own) + 2 * len(parts)),
+    base[...] = total
+
+
+def arrange(own, prior, halves, outs, starts, lens):
+    span = sum(piece.shape[0] for piece in own)
+    lists = (*halves, outs, own, prior)
+    return pl.pallas_call(
+        functools.partial(arrange_kernel, tuple(map(len, lists))),
+        out_shape=jax.ShapeDtypeStruct((span, own[0].shape[1]), F32),
+        in_specs=[HBM, HBM] + [VMEM] * sum(map(len, lists)),
         out_specs=VMEM,
         scratch_shapes=table_scratch(starts, lens),
         compiler_params=pltpu.CompilerParams(vmem_limit_bytes=16 * 2**20),
         cost_estimate=pl.CostEstimate(flops=2 * 10**9, bytes_accessed=3 * 10**6, transcendentals=0),
         name="arrange",
-    )(starts, lens, *parts, *outs, *own, *prior)
+    )(starts, lens, *[piece for pieces in lists for piece in pieces])
 
 
 def project_kernel(low, span, far_starts, far_lens, *refs):
@@ -342,7 +346,7 @@
     here = slice(low, low + rows)
     whole = parts[0].shape[1]
     left = jnp.concatenate(
-        [part[here, :] for part in parts] + [unpack_tail(part[...], span)[here] for part in parts], axis=1
+        [part[:rows, :] for part in parts] + [unpack_tail(part[...], rows) for part in parts], axis=1
     )
     right = jnp.concatenate(
         [weight[:whole, :] for weight in weights] + [weight[whole:, :] for weight in weights], axis=0
@@ -567,15 +571,18 @@
     context = attend(own, vision, clip_start, clip_len, heads)
     half = groups // 2
     near_rows = mix_rows(prior[:half], vision, heads)
-    context = attend(prior[half:], vision, clip_start, clip_len, heads, near_rows, [context])
-    parts = spread(context)
+    halves = attend(prior[half:], vision, clip_start, clip_len, heads, near_rows, [context])
+    parts = [spread(piece) for piece in halves]
     near_keys, far_keys = tuple(range(half)), tuple(range(half, groups))
-    base = arrange(own, prior, parts[:half], outs[:half], clip_start, clip_len)
+    near_parts = [pieces[:half] for pieces in parts]
+    base = arrange(own, prior, near_parts, outs[:half], clip_start, clip_len)
     query_sums, scales, key_rows, value_rows, pieces, old = [], [], [], [], [], []
     low = 0
     for index, share in enumerate(SHARES):
         rows = text_rows.shape[0] // share
-        sequence = project(low, rows, base, parts[half:], outs[half:], projector, text_rows, clip_start, clip_len)
+        sequence = project(
+            low, rows, base, parts[index][half:], outs[half:], projector, text_rows, clip_start, clip_len
+        )
         low += rows
         blocks = spread(sequence)
         query_sum, pair_sum, squares = near(blocks[:half], near_keys, layer)

time: 93.3 us -> 92.3 us (0.989)
  waiting for transfers between devices: 38.7 us -> 37 us
    ppermute x19 -> x22, waiting for transfers between devices: 37.2 us -> 36.5 us  [swapped(): lax.ppermute(value, axis, [(source, source ^ bit) for source in range(cou...]
    ppermute x19 -> x22, starting transfers between devices: 13.7 us -> 13.6 us  [swapped(): lax.ppermute(value, axis, [(source, source ^ bit) for source in range(cou...]
  transfers between devices with their start and end apart: 22 -> 25, of which waited for: 8 -> 9; matrix products, arithmetic and copies ran while one was open for 0% -> 0% of each run, Pallas kernels for 16% -> 18%
where the time goes in v5:
time: 92.3 us; the launch traced here: 92 us
  waiting for transfers between devices  37 us (40%)
  starting transfers between devices  26.9 us (29%)
  Pallas kernels  19.1 us (21%)
  local copies, waits for them, and re-layouts  5.95 us (6%)
  other arithmetic  2.69 us (3%)
    ppermute x22, waiting for transfers between devices, swapped(): lax.ppermute(value, axis, [(source, source ^ bit) for source in range(cou...  36.5 us
    ppermute x22, starting transfers between devices, swapped(): lax.ppermute(value, axis, [(source, source ^ bit) for source in range(cou...  13.6 us
    ppermute x2, starting transfers between devices, shifted(): lax.ppermute(value, axis, [(source, source + steps) for source in range(c...  7.11 us
    ppermute x1, starting transfers between devices, earlier_sum(): other = lax.ppermute(slim, axis, ahead).astype(F32)  6.23 us
    unnamed x28, local copies, waits for them, and re-layouts  5.95 us
    pallas_call x2, Pallas kernels, attend(): pl.pallas_call(functools.partial(attend_kernel, len(old) > 0, span // row...  4.6 us
    pallas_call x1, Pallas kernels, arrange(): pl.pallas_call(functools.partial(arrange_kernel, tuple(map(len, lists))),...  3.1 us
    pallas_call x2, Pallas kernels, project(): pl.pallas_call(functools.partial(project_kernel, low, span), out_shape=ja...  2.96 us
  transfers between devices with their start and end apart: 25, of which 9 were waited for; matrix products, arithmetic and copies ran while one was open for 0% of the time, Pallas kernels for 18%

profile of v5, /device:TPU:0, one launch (start us, length us, event | category | flops | bytes accessed | tf_op | source)
XLA Modules:
  0.0 92.0 jit_solution(2758530054823826935)
XLA Ops:
  0.0 3.0 %collective-permute-start = (bf16[128,1152]{1,0:T(8,128)(2,1)}, bf16[128,1152]{1,0:T(8,128)(2,1)S(1)}, u32[]{:S(2)}, u32[]{:S(2)}) collective-permute-start(bf16[128,1152]{1,0:T(8,128)(2,1)} %refs_6_.1), channel_id=1, source_target_pairs={{0,2},{1,3},{2,0},{3,1},{4,6},{5,7},{6,4},{7,5},{8,10},{9,11},{10,... | collective-permute-start | bytes 884744 | tf_op jit(solution)/shard_map/ppermute | solution.py:39
  3.0 3.4 %collective-permute-start.3 = (bf16[128,1152]{1,0:T(8,128)(2,1)}, bf16[128,1152]{1,0:T(8,128)(2,1)S(1)}, u32[]{:S(2)}, u32[]{:S(2)}) collective-permute-start(bf16[128,1152]{1,0:T(8,128)(2,1)} %refs_6_.1), channel_id=1, source_target_pairs={{0,4},{4,8},{8,12},{12,16},{16,20},{20,24},{24,28},{1,5},{5,9},{9,... | collective-permute-start | bytes 884744 | tf_op jit(solution)/shard_map/ppermute | solution.py:34
  6.5 3.7 %collective-permute-done.refs_2_.refs_8_ = bf16[128,1152]{1,0:T(8,128)(2,1)S(1)} collective-permute-done((bf16[128,1152]{1,0:T(8,128)(2,1)}, bf16[128,1152]{1,0:T(8,128)(2,1)S(1)}, u32[]{:S(2)}, u32[]{:S(2)}) %collective-permute-start) | collective-permute-done | bytes 294944 | tf_op jit(solution)/shard_map/ppermute | solution.py:39
  10.2 3.7 %collective-permute-start.1 = (bf16[128,1152]{1,0:T(8,128)(2,1)S(1)}, bf16[128,1152]{1,0:T(8,128)(2,1)S(1)}, u32[]{:S(2)}, u32[]{:S(2)}) collective-permute-start(bf16[128,1152]{1,0:T(8,128)(2,1)S(1)} %collective-permute-done.refs_2_.refs_8_), channel_id=1, source_target_pairs={{0,4},{4,8},{8,12},{12,16},{16,20},{20,24},{24,28},{1,5},{5,9},{9,... | collective-permute-start | bytes 884744 | tf_op jit(solution)/shard_map/ppermute | solution.py:34
  14.0 1.6 %collective-permute-start.12 = (bf16[288,1152]{1,0:T(8,128)(2,1)}, bf16[288,1152]{1,0:T(8,128)(2,1)S(1)}, u32[]{:S(2)}, u32[]{:S(2)}) collective-permute-start(bf16[288,1152]{1,0:T(8,128)(2,1)} %refs_4_.1), channel_id=1, source_target_pairs={{0,2},{1,3},{2,0},{3,1},{4,6},{5,7},{6,4},{7,5},{8,10},{9,11},{10,... | collective-permute-start | bytes 1990664 | tf_op jit(solution)/shard_map/ppermute | solution.py:39
  15.5 1.6 %copy-done.2 = bf16[1152,3,288]{0,2,1:T(8,128)(2,1)S(1)} copy-done((bf16[1152,3,288]{0,2,1:T(8,128)(2,1)S(1)}, bf16[1152,3,288]{0,2,1:T(8,128)(2,1)}, u32[]{:S(2)}) %copy-start.2) | copy-done | bytes 1990680
  19.3 3.7 %attend_own.1.refs_6_ = bf16[512,288]{1,0:T(8,128)(2,1)S(1)} custom-call(s32[8]{0:T(128)S(1)} %copy-done.4, s32[8]{0:T(128)S(1)} %copy-done.5, bf16[128,1152]{1,0:T(8,128)(2,1)S(1)} %copy-done.9, bf16[128,1152]{1,0:T(8,128)(2,1)S(1)} %collective-permute-done.5.refs_1_.refs_7_, bf16[128,1152]{1,0:T(8,128)(2,1)S(1)} %collective-permute-done.refs_2_.refs_8_, ...), custom_call_target="tpu_custom_call" | custom-call | flops 5000000000 | bytes 4000000 | tf_op jit(solution)/shard_map/attend_own/pallas_call | solution.py:273
  23.0 1.0 %prior_mix.1 = (bf16[256,288]{1,0:T(8,128)(2,1)S(1)}, bf16[256,288]{1,0:T(8,128)(2,1)S(1)}, bf16[256,288]{1,0:T(8,128)(2,1)S(1)}) custom-call(bf16[128,1152]{1,0:T(8,128)(2,1)S(1)} %collective-permute-done.3.refs_0_.refs_10_, bf16[128,1152]{1,0:T(8,128)(2,1)S(1)} %collective-permute-done.4.refs_1_.refs_11_, bf16[864,1152]{1,0:T(8,128)(2,1)S(1)} %warm.1.refs_2_.refs_4_), custom_call_target="tpu_custom_call" | custom-call | flops 1000000000 | bytes 4000000 | tf_op jit(solution)/shard_map/prior_mix/pallas_call | solution.py:175
  24.1 7.4 %collective-permute-done.12.refs_5_ = bf16[288,1152]{1,0:T(8,128)(2,1)S(1)} collective-permute-done((bf16[288,1152]{1,0:T(8,128)(2,1)}, bf16[288,1152]{1,0:T(8,128)(2,1)S(1)}, u32[]{:S(2)}, u32[]{:S(2)}) %collective-permute-start.12) | collective-permute-done | bytes 663584 | tf_op jit(solution)/shard_map/ppermute | solution.py:39
  32.4 1.6 %collective-permute-start.10 = (bf16[288,256]{1,0:T(8,128)(2,1)S(1)}, bf16[288,256]{1,0:T(8,128)(2,1)S(1)}, u32[]{:S(2)}, u32[]{:S(2)}) collective-permute-start(bf16[288,256]{1,0:T(8,128)(2,1)S(1)} %get-tuple-element.29.refs_0_), channel_id=1, source_target_pairs={{0,2},{1,3},{2,0},{3,1},{4,6},{5,7},{6,4},{7,5},{8,10},{9,11},{10,... | collective-permute-start | bytes 442376 | tf_op jit(solution)/shard_map/ppermute | solution.py:39
  35.0 4.2 %collective-permute-done.10.refs_3_ = bf16[288,256]{1,0:T(8,128)(2,1)S(1)} collective-permute-done((bf16[288,256]{1,0:T(8,128)(2,1)S(1)}, bf16[288,256]{1,0:T(8,128)(2,1)S(1)}, u32[]{:S(2)}, u32[]{:S(2)}) %collective-permute-start.10) | collective-permute-done | bytes 147488 | tf_op jit(solution)/shard_map/ppermute | solution.py:39
  39.2 2.7 %collective-permute-done.15.refs_3_ = bf16[288,256]{1,0:T(8,128)(2,1)S(1)} collective-permute-done((bf16[288,256]{1,0:T(8,128)(2,1)S(1)}, bf16[288,256]{1,0:T(8,128)(2,1)S(1)}, u32[]{:S(2)}, u32[]{:S(2)}) %collective-permute-start.15) | collective-permute-done | bytes 147488 | tf_op jit(solution)/shard_map/ppermute | solution.py:39
  41.9 3.1 %arrange.1.refs_0_ = f32[512,1152]{1,0:T(8,128)S(1)} custom-call(s32[8]{0:T(128)S(1)} %copy-done.4, s32[8]{0:T(128)S(1)} %copy-done.5, bf16[288,256]{1,0:T(8,128)(2,1)S(1)} %get-tuple-element.29.refs_0_, bf16[288,256]{1,0:T(8,128)(2,1)S(1)} %collective-permute-done.7.refs_1_, bf16[288,256]{1,0:T(8,128)(2,1)S(1)} %get-tuple-element.30.refs_2_, ...), custom_call_target="tpu_custom_call" | custom-call | flops 2000000000 | bytes 3000000 | tf_op jit(solution)/shard_map/arrange/pallas_call | solution.py:328
  45.0 1.5 %shard_map.100.refs_0_ = bf16[256,512]{1,0:T(8,128)(2,1)S(1)} custom-call(s32[8]{0:T(128)S(1)} %copy-done.4, s32[8]{0:T(128)S(1)} %copy-done.5, f32[512,1152]{1,0:T(8,128)S(1)} %arrange.1.refs_0_, bf16[1152,512]{1,0:T(8,128)(2,1)S(1)} %copy-done, bf16[512,512]{1,0:T(8,128)(2,1)S(1)} %copy-done.1, bf16[288,256]{1,0:T(8,128)(2,1)S(1)} %collective-permute-done.10.refs_3_, ...), custom_call_target="tpu_custom_call" | custom-call | flops 1000000000 | bytes 2000000 | tf_op jit(solution)/shard_map/pallas_call | solution.py:370
  46.5 1.6 %collective-permute-start.18 = (bf16[256,512]{1,0:T(8,128)(2,1)S(1)}, bf16[256,512]{1,0:T(8,128)(2,1)S(1)}, u32[]{:S(2)}, u32[]{:S(2)}) collective-permute-start(bf16[256,512]{1,0:T(8,128)(2,1)S(1)} %shard_map.100.refs_0_), channel_id=1, source_target_pairs={{0,2},{1,3},{2,0},{3,1},{4,6},{5,7},{6,4},{7,5},{8,10},{9,11},{10,... | collective-permute-start | bytes 786440 | tf_op jit(solution)/shard_map/ppermute | solution.py:39
  48.1 1.5 %shard_map.102.refs_0_ = bf16[256,512]{1,0:T(8,128)(2,1)S(1)} custom-call(s32[8]{0:T(128)S(1)} %copy-done.4, s32[8]{0:T(128)S(1)} %copy-done.5, f32[512,1152]{1,0:T(8,128)S(1)} %arrange.1.refs_0_, bf16[1152,512]{1,0:T(8,128)(2,1)S(1)} %copy-done, bf16[512,512]{1,0:T(8,128)(2,1)S(1)} %copy-done.1, bf16[288,256]{1,0:T(8,128)(2,1)S(1)} %collective-permute-done.15.refs_3_, ...), custom_call_target="tpu_custom_call" | custom-call | flops 1000000000 | bytes 2000000 | tf_op jit(solution)/shard_map/pallas_call | solution.py:370
  50.7 5.1 %collective-permute-done.18.refs_0_.refs_8_ = bf16[256,512]{1,0:T(8,128)(2,1)S(1)} collective-permute-done((bf16[256,512]{1,0:T(8,128)(2,1)S(1)}, bf16[256,512]{1,0:T(8,128)(2,1)S(1)}, u32[]{:S(2)}, u32[]{:S(2)}) %collective-permute-start.18) | collective-permute-done | bytes 262176 | tf_op jit(solution)/shard_map/ppermute | solution.py:39
  55.8 5.1 %collective-permute-done.20.refs_0_.refs_10_ = bf16[256,512]{1,0:T(8,128)(2,1)S(1)} collective-permute-done((bf16[256,512]{1,0:T(8,128)(2,1)S(1)}, bf16[256,512]{1,0:T(8,128)(2,1)S(1)}, u32[]{:S(2)}, u32[]{:S(2)}) %collective-permute-start.20) | collective-permute-done | bytes 262176 | tf_op jit(solution)/shard_map/ppermute | solution.py:39
  60.9 1.0 %shard_map.101 = (f32[256,512]{1,0:T(8,128)S(1)}, f32[2,256,512]{2,1,0:T(8,128)S(1)}, f32[256,128]{1,0:T(8,128)S(1)}) custom-call(bf16[3,2048,512]{2,1,0:T(8,128)(2,1)S(1)} %bitcast.9, bf16[256,512]{1,0:T(8,128)(2,1)S(1)} %shard_map.100.refs_0_, bf16[256,512]{1,0:T(8,128)(2,1)S(1)} %collective-permute-done.14.refs_1_), custom_call_target="tpu_custom_call" | custom-call | flops 3000000000 | bytes 7000000 | tf_op jit(solution)/shard_map/pallas_call | solution.py:408
  61.9 1.0 %shard_map.103 = (f32[256,512]{1,0:T(8,128)S(1)}, f32[2,256,512]{2,1,0:T(8,128)S(1)}, f32[256,128]{1,0:T(8,128)S(1)}) custom-call(bf16[3,2048,512]{2,1,0:T(8,128)(2,1)S(1)} %bitcast.10, bf16[256,512]{1,0:T(8,128)(2,1)S(1)} %shard_map.102.refs_0_, bf16[256,512]{1,0:T(8,128)(2,1)S(1)} %collective-permute-done.17.refs_1_), custom_call_target="tpu_custom_call" | custom-call | flops 3000000000 | bytes 7000000 | tf_op jit(solution)/shard_map/pallas_call | solution.py:408
  62.9 1.0 %shard_map.104 = (bf16[256,512]{1,0:T(8,128)(2,1)S(1)}, bf16[256,512]{1,0:T(8,128)(2,1)S(1)}, f32[4,128,128]{2,1,0:T(8,128)S(1)}, f32[256,128]{1,0:T(8,128)S(1)}) custom-call(bf16[3,2048,512]{2,1,0:T(8,128)(2,1)S(1)} %bitcast.11, f32[2,256,512]{2,1,0:T(8,128)S(1)} %get-tuple-element.33.pair_sum, f32[256,128]{1,0:T(8,128)S(1)} %get-tuple-element.34.squares, ...), custom_call_target="tpu_custom_call" | custom-call | flops 3000000000 | bytes 7000000 | tf_op jit(solution)/shard_map/pallas_call | solution.py:450
  63.9 1.0 %shard_map.105 = (bf16[256,512]{1,0:T(8,128)(2,1)S(1)}, bf16[256,512]{1,0:T(8,128)(2,1)S(1)}, bf16[4,128,128]{2,1,0:T(8,128)(2,1)S(1)}, f32[256,128]{1,0:T(8,128)S(1)}) custom-call(bf16[3,2048,512]{2,1,0:T(8,128)(2,1)S(1)} %bitcast.12, f32[2,256,512]{2,1,0:T(8,128)S(1)} %get-tuple-element.36.pair_sum, f32[256,128]{1,0:T(8,128)S(1)} %get-tuple-element.37.squares, ...), custom_call_target="tpu_custom_call" | custom-call | flops 3000000000 | bytes 7000000 | tf_op jit(solution)/shard_map/pallas_call | solution.py:450
  64.9 1.6 %collective-permute-start.22 = (bf16[4,128,128]{2,1,0:T(8,128)(2,1)S(1)}, bf16[4,128,128]{2,1,0:T(8,128)(2,1)S(1)}, u32[]{:S(2)}, u32[]{:S(2)}) collective-permute-start(bf16[4,128,128]{2,1,0:T(8,128)(2,1)S(1)} %get-tuple-element.46), channel_id=1, source_target_pairs={{0,4},{4,0},{8,12},{12,8},{16,20},{20,16},{24,28},{28,24},{1,5},{5... | collective-permute-start | bytes 393224 | tf_op jit(solution)/shard_map/ppermute | solution.py:39
  66.5 4.4 %collective-permute-done.22 = bf16[4,128,128]{2,1,0:T(8,128)(2,1)S(1)} collective-permute-done((bf16[4,128,128]{2,1,0:T(8,128)(2,1)S(1)}, bf16[4,128,128]{2,1,0:T(8,128)(2,1)S(1)}, u32[]{:S(2)}, u32[]{:S(2)}) %collective-permute-start.22) | collective-permute-done | bytes 131104 | tf_op jit(solution)/shard_map/ppermute | solution.py:39
  72.2 1.6 %collective-permute-start.23 = (bf16[4,128,128]{2,1,0:T(8,128)(2,1)}, bf16[4,128,128]{2,1,0:T(8,128)(2,1)}, u32[]{:S(2)}, u32[]{:S(2)}) collective-permute-start(bf16[4,128,128]{2,1,0:T(8,128)(2,1)} %fusion.3), channel_id=1, source_target_pairs={{0,8},{4,12},{8,0},{12,4},{16,24},{20,28},{24,16},{28,20},{1,9},{5... | collective-permute-start | bytes 393224 | tf_op jit(solution)/shard_map/ppermute | solution.py:39
  73.8 3.8 %collective-permute-done.23 = bf16[4,128,128]{2,1,0:T(8,128)(2,1)} collective-permute-done((bf16[4,128,128]{2,1,0:T(8,128)(2,1)}, bf16[4,128,128]{2,1,0:T(8,128)(2,1)}, u32[]{:S(2)}, u32[]{:S(2)}) %collective-permute-start.23) | collective-permute-done | bytes 131104 | tf_op jit(solution)/shard_map/ppermute | solution.py:39
  77.6 1.0 %fusion.2 = bf16[4,128,128]{2,1,0:T(8,128)(2,1)S(1)} fusion(bf16[4,128,128]{2,1,0:T(8,128)(2,1)} %collective-permute-done.23, bf16[4,128,128]{2,1,0:T(8,128)(2,1)} %copy-done.10, bf16[4,128,128]{2,1,0:T(8,128)(2,1)S(1)} %get-tuple-element.46), kind=kLoop, calls=%fused_computation.6 | loop fusion | flops 393216 | bytes 524288 | tf_op jit(solution)/shard_map/convert_element_type | solution.py:68
  78.6 6.2 %collective-permute-start.24 = (bf16[4,128,128]{2,1,0:T(8,128)(2,1)S(1)}, bf16[4,128,128]{2,1,0:T(8,128)(2,1)S(1)}, u32[]{:S(2)}, u32[]{:S(2)}) collective-permute-start(bf16[4,128,128]{2,1,0:T(8,128)(2,1)S(1)} %fusion.2), channel_id=1, source_target_pairs={{0,16},{4,20},{8,24},{12,28},{1,17},{5,21},{9,25},{13,29},{2,18},{... | collective-permute-start | bytes 393224 | tf_op jit(solution)/shard_map/ppermute | solution.py:73
  84.8 2.8 %copy-done.7 = bf16[2048,3,512]{2,0,1:T(8,128)(2,1)S(1)} copy-done((bf16[2048,3,512]{2,0,1:T(8,128)(2,1)S(1)}, bf16[2048,3,512]{2,0,1:T(8,128)(2,1)}, u32[]{:S(2)}) %copy-start.7) | copy-done | bytes 6291480
  87.6 2.0 %within.1 = (bf16[512,512]{1,0:T(8,128)(2,1)S(1)}, f32[512,512]{1,0:T(8,128)S(1)}) custom-call(bf16[3,2048,512]{2,1,0:T(8,128)(2,1)S(1)} %bitcast.13, f32[256,512]{1,0:T(8,128)S(1)} %get-tuple-element.31.refs_0_, f32[256,512]{1,0:T(8,128)S(1)} %get-tuple-element.32.refs_1_, f32[256,128]{1,0:T(8,128)S(1)} %get-tuple-element.35.refs_2_, ...), custom_call_target="tpu_custom_call" | custom-call | flops 3000000000 | bytes 5000000 | tf_op jit(solution)/shard_map/within/pallas_call | solution.py:512
  89.7 1.0 %fusion.1.carried = f32[4,128,128]{2,1,0:T(8,128)S(1)} fusion(bf16[4,128,128]{2,1,0:T(8,128)(2,1)S(1)} %copy-done.11, bf16[4,128,128]{2,1,0:T(8,128)(2,1)} %collective-permute-done.23, bf16[4,128,128]{2,1,0:T(8,128)(2,1)S(1)} %collective-permute-done.24, pred[]{:T(512)S(6)} %ne.11, pred[]{:T(512)S(6)} %ne.10, pred[]{:T(512)S(6)} %ne.9), kind=kLoop, calls=%fused_computation.5 | loop fusion | flops 524288 | bytes 655363 | tf_op jit(solution)/shard_map/add | solution.py:74
  90.7 1.3 %finish.1 = bf16[512,512]{1,0:T(8,128)(2,1)} custom-call(bf16[512,512]{1,0:T(8,128)(2,1)S(1)} %get-tuple-element.44.query, f32[512,512]{1,0:T(8,128)S(1)} %get-tuple-element.45.intra, f32[4,128,128]{2,1,0:T(8,128)S(1)} %fusion.1.carried, f32[4,128,128]{2,1,0:T(8,128)S(1)} %copy-done.3, f32[1,512]{1,0:T(1,128)S(1)} %bitcast.6), custom_call_target="tpu_custom_call" | custom-call | flops 100000000 | bytes 3000000 | tf_op jit(solution)/shard_map/finish/pallas_call | solution.py:540
  (63 shorter events, 6.8 us)
Async XLA Ops:
  0.0 10.2 %collective-permute-start = (bf16[128,1152]{1,0:T(8,128)(2,1)}, bf16[128,1152]{1,0:T(8,128)(2,1)S(1)}, u32[]{:S(2)}, u32[]{:S(2)}) collective-permute-start(bf16[128,1152]{1,0:T(8,128)(2,1)} %refs_6_.1), channel_id=1, source_target_pairs={{0,2},{1,3},{2,0},{3,1},{4,6},{5,7},{6,4},{7,5},{8,10},{9,11},{10,... | collective-permute-start | bytes 884744 | tf_op jit(solution)/shard_map/ppermute | solution.py:39
  3.0 14.3 %collective-permute-start.3 = (bf16[128,1152]{1,0:T(8,128)(2,1)}, bf16[128,1152]{1,0:T(8,128)(2,1)S(1)}, u32[]{:S(2)}, u32[]{:S(2)}) collective-permute-start(bf16[128,1152]{1,0:T(8,128)(2,1)} %refs_6_.1), channel_id=1, source_target_pairs={{0,4},{4,8},{8,12},{12,16},{16,20},{20,24},{24,28},{1,5},{5,9},{9,... | collective-permute-start | bytes 884744 | tf_op jit(solution)/shard_map/ppermute | solution.py:34
  6.4 11.9 %collective-permute-start.5 = (bf16[128,1152]{1,0:T(8,128)(2,1)}, bf16[128,1152]{1,0:T(8,128)(2,1)S(1)}, u32[]{:S(2)}, u32[]{:S(2)}) collective-permute-start(bf16[128,1152]{1,0:T(8,128)(2,1)} %refs_6_.1), channel_id=1, source_target_pairs={{0,1},{1,0},{2,3},{3,2},{4,5},{5,4},{6,7},{7,6},{8,9},{9,8},{10,11... | collective-permute-start | bytes 884744 | tf_op jit(solution)/shard_map/ppermute | solution.py:39
  10.2 9.1 %collective-permute-start.1 = (bf16[128,1152]{1,0:T(8,128)(2,1)S(1)}, bf16[128,1152]{1,0:T(8,128)(2,1)S(1)}, u32[]{:S(2)}, u32[]{:S(2)}) collective-permute-start(bf16[128,1152]{1,0:T(8,128)(2,1)S(1)} %collective-permute-done.refs_2_.refs_8_), channel_id=1, source_target_pairs={{0,4},{4,8},{8,12},{12,16},{16,20},{20,24},{24,28},{1,5},{5,9},{9,... | collective-permute-start | bytes 884744 | tf_op jit(solution)/shard_map/ppermute | solution.py:34
  13.9 5.4 %collective-permute-start.6 = (bf16[128,1152]{1,0:T(8,128)(2,1)S(1)}, bf16[128,1152]{1,0:T(8,128)(2,1)S(1)}, u32[]{:S(2)}, u32[]{:S(2)}) collective-permute-start(bf16[128,1152]{1,0:T(8,128)(2,1)S(1)} %collective-permute-done.refs_2_.refs_8_), channel_id=1, source_target_pairs={{0,1},{1,0},{2,3},{3,2},{4,5},{5,4},{6,7},{7,6},{8,9},{9,8},{10,11... | collective-permute-start | bytes 884744 | tf_op jit(solution)/shard_map/ppermute | solution.py:39
  14.0 17.5 %collective-permute-start.12 = (bf16[288,1152]{1,0:T(8,128)(2,1)}, bf16[288,1152]{1,0:T(8,128)(2,1)S(1)}, u32[]{:S(2)}, u32[]{:S(2)}) collective-permute-start(bf16[288,1152]{1,0:T(8,128)(2,1)} %refs_4_.1), channel_id=1, source_target_pairs={{0,2},{1,3},{2,0},{3,1},{4,6},{5,7},{6,4},{7,5},{8,10},{9,11},{10,... | collective-permute-start | bytes 1990664 | tf_op jit(solution)/shard_map/ppermute | solution.py:39
  18.2 16.3 %collective-permute-start.9 = (bf16[288,1152]{1,0:T(8,128)(2,1)S(1)}, bf16[288,1152]{1,0:T(8,128)(2,1)S(1)}, u32[]{:S(2)}, u32[]{:S(2)}) collective-permute-start(bf16[288,1152]{1,0:T(8,128)(2,1)S(1)} %copy-done.8), channel_id=1, source_target_pairs={{0,1},{1,0},{2,3},{3,2},{4,5},{5,4},{6,7},{7,6},{8,9},{9,8},{10,11... | collective-permute-start | bytes 1990664 | tf_op jit(solution)/shard_map/ppermute | solution.py:39
  18.3 4.7 %collective-permute-start.4 = (bf16[128,1152]{1,0:T(8,128)(2,1)S(1)}, bf16[128,1152]{1,0:T(8,128)(2,1)S(1)}, u32[]{:S(2)}, u32[]{:S(2)}) collective-permute-start(bf16[128,1152]{1,0:T(8,128)(2,1)S(1)} %collective-permute-done.3.refs_0_.refs_10_), channel_id=1, source_target_pairs={{0,1},{1,0},{2,3},{3,2},{4,5},{5,4},{6,7},{7,6},{8,9},{9,8},{10,11... | collective-permute-start | bytes 884744 | tf_op jit(solution)/shard_map/ppermute | solution.py:39
  19.2 12.2 %collective-permute-start.2 = (bf16[128,1152]{1,0:T(8,128)(2,1)S(1)}, bf16[128,1152]{1,0:T(8,128)(2,1)S(1)}, u32[]{:S(2)}, u32[]{:S(2)}) collective-permute-start(bf16[128,1152]{1,0:T(8,128)(2,1)S(1)} %collective-permute-done.1.refs_0_.refs_12_), channel_id=1, source_target_pairs={{0,1},{1,0},{2,3},{3,2},{4,5},{5,4},{6,7},{7,6},{8,9},{9,8},{10,11... | collective-permute-start | bytes 884744 | tf_op jit(solution)/shard_map/ppermute | solution.py:39
  31.5 13.5 %collective-permute-start.13 = (bf16[288,1152]{1,0:T(8,128)(2,1)S(1)}, bf16[288,1152]{1,0:T(8,128)(2,1)S(1)}, u32[]{:S(2)}, u32[]{:S(2)}) collective-permute-start(bf16[288,1152]{1,0:T(8,128)(2,1)S(1)} %collective-permute-done.12.refs_5_), channel_id=1, source_target_pairs={{0,1},{1,0},{2,3},{3,2},{4,5},{5,4},{6,7},{7,6},{8,9},{9,8},{10,11... | collective-permute-start | bytes 1990664 | tf_op jit(solution)/shard_map/ppermute | solution.py:39
  32.4 6.8 %collective-permute-start.10 = (bf16[288,256]{1,0:T(8,128)(2,1)S(1)}, bf16[288,256]{1,0:T(8,128)(2,1)S(1)}, u32[]{:S(2)}, u32[]{:S(2)}) collective-permute-start(bf16[288,256]{1,0:T(8,128)(2,1)S(1)} %get-tuple-element.29.refs_0_), channel_id=1, source_target_pairs={{0,2},{1,3},{2,0},{3,1},{4,6},{5,7},{6,4},{7,5},{8,10},{9,11},{10,... | collective-permute-start | bytes 442376 | tf_op jit(solution)/shard_map/ppermute | solution.py:39
  33.9 11.1 %copy-start = (bf16[1152,512]{1,0:T(8,128)(2,1)S(1)}, bf16[1152,512]{1,0:T(8,128)(2,1)}, u32[]{:S(2)}) copy-start(bf16[1152,512]{1,0:T(8,128)(2,1)} %refs_1_.3) | copy-start | bytes 3538948
  33.9 11.1 %copy-start.1 = (bf16[512,512]{1,0:T(8,128)(2,1)S(1)}, bf16[512,512]{1,0:T(8,128)(2,1)}, u32[]{:S(2)}) copy-start(bf16[512,512]{1,0:T(8,128)(2,1)} %refs_2_.3) | copy-start | bytes 1572868
  33.9 7.9 %collective-permute-start.15 = (bf16[288,256]{1,0:T(8,128)(2,1)S(1)}, bf16[288,256]{1,0:T(8,128)(2,1)S(1)}, u32[]{:S(2)}, u32[]{:S(2)}) collective-permute-start(bf16[288,256]{1,0:T(8,128)(2,1)S(1)} %get-tuple-element.30.refs_2_), channel_id=1, source_target_pairs={{0,2},{1,3},{2,0},{3,1},{4,6},{5,7},{6,4},{7,5},{8,10},{9,11},{10,... | collective-permute-start | bytes 442376 | tf_op jit(solution)/shard_map/ppermute | solution.py:39
  34.5 7.4 %collective-permute-start.7 = (bf16[288,256]{1,0:T(8,128)(2,1)S(1)}, bf16[288,256]{1,0:T(8,128)(2,1)S(1)}, u32[]{:S(2)}, u32[]{:S(2)}) collective-permute-start(bf16[288,256]{1,0:T(8,128)(2,1)S(1)} %get-tuple-element.29.refs_0_), channel_id=1, source_target_pairs={{0,1},{1,0},{2,3},{3,2},{4,5},{5,4},{6,7},{7,6},{8,9},{9,8},{10,11... | collective-permute-start | bytes 442376 | tf_op jit(solution)/shard_map/ppermute | solution.py:39
  34.5 7.4 %collective-permute-start.8 = (bf16[288,256]{1,0:T(8,128)(2,1)S(1)}, bf16[288,256]{1,0:T(8,128)(2,1)S(1)}, u32[]{:S(2)}, u32[]{:S(2)}) collective-permute-start(bf16[288,256]{1,0:T(8,128)(2,1)S(1)} %get-tuple-element.30.refs_2_), channel_id=1, source_target_pairs={{0,1},{1,0},{2,3},{3,2},{4,5},{5,4},{6,7},{7,6},{8,9},{9,8},{10,11... | collective-permute-start | bytes 442376 | tf_op jit(solution)/shard_map/ppermute | solution.py:39
  39.1 5.9 %collective-permute-start.11 = (bf16[288,256]{1,0:T(8,128)(2,1)S(1)}, bf16[288,256]{1,0:T(8,128)(2,1)S(1)}, u32[]{:S(2)}, u32[]{:S(2)}) collective-permute-start(bf16[288,256]{1,0:T(8,128)(2,1)S(1)} %collective-permute-done.10.refs_3_), channel_id=1, source_target_pairs={{0,1},{1,0},{2,3},{3,2},{4,5},{5,4},{6,7},{7,6},{8,9},{9,8},{10,11... | collective-permute-start | bytes 442376 | tf_op jit(solution)/shard_map/ppermute | solution.py:39
  41.8 6.2 %collective-permute-start.16 = (bf16[288,256]{1,0:T(8,128)(2,1)S(1)}, bf16[288,256]{1,0:T(8,128)(2,1)S(1)}, u32[]{:S(2)}, u32[]{:S(2)}) collective-permute-start(bf16[288,256]{1,0:T(8,128)(2,1)S(1)} %collective-permute-done.15.refs_3_), channel_id=1, source_target_pairs={{0,1},{1,0},{2,3},{3,2},{4,5},{5,4},{6,7},{7,6},{8,9},{9,8},{10,11... | collective-permute-start | bytes 442376 | tf_op jit(solution)/shard_map/ppermute | solution.py:39
  41.9 19.1 %slice-start = ((s8[6291456]{0:T(1024)(128)(4,1)}), s8[4194304]{0:T(1024)(128)(4,1)S(1)}, s32[]{:S(2)}) async-start(s8[6291456]{0:T(1024)(128)(4,1)} %bitcast.7), calls=%async_computation | async-start | bytes 8388608
  45.0 15.9 %slice-start.1 = ((s8[6291456]{0:T(1024)(128)(4,1)}), s8[2097152]{0:T(1024)(128)(4,1)S(1)}, s32[]{:S(2)}) async-start(s8[6291456]{0:T(1024)(128)(4,1)} %bitcast.7), calls=%async_computation.1 | async-start | bytes 4194304
  46.5 9.2 %collective-permute-start.18 = (bf16[256,512]{1,0:T(8,128)(2,1)S(1)}, bf16[256,512]{1,0:T(8,128)(2,1)S(1)}, u32[]{:S(2)}, u32[]{:S(2)}) collective-permute-start(bf16[256,512]{1,0:T(8,128)(2,1)S(1)} %shard_map.100.refs_0_), channel_id=1, source_target_pairs={{0,2},{1,3},{2,0},{3,1},{4,6},{5,7},{6,4},{7,5},{8,10},{9,11},{10,... | collective-permute-start | bytes 786440 | tf_op jit(solution)/shard_map/ppermute | solution.py:39
  49.6 11.3 %collective-permute-start.20 = (bf16[256,512]{1,0:T(8,128)(2,1)S(1)}, bf16[256,512]{1,0:T(8,128)(2,1)S(1)}, u32[]{:S(2)}, u32[]{:S(2)}) collective-permute-start(bf16[256,512]{1,0:T(8,128)(2,1)S(1)} %shard_map.102.refs_0_), channel_id=1, source_target_pairs={{0,2},{1,3},{2,0},{3,1},{4,6},{5,7},{6,4},{7,5},{8,10},{9,11},{10,... | collective-permute-start | bytes 786440 | tf_op jit(solution)/shard_map/ppermute | solution.py:39
  50.2 10.8 %collective-permute-start.14 = (bf16[256,512]{1,0:T(8,128)(2,1)S(1)}, bf16[256,512]{1,0:T(8,128)(2,1)S(1)}, u32[]{:S(2)}, u32[]{:S(2)}) collective-permute-start(bf16[256,512]{1,0:T(8,128)(2,1)S(1)} %shard_map.100.refs_0_), channel_id=1, source_target_pairs={{0,1},{1,0},{2,3},{3,2},{4,5},{5,4},{6,7},{7,6},{8,9},{9,8},{10,11... | collective-permute-start | bytes 786440 | tf_op jit(solution)/shard_map/ppermute | solution.py:39
  50.2 11.8 %collective-permute-start.17 = (bf16[256,512]{1,0:T(8,128)(2,1)S(1)}, bf16[256,512]{1,0:T(8,128)(2,1)S(1)}, u32[]{:S(2)}, u32[]{:S(2)}) collective-permute-start(bf16[256,512]{1,0:T(8,128)(2,1)S(1)} %shard_map.102.refs_0_), channel_id=1, source_target_pairs={{0,1},{1,0},{2,3},{3,2},{4,5},{5,4},{6,7},{7,6},{8,9},{9,8},{10,11... | collective-permute-start | bytes 786440 | tf_op jit(solution)/shard_map/ppermute | solution.py:39
  55.8 7.2 %collective-permute-start.19 = (bf16[256,512]{1,0:T(8,128)(2,1)S(1)}, bf16[256,512]{1,0:T(8,128)(2,1)S(1)}, u32[]{:S(2)}, u32[]{:S(2)}) collective-permute-start(bf16[256,512]{1,0:T(8,128)(2,1)S(1)} %collective-permute-done.18.refs_0_.refs_8_), channel_id=1, source_target_pairs={{0,1},{1,0},{2,3},{3,2},{4,5},{5,4},{6,7},{7,6},{8,9},{9,8},{10,11... | collective-permute-start | bytes 786440 | tf_op jit(solution)/shard_map/ppermute | solution.py:39
  60.9 3.0 %collective-permute-start.21 = (bf16[256,512]{1,0:T(8,128)(2,1)S(1)}, bf16[256,512]{1,0:T(8,128)(2,1)S(1)}, u32[]{:S(2)}, u32[]{:S(2)}) collective-permute-start(bf16[256,512]{1,0:T(8,128)(2,1)S(1)} %collective-permute-done.20.refs_0_.refs_10_), channel_id=1, source_target_pairs={{0,1},{1,0},{2,3},{3,2},{4,5},{5,4},{6,7},{7,6},{8,9},{9,8},{10,11... | collective-permute-start | bytes 786440 | tf_op jit(solution)/shard_map/ppermute | solution.py:39
  64.9 6.0 %collective-permute-start.22 = (bf16[4,128,128]{2,1,0:T(8,128)(2,1)S(1)}, bf16[4,128,128]{2,1,0:T(8,128)(2,1)S(1)}, u32[]{:S(2)}, u32[]{:S(2)}) collective-permute-start(bf16[4,128,128]{2,1,0:T(8,128)(2,1)S(1)} %get-tuple-element.46), channel_id=1, source_target_pairs={{0,4},{4,0},{8,12},{12,8},{16,20},{20,16},{24,28},{28,24},{1,5},{5... | collective-permute-start | bytes 393224 | tf_op jit(solution)/shard_map/ppermute | solution.py:39
  72.2 5.4 %collective-permute-start.23 = (bf16[4,128,128]{2,1,0:T(8,128)(2,1)}, bf16[4,128,128]{2,1,0:T(8,128)(2,1)}, u32[]{:S(2)}, u32[]{:S(2)}) collective-permute-start(bf16[4,128,128]{2,1,0:T(8,128)(2,1)} %fusion.3), channel_id=1, source_target_pairs={{0,8},{4,12},{8,0},{12,4},{16,24},{20,28},{24,16},{28,20},{1,9},{5... | collective-permute-start | bytes 393224 | tf_op jit(solution)/shard_map/ppermute | solution.py:39
  78.6 11.1 %collective-permute-start.24 = (bf16[4,128,128]{2,1,0:T(8,128)(2,1)S(1)}, bf16[4,128,128]{2,1,0:T(8,128)(2,1)S(1)}, u32[]{:S(2)}, u32[]{:S(2)}) collective-permute-start(bf16[4,128,128]{2,1,0:T(8,128)(2,1)S(1)} %fusion.2), channel_id=1, source_target_pairs={{0,16},{4,20},{8,24},{12,28},{1,17},{5,21},{9,25},{13,29},{2,18},{... | collective-permute-start | bytes 393224 | tf_op jit(solution)/shard_map/ppermute | solution.py:73
  84.8 2.8 %copy-start.7 = (bf16[2048,3,512]{2,0,1:T(8,128)(2,1)S(1)}, bf16[2048,3,512]{2,0,1:T(8,128)(2,1)}, u32[]{:S(2)}) copy-start(bf16[2048,3,512]{2,0,1:T(8,128)(2,1)} %param.17) | copy-start | bytes 18874372
  87.6 3.1 %copy-start.3 = (f32[4,128,128]{2,1,0:T(8,128)S(1)}, f32[4,128,128]{2,1,0:T(8,128)}, u32[]{:S(2)}) copy-start(f32[4,128,128]{2,1,0:T(8,128)} %state.1) | copy-start | bytes 786436
  87.6 3.1 %copy-start.6 = (f32[512]{0:T(512)S(1)}, f32[512]{0:T(512)}, u32[]{:S(2)}) copy-start(f32[512]{0:T(512)} %param.18) | copy-start | bytes 6148
  (7 other events, 12.0 us)
